TPU v7x, 32 devices: a whole 2x2x4 slice. The times are simulated.
32 devices in a mesh: gx: 8 (over y, x, core), gy: 4 (over z).
Axes of the slice: x: 2, y: 2, z: 4, core: 2. Of those that a mesh axis runs over, the one named last changes fastest.
Arguments:
- coarse_source: float32 [256, 4096], P('gx', 'gy'), may hold values from -6 to 6
- coarse_coefficient: float32 [256, 4096], P('gx', 'gy'), may hold values from 0.25 to 4
- coarse_start: float32 [256, 4096], P('gx', 'gy'), may hold values from -6 to 6
- fine_source: float32 [32, 32, 1024], P(('gx', 'gy')), may hold values from -6 to 6
- fine_coefficient: float32 [32, 32, 1024], P(('gx', 'gy')), may hold values from 0.25 to 4
- fine_start: float32 [32, 32, 1024], P(('gx', 'gy')), may hold values from -6 to 6
- fine_position: int32 [32], replicated, may hold values from 0 to 255, as said below
- first_colour: int32 [3], replicated, may hold values from 0 to 1
Outputs:
- coarse_solution: float32 [256, 4096], P('gx', 'gy')
- fine_solution: float32 [32, 32, 1024], P(('gx', 'gy'))
Inputs may be any that keep to these rules, and one draw needn't show every extreme that they name: `fine_position`: entry r is the box held by device r = gx index * 4 + gy index; its coarse device p // 8 has the same gy index as device r; only octants whose three bits sum to an even number occur, so no two boxes share a face; positions are distinct; in every gy index some coarse device lies under four boxes, and some box lies 8 // 2 gx indices away from its coarse device.
All inputs are finite; a program needn't handle non-finite values.
Results may differ from a plain program's by a relative error of at most 0.0003.
Values sent between devices are 32-bit elements; how exact they have to be, the bound alone decides.
No kernel may reach another device: no remote copies, remote signals or barrier semaphores. Data moves between devices by JAX's collectives and lax.ppermute only.
A program may use at most 64 MiB of HBM per device.

v0:
```python
import jax
import jax.numpy as jnp
from jax import lax
from jax.sharding import PartitionSpec as P

SWEEPS = 4


HIGHEST = lax.Precision.HIGHEST


def with_halo(value, sides, width):
    for axis, dim in sides:
        size, length = (lax.axis_size(axis), value.shape[dim])
        up = [(i, (i + 1) % size) for i in range(size - 1)]
        down = [(j, i) for i, j in up]
        last = lax.slice_in_dim(value, length - width, length, axis=dim)
        first = lax.slice_in_dim(value, 0, width, axis=dim)
        before = lax.ppermute(last, axis, up)
        after = lax.ppermute(first, axis, down)
        value = jnp.concatenate([before, value, after], axis=dim)
    return value


def shifted(values, stride, before, beyond):
    column = lax.broadcasted_iota(jnp.int32, values.shape, 1) % stride
    blanks = jnp.zeros_like(values[:, :1])
    toward = jnp.concatenate([blanks, values[:, :-1]], axis=1)
    backward = jnp.concatenate([values[:, 1:], blanks], axis=1)
    behind = jnp.where(column == 0, before, toward)
    forward = jnp.where(column == stride - 1, beyond, backward)
    return (behind, forward)


def neighbours(values, borders, stride, before, beyond):
    x_before, x_beyond, y_before, y_beyond = borders
    x_minus = jnp.concatenate([x_before, values[:-1]], axis=0)
    x_plus = jnp.concatenate([values[1:], x_beyond], axis=0)
    y_minus = jnp.concatenate([y_before, values[:, :-stride]], axis=1)
    y_plus = jnp.concatenate([values[:, stride:], y_beyond], axis=1)
    z_minus, z_plus = shifted(values, stride, before, beyond)
    return (x_minus, x_plus, y_minus, y_plus, z_minus, z_plus)


def face_terms(coefficient, around):
    weights = tuple((0.5 * (coefficient + neighbour) for neighbour in around))
    diagonal = weights[0] + weights[1] + weights[2] + weights[3] + weights[4] + weights[5]
    return (weights, diagonal)


def coupling(weights, around):
    total = weights[0] * around[0]
    for number in range(1, 6):
        total = total + weights[number] * around[number]
    return total


def relaxed(values, source, coupled, diagonal, factor, parity, colour):
    fresh = (source + factor * coupled) / (factor * diagonal)
    return jnp.where(parity == colour, fresh, values)


def residual_of(values, source, weights, diagonal, around, factor):
    return source - factor * (diagonal * values - coupling(weights, around))


def parity_of(rows_count, breadth, stride):
    along_x = lax.broadcasted_iota(jnp.int32, (rows_count, breadth), 0)
    flattened = lax.broadcasted_iota(jnp.int32, (rows_count, breadth), 1)
    return (along_x + flattened // stride + flattened % stride) % 2


def coarsen(values, stride):
    rows_count = values.shape[0]
    planes = values.shape[1] // stride
    volume = values.reshape(rows_count // 2, 2, planes // 2, 2, stride // 2, 2)
    summed = volume[:, 0] + volume[:, 1]
    summed = summed[:, :, 0] + summed[:, :, 1]
    summed = summed[..., 0] + summed[..., 1]
    return (0.125 * summed).reshape(rows_count // 2, planes // 2 * (stride // 2))


def refine(values, stride):
    rows_count = values.shape[0]
    planes = values.shape[1] // stride
    volume = values.reshape(rows_count, planes, stride)
    volume = jnp.repeat(jnp.repeat(jnp.repeat(volume, 2, axis=0), 2, axis=1), 2, axis=2)
    return volume.reshape(2 * rows_count, 4 * planes * stride)


def enlarge(surface):
    return jnp.repeat(jnp.repeat(surface, 2, axis=0), 2, axis=1)


def octants(values, box_edge):
    half_edge = box_edge // 2
    volume = values.reshape(2, half_edge, 2, half_edge, 2, half_edge)
    return volume.transpose(0, 2, 4, 1, 3, 5).reshape(8, half_edge**3)


def assemble(pieces, box_edge):
    half_edge = box_edge // 2
    volume = pieces.reshape(2, 2, 2, half_edge, half_edge, half_edge)
    return volume.transpose(0, 3, 1, 4, 2, 5).reshape(box_edge, box_edge * box_edge)


def fine_sweep(surfaces, source, coefficient, start, leading, parity, box_edge):
    widened = [enlarge(surface) for surface in surfaces]
    ghosts = (
        widened[0].reshape(1, box_edge * box_edge),
        widened[1].reshape(1, box_edge * box_edge),
        widened[2],
        widened[3],
    )
    ghost_before = jnp.repeat(widened[4], box_edge, axis=1)
    ghost_beyond = jnp.repeat(widened[5], box_edge, axis=1)
    inside = (
        coefficient[:1],
        coefficient[-1:],
        coefficient[:, :box_edge],
        coefficient[:, -box_edge:],
    )
    weights, diagonal = face_terms(
        coefficient, neighbours(coefficient, inside, box_edge, coefficient, coefficient)
    )
    values = start
    for colour in (leading, 1 - leading):
        coupled = coupling(
            weights, neighbours(values, ghosts, box_edge, ghost_before, ghost_beyond)
        )
        values = relaxed(values, source, coupled, diagonal, 4.0, parity, colour)
    remainder = residual_of(
        values,
        source,
        weights,
        diagonal,
        neighbours(values, ghosts, box_edge, ghost_before, ghost_beyond),
        4.0,
    )
    return (values, coarsen(remainder, box_edge))


def bottom_sweeps(source, weights, diagonal, parity, leading, borders_of, half_edge):
    values = jnp.zeros_like(source)
    started = False
    for passage in range(SWEEPS):
        for colour in (leading, 1 - leading):
            if started:
                coupled = coupling(
                    weights, neighbours(values, borders_of(values), half_edge, 0.0, 0.0)
                )
            else:
                coupled = jnp.zeros_like(values)
            started = True
            values = relaxed(values, source, coupled, diagonal, 0.25, parity, colour)
    return values


def coarse_borders(stacked):
    box_edge = stacked.shape[1]
    rowwise = with_halo(stacked, (("gx", 1),), 1)
    colwise = with_halo(stacked, (("gy", 2),), box_edge)
    listed = [
        (
            rowwise[number, :1],
            rowwise[number, -1:],
            colwise[number, :, :box_edge],
            colwise[number, :, -box_edge:],
        )
        for number in range(stacked.shape[0])
    ]
    return (listed, rowwise, colwise)


def spread_borders(stacked):
    half_edge = stacked.shape[1]
    rowwise = with_halo(stacked, (("gx", 1),), 1)
    colwise = with_halo(stacked, (("gy", 2),), half_edge)
    return (rowwise[0, :1], rowwise[0, -1:], colwise[0, :, :half_edge], colwise[0, :, -half_edge:])


def on_device(
    coarse_source,
    coarse_coefficient,
    coarse_start,
    fine_source,
    fine_coefficient,
    fine_start,
    fine_position,
    first_colour,
):
    box_edge = coarse_source.shape[0]
    half_edge = box_edge // 2
    groups_x = lax.axis_size("gx")
    groups_y = lax.axis_size("gy")
    place_x = lax.axis_index("gx")
    place_y = lax.axis_index("gy")
    myrank = place_x * groups_y + place_y
    layout = fine_position.reshape(groups_x, groups_y)
    own_box = lax.dynamic_slice(layout, (place_x, place_y), (1, 1))[0, 0]
    row_boxes = lax.dynamic_slice_in_dim(layout, place_y, 1, 1)[:, 0]
    octant_ids = jnp.arange(8, dtype=jnp.int32)
    matches = (row_boxes[:, None] == myrank * 8 + octant_ids[None, :]).astype(jnp.float32)
    covered = jnp.sum(matches, axis=0)
    owner_x = own_box // 8 // groups_y
    target = (jnp.arange(groups_x, dtype=jnp.int32) == owner_x).astype(jnp.float32)
    listed, rowwise, colwise = coarse_borders(jnp.stack([coarse_coefficient, coarse_start]))
    parity_coarse = parity_of(box_edge, box_edge * box_edge, box_edge)
    weights_c, diagonal_c = face_terms(
        coarse_coefficient, neighbours(coarse_coefficient, listed[0], box_edge, 0.0, 0.0)
    )
    resid_c = residual_of(
        coarse_start,
        coarse_source,
        weights_c,
        diagonal_c,
        neighbours(coarse_start, listed[1], box_edge, 0.0, 0.0),
        1.0,
    )
    rows_start = rowwise[1]
    cols_start = colwise[1].reshape(box_edge, box_edge + 2, box_edge)
    deep_start = jnp.pad(
        coarse_start.reshape(box_edge, box_edge, box_edge), ((0, 0), (0, 0), (1, 1))
    )
    circle_faces = []
    for octant in range(8):
        low_x = octant // 4 * half_edge
        low_y = octant // 2 % 2 * half_edge
        low_z = octant % 2 * half_edge
        plane_low = rows_start[low_x].reshape(box_edge, box_edge)
        plane_high = rows_start[low_x + half_edge + 1].reshape(box_edge, box_edge)
        surfaces = [
            plane_low[low_y : low_y + half_edge, low_z : low_z + half_edge],
            plane_high[low_y : low_y + half_edge, low_z : low_z + half_edge],
            cols_start[low_x : low_x + half_edge, low_y, low_z : low_z + half_edge],
            cols_start[low_x : low_x + half_edge, low_y + half_edge + 1, low_z : low_z + half_edge],
            deep_start[low_x : low_x + half_edge, low_y : low_y + half_edge, low_z],
            deep_start[low_x : low_x + half_edge, low_y : low_y + half_edge, low_z + half_edge + 1],
        ]
        circle_faces.append(jnp.stack(surfaces).reshape(6 * half_edge * half_edge))
    circle_faces = jnp.stack(circle_faces)
    outgoing = jnp.dot(matches, circle_faces, precision=HIGHEST)
    incoming = lax.all_to_all(outgoing, "gx", split_axis=0, concat_axis=0, tiled=True)
    circle_data = jnp.dot(target, incoming, precision=HIGHEST).reshape(6, half_edge, half_edge)
    parity_fine = parity_of(box_edge, box_edge * box_edge, box_edge)
    smoothed, restricted = fine_sweep(
        [circle_data[number] for number in range(6)],
        fine_source[0],
        fine_coefficient[0],
        fine_start[0],
        first_colour[0],
        parity_fine,
        box_edge,
    )
    arrived = lax.all_to_all(
        target[:, None] * restricted.reshape(1, -1), "gx", split_axis=0, concat_axis=0, tiled=True
    )
    replaced = jnp.dot(matches.T, arrived, precision=HIGHEST)
    pieces = octants(resid_c, box_edge)
    pieces = jnp.where(covered[:, None] > 0.5, replaced, pieces)
    composite = assemble(pieces, box_edge)
    leading = first_colour[1]
    blanks = jnp.zeros_like(composite)
    correction = relaxed(blanks, composite, blanks, diagonal_c, 1.0, parity_coarse, leading)
    borders_e = coarse_borders(correction[None])[0][0]
    coupled = coupling(weights_c, neighbours(correction, borders_e, box_edge, 0.0, 0.0))
    correction = relaxed(
        correction, composite, coupled, diagonal_c, 1.0, parity_coarse, 1 - leading
    )
    borders_e = coarse_borders(correction[None])[0][0]
    leftover = residual_of(
        correction,
        composite,
        weights_c,
        diagonal_c,
        neighbours(correction, borders_e, box_edge, 0.0, 0.0),
        1.0,
    )
    bottom_source = coarsen(leftover, box_edge)
    bottom_coefficient = coarsen(coarse_coefficient, box_edge)

    def borders_of(values):
        return spread_borders(values[None])

    weights_b, diagonal_b = face_terms(
        bottom_coefficient,
        neighbours(bottom_coefficient, borders_of(bottom_coefficient), half_edge, 0.0, 0.0),
    )
    parity_bottom = parity_of(bottom_source.shape[0], bottom_source.shape[1], half_edge)
    bottom_values = bottom_sweeps(
        bottom_source, weights_b, diagonal_b, parity_bottom, first_colour[2], borders_of, half_edge
    )
    correction = correction + refine(bottom_values, half_edge)
    coarse_solution = coarse_start + correction
    outgoing_back = jnp.dot(matches, octants(correction, box_edge), precision=HIGHEST)
    returned = lax.all_to_all(outgoing_back, "gx", split_axis=0, concat_axis=0, tiled=True)
    own_part = jnp.dot(target, returned, precision=HIGHEST).reshape(
        half_edge, half_edge * half_edge
    )
    fine_solution = smoothed + refine(own_part, half_edge)
    return (coarse_solution, fine_solution[None])


def solution(mesh):
    placed = (
        P("gx", "gy"),
        P("gx", "gy"),
        P("gx", "gy"),
        P(("gx", "gy"), None, None),
        P(("gx", "gy"), None, None),
        P(("gx", "gy"), None, None),
        P(),
        P(),
    )
    return jax.shard_map(
        on_device,
        mesh=mesh,
        in_specs=placed,
        out_specs=(P("gx", "gy"), P(("gx", "gy"), None, None)),
        check_vma=False,
    )
```

profile of v0, /device:TPU:0, one launch (start us, length us, event | category | flops | bytes accessed | tf_op | source)
XLA Modules:
  0.0 289.9 jit_solution(6443884115537901731)
XLA Ops:
  4.8 5.6 %collective-permute-start.1 = (f32[2,32,32]{2,1,0:T(8,128)}, f32[2,32,32]{2,1,0:T(8,128)}, u32[]{:S(2)}, u32[]{:S(2)}) collective-permute-start(f32[2,32,32]{2,1,0:T(8,128)} %get-tuple-element.60), channel_id=1, source_target_pairs={{0,1},{1,2},{2,3},{4,5},{5,6},{6,7},{8,9},{9,10},{10,11},{12,13},{... | collective-permute-start | bytes 24584 | tf_op jit(solution)/shard_map/ppermute | solution.py:19
  15.0 10.5 %reshape.306 = f32[16,2,16,2,16,2]{5,4,3,2,1,0:T(8,128)} reshape(f32[32,1024]{1,0:T(8,128)} %param.9) | data formatting | bytes 262144 | tf_op jit(solution)/shard_map/reshape | solution.py:76
  25.5 4.5 %fusion.269 = (f32[16,1,16,2,16,2]{5,4,3,2,1,0:T(8,128)S(1)}, f32[16,1,16,2,16,2]{5,4,3,2,1,0:T(8,128)S(1)}) fusion(f32[16,2,16,2,16,2]{5,4,3,2,1,0:T(8,128)} %reshape.306), kind=kLoop, calls=%fused_computation.461 | loop fusion | bytes 262144 | tf_op jit(solution)/shard_map/slice | solution.py:77
  32.8 4.8 %collective-permute-start.14 = (f32[1,16,16]{2,1,0:T(8,128)}, f32[1,16,16]{2,1,0:T(8,128)}, u32[]{:S(2)}, u32[]{:S(2)}) collective-permute-start(f32[1,16,16]{2,1,0:T(8,128)} %get-tuple-element.202), channel_id=1, source_target_pairs={{0,1},{1,2},{2,3},{4,5},{5,6},{6,7},{8,9},{9,10},{10,11},{12,13},{... | collective-permute-start | bytes 3080 | tf_op jit(solution)/shard_map/ppermute | solution.py:19
  80.2 4.0 %all-to-all-start = ((f32[8,1,1536]{2,1,0:T(1,128)}), f32[8,1,1536]{2,1,0:T(1,128)S(1)}, u32[]{:S(2)}, u32[]{:S(2)}) async-start(f32[8,1,1536]{2,1,0:T(1,128)} %copy.224), calls=%async_computation | async-start | bytes 98304 | tf_op jit(solution)/shard_map/all_to_all | solution.py:243
  94.3 9.7 %reshape.300 = f32[16,2,16,2,16,2]{5,4,3,2,1,0:T(8,128)} reshape(f32[32,1024]{1,0:T(8,128)S(1)} %fusion.43) | data formatting | bytes 262144 | tf_op jit(solution)/shard_map/reshape | solution.py:76
  104.0 4.5 %fusion = f32[16,16,2,16,2]{4,3,2,1,0:T(8,128)S(1)} fusion(f32[16,2,16,2,16,2]{5,4,3,2,1,0:T(8,128)} %reshape.300), kind=kLoop, calls=%fused_computation.3 | loop fusion | flops 16384 | bytes 196608 | tf_op jit(solution)/shard_map/add | solution.py:77
  133.3 4.7 %collective-permute-start.10 = (f32[1,32,32]{2,1,0:T(8,128)S(1)}, f32[1,32,32]{2,1,0:T(8,128)S(1)}, u32[]{:S(2)}, u32[]{:S(2)}) collective-permute-start(f32[1,32,32]{2,1,0:T(8,128)S(1)} %get-tuple-element.68), channel_id=1, source_target_pairs={{0,1},{1,2},{2,3},{4,5},{5,6},{6,7},{8,9},{9,10},{10,11},{12,13},{... | collective-permute-start | bytes 12296 | tf_op jit(solution)/shard_map/ppermute | solution.py:19
  150.6 9.7 %reshape.305 = f32[16,2,16,2,16,2]{5,4,3,2,1,0:T(8,128)} reshape(f32[32,1024]{1,0:T(8,128)S(1)} %fusion.58) | data formatting | bytes 262144 | tf_op jit(solution)/shard_map/reshape | solution.py:76
  160.3 4.5 %fusion.270 = (f32[16,1,16,2,16,2]{5,4,3,2,1,0:T(8,128)S(1)}, f32[16,1,16,2,16,2]{5,4,3,2,1,0:T(8,128)S(1)}) fusion(f32[16,2,16,2,16,2]{5,4,3,2,1,0:T(8,128)} %reshape.305), kind=kLoop, calls=%fused_computation.462 | loop fusion | bytes 262144 | tf_op jit(solution)/shard_map/slice | solution.py:77
  168.8 5.2 %collective-permute-start.18 = (f32[1,16,16]{2,1,0:T(8,128)S(1)}, f32[1,16,16]{2,1,0:T(8,128)S(1)}, u32[]{:S(2)}, u32[]{:S(2)}) collective-permute-start(f32[1,16,16]{2,1,0:T(8,128)S(1)} %get-tuple-element.192), channel_id=1, source_target_pairs={{0,1},{1,2},{2,3},{4,5},{5,6},{6,7},{8,9},{9,10},{10,11},{12,13},{... | collective-permute-start | bytes 3080 | tf_op jit(solution)/shard_map/ppermute | solution.py:19
  175.3 4.2 %collective-permute-start.16 = (f32[1,1,256]{2,1,0:T(1,128)S(1)}, f32[1,1,256]{2,1,0:T(1,128)S(1)}, u32[]{:S(2)}, u32[]{:S(2)}) collective-permute-start(f32[1,1,256]{2,1,0:T(1,128)S(1)} %get-tuple-element.196), channel_id=1, source_target_pairs={{0,4},{4,8},{8,12},{12,16},{16,20},{20,24},{24,28},{1,5},{5,9},{9,... | collective-permute-start | bytes 3080 | tf_op jit(solution)/shard_map/ppermute | solution.py:19
  184.4 4.5 %collective-permute-start.22 = (f32[1,16,16]{2,1,0:T(8,128)S(1)}, f32[1,16,16]{2,1,0:T(8,128)S(1)}, u32[]{:S(2)}, u32[]{:S(2)}) collective-permute-start(f32[1,16,16]{2,1,0:T(8,128)S(1)} %get-tuple-element.182), channel_id=1, source_target_pairs={{0,1},{1,2},{2,3},{4,5},{5,6},{6,7},{8,9},{9,10},{10,11},{12,13},{... | collective-permute-start | bytes 3080 | tf_op jit(solution)/shard_map/ppermute | solution.py:19
  199.6 4.5 %collective-permute-start.26 = (f32[1,16,16]{2,1,0:T(8,128)S(1)}, f32[1,16,16]{2,1,0:T(8,128)S(1)}, u32[]{:S(2)}, u32[]{:S(2)}) collective-permute-start(f32[1,16,16]{2,1,0:T(8,128)S(1)} %get-tuple-element.172), channel_id=1, source_target_pairs={{0,1},{1,2},{2,3},{4,5},{5,6},{6,7},{8,9},{9,10},{10,11},{12,13},{... | collective-permute-start | bytes 3080 | tf_op jit(solution)/shard_map/ppermute | solution.py:19
  205.5 5.2 %collective-permute-start.24 = (f32[1,1,256]{2,1,0:T(1,128)S(1)}, f32[1,1,256]{2,1,0:T(1,128)S(1)}, u32[]{:S(2)}, u32[]{:S(2)}) collective-permute-start(f32[1,1,256]{2,1,0:T(1,128)S(1)} %get-tuple-element.176), channel_id=1, source_target_pairs={{0,4},{4,8},{8,12},{12,16},{16,20},{20,24},{24,28},{1,5},{5,9},{9,... | collective-permute-start | bytes 3080 | tf_op jit(solution)/shard_map/ppermute | solution.py:19
  214.0 4.5 %collective-permute-start.30 = (f32[1,16,16]{2,1,0:T(8,128)S(1)}, f32[1,16,16]{2,1,0:T(8,128)S(1)}, u32[]{:S(2)}, u32[]{:S(2)}) collective-permute-start(f32[1,16,16]{2,1,0:T(8,128)S(1)} %get-tuple-element.162), channel_id=1, source_target_pairs={{0,1},{1,2},{2,3},{4,5},{5,6},{6,7},{8,9},{9,10},{10,11},{12,13},{... | collective-permute-start | bytes 3080 | tf_op jit(solution)/shard_map/ppermute | solution.py:19
  219.9 4.7 %collective-permute-start.28 = (f32[1,1,256]{2,1,0:T(1,128)S(1)}, f32[1,1,256]{2,1,0:T(1,128)S(1)}, u32[]{:S(2)}, u32[]{:S(2)}) collective-permute-start(f32[1,1,256]{2,1,0:T(1,128)S(1)} %get-tuple-element.166), channel_id=1, source_target_pairs={{0,4},{4,8},{8,12},{12,16},{16,20},{20,24},{24,28},{1,5},{5,9},{9,... | collective-permute-start | bytes 3080 | tf_op jit(solution)/shard_map/ppermute | solution.py:19
  228.6 4.5 %collective-permute-start.34 = (f32[1,16,16]{2,1,0:T(8,128)S(1)}, f32[1,16,16]{2,1,0:T(8,128)S(1)}, u32[]{:S(2)}, u32[]{:S(2)}) collective-permute-start(f32[1,16,16]{2,1,0:T(8,128)S(1)} %get-tuple-element.152), channel_id=1, source_target_pairs={{0,1},{1,2},{2,3},{4,5},{5,6},{6,7},{8,9},{9,10},{10,11},{12,13},{... | collective-permute-start | bytes 3080 | tf_op jit(solution)/shard_map/ppermute | solution.py:19
  234.5 4.7 %collective-permute-start.32 = (f32[1,1,256]{2,1,0:T(1,128)S(1)}, f32[1,1,256]{2,1,0:T(1,128)S(1)}, u32[]{:S(2)}, u32[]{:S(2)}) collective-permute-start(f32[1,1,256]{2,1,0:T(1,128)S(1)} %get-tuple-element.156), channel_id=1, source_target_pairs={{0,4},{4,8},{8,12},{12,16},{16,20},{20,24},{24,28},{1,5},{5,9},{9,... | collective-permute-start | bytes 3080 | tf_op jit(solution)/shard_map/ppermute | solution.py:19
  242.6 4.5 %collective-permute-start.38 = (f32[1,16,16]{2,1,0:T(8,128)S(1)}, f32[1,16,16]{2,1,0:T(8,128)S(1)}, u32[]{:S(2)}, u32[]{:S(2)}) collective-permute-start(f32[1,16,16]{2,1,0:T(8,128)S(1)} %get-tuple-element.142), channel_id=1, source_target_pairs={{0,1},{1,2},{2,3},{4,5},{5,6},{6,7},{8,9},{9,10},{10,11},{12,13},{... | collective-permute-start | bytes 3080 | tf_op jit(solution)/shard_map/ppermute | solution.py:19
  248.4 4.7 %collective-permute-start.36 = (f32[1,1,256]{2,1,0:T(1,128)S(1)}, f32[1,1,256]{2,1,0:T(1,128)S(1)}, u32[]{:S(2)}, u32[]{:S(2)}) collective-permute-start(f32[1,1,256]{2,1,0:T(1,128)S(1)} %get-tuple-element.146), channel_id=1, source_target_pairs={{0,4},{4,8},{8,12},{12,16},{16,20},{20,24},{24,28},{1,5},{5,9},{9,... | collective-permute-start | bytes 3080 | tf_op jit(solution)/shard_map/ppermute | solution.py:19
  257.1 4.5 %collective-permute-start.42 = (f32[1,16,16]{2,1,0:T(8,128)S(1)}, f32[1,16,16]{2,1,0:T(8,128)S(1)}, u32[]{:S(2)}, u32[]{:S(2)}) collective-permute-start(f32[1,16,16]{2,1,0:T(8,128)S(1)} %get-tuple-element.132), channel_id=1, source_target_pairs={{0,1},{1,2},{2,3},{4,5},{5,6},{6,7},{8,9},{9,10},{10,11},{12,13},{... | collective-permute-start | bytes 3080 | tf_op jit(solution)/shard_map/ppermute | solution.py:19
  263.0 4.7 %collective-permute-start.40 = (f32[1,1,256]{2,1,0:T(1,128)S(1)}, f32[1,1,256]{2,1,0:T(1,128)S(1)}, u32[]{:S(2)}, u32[]{:S(2)}) collective-permute-start(f32[1,1,256]{2,1,0:T(1,128)S(1)} %get-tuple-element.136), channel_id=1, source_target_pairs={{0,4},{4,8},{8,12},{12,16},{16,20},{20,24},{24,28},{1,5},{5,9},{9,... | collective-permute-start | bytes 3080 | tf_op jit(solution)/shard_map/ppermute | solution.py:19
  274.8 12.1 %all_to_all.33 = f32[8,1,4096]{2,1,0:T(1,128)S(1)} all-to-all(f32[8,1,4096]{2,1,0:T(1,128)S(1)} %copy.246), channel_id=1, replica_groups=mesh['gx'=8,'gy'=4] {'gx'}, dimensions={0} | all-to-all | bytes 262144 | tf_op jit(solution)/shard_map/all_to_all | solution.py:296
  (453 shorter events, 147.2 us)
Async XLA Ops:
  2.0 72.4 %collective-permute-start.3 = (f32[2,1,1024]{2,1,0:T(1,128)}, f32[2,1,1024]{2,1,0:T(1,128)}, u32[]{:S(2)}, u32[]{:S(2)}) collective-permute-start(f32[2,1,1024]{2,1,0:T(1,128)} %get-tuple-element.61), channel_id=1, source_target_pairs={{4,0},{8,4},{12,8},{16,12},{20,16},{24,20},{28,24},{5,1},{9,5},{13... | collective-permute-start | bytes 24584 | tf_op jit(solution)/shard_map/ppermute | solution.py:20
  4.8 70.4 %collective-permute-start.1 = (f32[2,32,32]{2,1,0:T(8,128)}, f32[2,32,32]{2,1,0:T(8,128)}, u32[]{:S(2)}, u32[]{:S(2)}) collective-permute-start(f32[2,32,32]{2,1,0:T(8,128)} %get-tuple-element.60), channel_id=1, source_target_pairs={{0,1},{1,2},{2,3},{4,5},{5,6},{6,7},{8,9},{9,10},{10,11},{12,13},{... | collective-permute-start | bytes 24584 | tf_op jit(solution)/shard_map/ppermute | solution.py:19
  10.4 64.8 %collective-permute-start.2 = (f32[2,32,32]{2,1,0:T(8,128)}, f32[2,32,32]{2,1,0:T(8,128)}, u32[]{:S(2)}, u32[]{:S(2)}) collective-permute-start(f32[2,32,32]{2,1,0:T(8,128)} %get-tuple-element.59), channel_id=1, source_target_pairs={{1,0},{2,1},{3,2},{5,4},{6,5},{7,6},{9,8},{10,9},{11,10},{13,12},{... | collective-permute-start | bytes 24584 | tf_op jit(solution)/shard_map/ppermute | solution.py:20
  11.7 65.6 %collective-permute-start = (f32[2,1,1024]{2,1,0:T(1,128)}, f32[2,1,1024]{2,1,0:T(1,128)}, u32[]{:S(2)}, u32[]{:S(2)}) collective-permute-start(f32[2,1,1024]{2,1,0:T(1,128)} %get-tuple-element.62), channel_id=1, source_target_pairs={{0,4},{4,8},{8,12},{12,16},{16,20},{20,24},{24,28},{1,5},{5,9},{9,... | collective-permute-start | bytes 24584 | tf_op jit(solution)/shard_map/ppermute | solution.py:19
  32.8 134.2 %collective-permute-start.14 = (f32[1,16,16]{2,1,0:T(8,128)}, f32[1,16,16]{2,1,0:T(8,128)}, u32[]{:S(2)}, u32[]{:S(2)}) collective-permute-start(f32[1,16,16]{2,1,0:T(8,128)} %get-tuple-element.202), channel_id=1, source_target_pairs={{0,1},{1,2},{2,3},{4,5},{5,6},{6,7},{8,9},{9,10},{10,11},{12,13},{... | collective-permute-start | bytes 3080 | tf_op jit(solution)/shard_map/ppermute | solution.py:19
  80.2 9.0 %all-to-all-start = ((f32[8,1,1536]{2,1,0:T(1,128)}), f32[8,1,1536]{2,1,0:T(1,128)S(1)}, u32[]{:S(2)}, u32[]{:S(2)}) async-start(f32[8,1,1536]{2,1,0:T(1,128)} %copy.224), calls=%async_computation | async-start | bytes 98304 | tf_op jit(solution)/shard_map/all_to_all | solution.py:243
  111.1 8.8 %all-to-all-start.1 = ((f32[8,1,4096]{2,1,0:T(1,128)}), f32[8,1,4096]{2,1,0:T(1,128)S(1)}, u32[]{:S(2)}, u32[]{:S(2)}) async-start(f32[8,1,4096]{2,1,0:T(1,128)} %broadcast_multiply_fusion), calls=%async_computation.1 | async-start | bytes 262144 | tf_op jit(solution)/shard_map/all_to_all | solution.py:255
  133.3 11.3 %collective-permute-start.10 = (f32[1,32,32]{2,1,0:T(8,128)S(1)}, f32[1,32,32]{2,1,0:T(8,128)S(1)}, u32[]{:S(2)}, u32[]{:S(2)}) collective-permute-start(f32[1,32,32]{2,1,0:T(8,128)S(1)} %get-tuple-element.68), channel_id=1, source_target_pairs={{0,1},{1,2},{2,3},{4,5},{5,6},{6,7},{8,9},{9,10},{10,11},{12,13},{... | collective-permute-start | bytes 12296 | tf_op jit(solution)/shard_map/ppermute | solution.py:19
  138.0 7.9 %collective-permute-start.11 = (f32[1,32,32]{2,1,0:T(8,128)S(1)}, f32[1,32,32]{2,1,0:T(8,128)S(1)}, u32[]{:S(2)}, u32[]{:S(2)}) collective-permute-start(f32[1,32,32]{2,1,0:T(8,128)S(1)} %get-tuple-element.67), channel_id=1, source_target_pairs={{1,0},{2,1},{3,2},{5,4},{6,5},{7,6},{9,8},{10,9},{11,10},{13,12},{... | collective-permute-start | bytes 12296 | tf_op jit(solution)/shard_map/ppermute | solution.py:20
  139.3 9.7 %collective-permute-start.8 = (f32[1,1,1024]{2,1,0:T(1,128)S(1)}, f32[1,1,1024]{2,1,0:T(1,128)S(1)}, u32[]{:S(2)}, u32[]{:S(2)}) collective-permute-start(f32[1,1,1024]{2,1,0:T(1,128)S(1)} %get-tuple-element.72), channel_id=1, source_target_pairs={{0,4},{4,8},{8,12},{12,16},{16,20},{20,24},{24,28},{1,5},{5,9},{9,... | collective-permute-start | bytes 12296 | tf_op jit(solution)/shard_map/ppermute | solution.py:19
  144.7 22.4 %collective-permute-start.15 = (f32[1,16,16]{2,1,0:T(8,128)S(1)}, f32[1,16,16]{2,1,0:T(8,128)S(1)}, u32[]{:S(2)}, u32[]{:S(2)}) collective-permute-start(f32[1,16,16]{2,1,0:T(8,128)S(1)} %copy-done.60), channel_id=1, source_target_pairs={{1,0},{2,1},{3,2},{5,4},{6,5},{7,6},{9,8},{10,9},{11,10},{13,12},{... | collective-permute-start | bytes 3080 | tf_op jit(solution)/shard_map/ppermute | solution.py:20
  146.0 21.0 %collective-permute-start.12 = (f32[1,1,256]{2,1,0:T(1,128)S(1)}, f32[1,1,256]{2,1,0:T(1,128)S(1)}, u32[]{:S(2)}, u32[]{:S(2)}) collective-permute-start(f32[1,1,256]{2,1,0:T(1,128)S(1)} %copy-done.65), channel_id=1, source_target_pairs={{0,4},{4,8},{8,12},{12,16},{16,20},{20,24},{24,28},{1,5},{5,9},{9,... | collective-permute-start | bytes 3080 | tf_op jit(solution)/shard_map/ppermute | solution.py:19
  149.0 18.0 %collective-permute-start.13 = (f32[1,1,256]{2,1,0:T(1,128)S(1)}, f32[1,1,256]{2,1,0:T(1,128)S(1)}, u32[]{:S(2)}, u32[]{:S(2)}) collective-permute-start(f32[1,1,256]{2,1,0:T(1,128)S(1)} %copy-done.64), channel_id=1, source_target_pairs={{4,0},{8,4},{12,8},{16,12},{20,16},{24,20},{28,24},{5,1},{9,5},{13... | collective-permute-start | bytes 3080 | tf_op jit(solution)/shard_map/ppermute | solution.py:20
  168.8 12.0 %collective-permute-start.18 = (f32[1,16,16]{2,1,0:T(8,128)S(1)}, f32[1,16,16]{2,1,0:T(8,128)S(1)}, u32[]{:S(2)}, u32[]{:S(2)}) collective-permute-start(f32[1,16,16]{2,1,0:T(8,128)S(1)} %get-tuple-element.192), channel_id=1, source_target_pairs={{0,1},{1,2},{2,3},{4,5},{5,6},{6,7},{8,9},{9,10},{10,11},{12,13},{... | collective-permute-start | bytes 3080 | tf_op jit(solution)/shard_map/ppermute | solution.py:19
  184.4 11.1 %collective-permute-start.22 = (f32[1,16,16]{2,1,0:T(8,128)S(1)}, f32[1,16,16]{2,1,0:T(8,128)S(1)}, u32[]{:S(2)}, u32[]{:S(2)}) collective-permute-start(f32[1,16,16]{2,1,0:T(8,128)S(1)} %get-tuple-element.182), channel_id=1, source_target_pairs={{0,1},{1,2},{2,3},{4,5},{5,6},{6,7},{8,9},{9,10},{10,11},{12,13},{... | collective-permute-start | bytes 3080 | tf_op jit(solution)/shard_map/ppermute | solution.py:19
  199.6 12.4 %collective-permute-start.26 = (f32[1,16,16]{2,1,0:T(8,128)S(1)}, f32[1,16,16]{2,1,0:T(8,128)S(1)}, u32[]{:S(2)}, u32[]{:S(2)}) collective-permute-start(f32[1,16,16]{2,1,0:T(8,128)S(1)} %get-tuple-element.172), channel_id=1, source_target_pairs={{0,1},{1,2},{2,3},{4,5},{5,6},{6,7},{8,9},{9,10},{10,11},{12,13},{... | collective-permute-start | bytes 3080 | tf_op jit(solution)/shard_map/ppermute | solution.py:19
  204.2 7.8 %collective-permute-start.27 = (f32[1,16,16]{2,1,0:T(8,128)S(1)}, f32[1,16,16]{2,1,0:T(8,128)S(1)}, u32[]{:S(2)}, u32[]{:S(2)}) collective-permute-start(f32[1,16,16]{2,1,0:T(8,128)S(1)} %get-tuple-element.171), channel_id=1, source_target_pairs={{1,0},{2,1},{3,2},{5,4},{6,5},{7,6},{9,8},{10,9},{11,10},{13,12},{... | collective-permute-start | bytes 3080 | tf_op jit(solution)/shard_map/ppermute | solution.py:20
  214.0 11.9 %collective-permute-start.30 = (f32[1,16,16]{2,1,0:T(8,128)S(1)}, f32[1,16,16]{2,1,0:T(8,128)S(1)}, u32[]{:S(2)}, u32[]{:S(2)}) collective-permute-start(f32[1,16,16]{2,1,0:T(8,128)S(1)} %get-tuple-element.162), channel_id=1, source_target_pairs={{0,1},{1,2},{2,3},{4,5},{5,6},{6,7},{8,9},{9,10},{10,11},{12,13},{... | collective-permute-start | bytes 3080 | tf_op jit(solution)/shard_map/ppermute | solution.py:19
  228.6 11.9 %collective-permute-start.34 = (f32[1,16,16]{2,1,0:T(8,128)S(1)}, f32[1,16,16]{2,1,0:T(8,128)S(1)}, u32[]{:S(2)}, u32[]{:S(2)}) collective-permute-start(f32[1,16,16]{2,1,0:T(8,128)S(1)} %get-tuple-element.152), channel_id=1, source_target_pairs={{0,1},{1,2},{2,3},{4,5},{5,6},{6,7},{8,9},{9,10},{10,11},{12,13},{... | collective-permute-start | bytes 3080 | tf_op jit(solution)/shard_map/ppermute | solution.py:19
  233.2 7.3 %collective-permute-start.35 = (f32[1,16,16]{2,1,0:T(8,128)S(1)}, f32[1,16,16]{2,1,0:T(8,128)S(1)}, u32[]{:S(2)}, u32[]{:S(2)}) collective-permute-start(f32[1,16,16]{2,1,0:T(8,128)S(1)} %get-tuple-element.151), channel_id=1, source_target_pairs={{1,0},{2,1},{3,2},{5,4},{6,5},{7,6},{9,8},{10,9},{11,10},{13,12},{... | collective-permute-start | bytes 3080 | tf_op jit(solution)/shard_map/ppermute | solution.py:20
  242.6 11.9 %collective-permute-start.38 = (f32[1,16,16]{2,1,0:T(8,128)S(1)}, f32[1,16,16]{2,1,0:T(8,128)S(1)}, u32[]{:S(2)}, u32[]{:S(2)}) collective-permute-start(f32[1,16,16]{2,1,0:T(8,128)S(1)} %get-tuple-element.142), channel_id=1, source_target_pairs={{0,1},{1,2},{2,3},{4,5},{5,6},{6,7},{8,9},{9,10},{10,11},{12,13},{... | collective-permute-start | bytes 3080 | tf_op jit(solution)/shard_map/ppermute | solution.py:19
  247.1 7.3 %collective-permute-start.39 = (f32[1,16,16]{2,1,0:T(8,128)S(1)}, f32[1,16,16]{2,1,0:T(8,128)S(1)}, u32[]{:S(2)}, u32[]{:S(2)}) collective-permute-start(f32[1,16,16]{2,1,0:T(8,128)S(1)} %get-tuple-element.141), channel_id=1, source_target_pairs={{1,0},{2,1},{3,2},{5,4},{6,5},{7,6},{9,8},{10,9},{11,10},{13,12},{... | collective-permute-start | bytes 3080 | tf_op jit(solution)/shard_map/ppermute | solution.py:20
  257.1 11.9 %collective-permute-start.42 = (f32[1,16,16]{2,1,0:T(8,128)S(1)}, f32[1,16,16]{2,1,0:T(8,128)S(1)}, u32[]{:S(2)}, u32[]{:S(2)}) collective-permute-start(f32[1,16,16]{2,1,0:T(8,128)S(1)} %get-tuple-element.132), channel_id=1, source_target_pairs={{0,1},{1,2},{2,3},{4,5},{5,6},{6,7},{8,9},{9,10},{10,11},{12,13},{... | collective-permute-start | bytes 3080 | tf_op jit(solution)/shard_map/ppermute | solution.py:19
  261.7 7.3 %collective-permute-start.43 = (f32[1,16,16]{2,1,0:T(8,128)S(1)}, f32[1,16,16]{2,1,0:T(8,128)S(1)}, u32[]{:S(2)}, u32[]{:S(2)}) collective-permute-start(f32[1,16,16]{2,1,0:T(8,128)S(1)} %get-tuple-element.131), channel_id=1, source_target_pairs={{1,0},{2,1},{3,2},{5,4},{6,5},{7,6},{9,8},{10,9},{11,10},{13,12},{... | collective-permute-start | bytes 3080 | tf_op jit(solution)/shard_map/ppermute | solution.py:20
  (91 other events, 603.9 us)
where the time goes:
time: 293 us; the launch traced here: 290 us
  starting transfers between devices  130 us (44%)
  local copies, waits for them, and re-layouts  86.7 us (30%)
  other arithmetic  28.7 us (10%)
  waiting for transfers between devices  23.1 us (8%)
  blocking collectives  12.1 us (4%)
  between operations  7.54 us (3%)
    ppermute x22, starting transfers between devices, with_halo(): before = lax.ppermute(last, axis, up)  93.6 us
    reshape x3, local copies, waits for them, and re-layouts, coarsen(): volume = values.reshape(rows_count // 2, 2, planes // 2, 2, stride // 2, 2)  29.9 us
    ppermute x22, starting transfers between devices, with_halo(): after = lax.ppermute(first, axis, down)  28.6 us
    ppermute x22, waiting for transfers between devices, with_halo(): after = lax.ppermute(first, axis, down)  17.1 us
    all_to_all x1, blocking collectives, on_device(): lax.all_to_all(outgoing_back, 'gx', split_axis=0, concat_axis=0, tiled=True)  12.1 us
    slice x2, local copies, waits for them, and re-layouts, coarsen(): summed = volume[:, 0] + volume[:, 1]  8.91 us
    unnamed x171, local copies, waits for them, and re-layouts  7.16 us
    select_n x12, other arithmetic, relaxed(): return jnp.where(parity == colour, fresh, values)  6.39 us
  transfers between devices with their start and end apart: 46, of which 11 were waited for; matrix products, arithmetic and copies ran while one was open for 36% of the time, Pallas kernels for 0%

commit v1 on v0

v1 whole, which is shorter than its diff:
```python
import functools

import jax
import jax.numpy as jnp
from jax import lax
from jax.experimental import pallas as pl
from jax.experimental.pallas import tpu as pltpu
from jax.sharding import PartitionSpec as P

SWEEPS = 4
LANES = 128
ROWS = 8
F32 = jnp.float32
BF16 = jnp.bfloat16
VMEM = pl.BlockSpec(memory_space=pltpu.VMEM)
SMEM = pl.BlockSpec(memory_space=pltpu.SMEM)


def iotas(shape):
    return (
        lax.broadcasted_iota(jnp.int32, shape, 0),
        lax.broadcasted_iota(jnp.int32, shape, 1),
    )


def ones_where(mask):
    return jnp.where(mask, 1.0, 0.0).astype(BF16)


def select_dot(value, chosen):
    high = value.astype(BF16)
    rest = value - high.astype(F32)
    middle = rest.astype(BF16)
    low = (rest - middle.astype(F32)).astype(BF16)
    total = jnp.dot(low, chosen, preferred_element_type=F32)
    total = total + jnp.dot(middle, chosen, preferred_element_type=F32)
    return total + jnp.dot(high, chosen, preferred_element_type=F32)


def ahead(value, lanes):
    return pltpu.roll(value, value.shape[1] - lanes, 1)


def behind(value, lanes):
    return pltpu.roll(value, lanes, 1)


def parity_block(row, shape, stride):
    x, lane = iotas(shape)
    return (x + row + lane // stride + lane % stride) % 2


def coarsening(edge, fine_lanes, coarse_lanes):
    half = edge // 2
    fine, coarse = iotas((fine_lanes, coarse_lanes))
    same_y = fine // edge // 2 == coarse // half
    return ones_where(same_y & (fine % edge // 2 == coarse % half))


def refining(edge, coarse_lanes, fine_lanes):
    half = edge // 2
    coarse, fine = iotas((coarse_lanes, fine_lanes))
    same_y = fine // edge // 2 == coarse // half
    return ones_where(same_y & (fine % edge // 2 == coarse % half))


def double_rows(ref, value):
    rows = value.shape[0]
    for tile in range(value.shape[1] // LANES):
        part = value[:, tile * LANES : (tile + 1) * LANES]
        ref[tile, pl.ds(0, rows, 2), :] = part
        ref[tile, pl.ds(1, rows, 2), :] = part


def pair_rows(ref, tile, first, rows):
    return ref[tile, pl.ds(first, rows, 2), :] + ref[tile, pl.ds(first + 1, rows, 2), :]


def tiles_of(lane):
    return slice(lane * LANES, (lane + 1) * LANES)


def flat(ref, rows, tiles):
    return jnp.concatenate([ref[tile, rows, :] for tile in tiles], axis=1)


def place(positions, number, groups_y):
    position = positions[number]
    holder = position // 8
    return (holder // groups_y, position % 8)


def residual_kernel(
    groups_x, groups_y, position, start, coefficient, source, low, high,
    residual, upward, downward, slots,
    table,
):
    edge = start.shape[0]
    half = edge // 2
    lanes = start.shape[1]
    unit = LANES
    me = lax.axis_index("gx")
    mine_y = lax.axis_index("gy")
    table[...] = jnp.zeros_like(table)

    wide = lanes + 2 * unit
    _, lane = iotas((ROWS, wide))
    depth = lane % edge
    blank = jnp.zeros((1, wide), F32)
    for row in range(0, edge, ROWS):
        rows = slice(row, row + ROWS)

        def widened(array, offset, rows=rows):
            return jnp.concatenate(
                [
                    low[rows, offset[0] : offset[0] + unit],
                    array[rows, :],
                    high[rows, offset[1] : offset[1] + unit],
                ],
                axis=1,
            )

        v = widened(start, (0, 0))
        k = widened(coefficient, (low.shape[1] - unit, unit))

        def term(k_other, v_other, k=k, v=v):
            return 0.5 * (k + k_other) * (v_other - v)

        total = term(behind(k, edge), behind(v, edge))
        total = total + term(ahead(k, edge), ahead(v, edge))
        first = depth == 0
        last = depth == edge - 1
        total = total + term(
            jnp.where(first, 0.0, behind(k, 1)), jnp.where(first, 0.0, behind(v, 1))
        )
        total = total + term(
            jnp.where(last, 0.0, ahead(k, 1)), jnp.where(last, 0.0, ahead(v, 1))
        )
        total = total[:, unit : unit + lanes]
        v = start[rows, :]
        k = coefficient[rows, :]

        def flux(near, k=k, v=v):
            return 0.5 * (k + coefficient[near, :]) * (start[near, :] - v)

        x, _ = iotas((ROWS, lanes))
        if row == 0:
            near = jnp.concatenate([start[0:1, :], start[0 : ROWS - 1, :]], axis=0)
            knear = jnp.concatenate(
                [coefficient[0:1, :], coefficient[0 : ROWS - 1, :]], axis=0
            )
            total = total + 0.5 * (k + knear) * (near - v)
        else:
            total = total + flux(slice(row - 1, row + ROWS - 1))
        if row + ROWS == edge:
            near = jnp.concatenate(
                [start[row + 1 : edge, :], start[edge - 1 : edge, :]], axis=0
            )
            knear = jnp.concatenate(
                [coefficient[row + 1 : edge, :], coefficient[edge - 1 : edge, :]], axis=0
            )
            total = total + 0.5 * (k + knear) * (near - v)
        else:
            total = total + flux(slice(row + 1, row + ROWS + 1))
        residual[rows, :] = source[rows, :] + total

    pad = low.shape[1] - unit
    for buffer, rows, k_row, v_row in (
        (upward, slice(half, edge), half - 1, edge - 1),
        (downward, slice(0, half), half, 0),
    ):
        buffer[:, 0:lanes] = residual[rows, :]
        buffer[:, lanes : lanes + pad] = low[rows, unit:]
        buffer[:, lanes + pad : 2 * lanes + pad] = coefficient[rows, :]
        body = 2 * lanes + 2 * pad
        buffer[:, 2 * lanes + pad : body] = high[rows, unit:]
        buffer[:, body:] = jnp.zeros((half, buffer.shape[1] - body), F32)
        pieces = []
        for at in range(0, lanes, unit):
            pieces.append((start, v_row, at))
        for at in range(0, pad, unit):
            pieces.append((low, k_row, unit + at))
        for at in range(0, lanes, unit):
            pieces.append((coefficient, k_row, at))
        for at in range(0, pad, unit):
            pieces.append((high, k_row, unit + at))
        for number, (array, row, at) in enumerate(pieces):
            spot = body + number // half * unit
            line = number % half
            buffer[line : line + 1, spot : spot + unit] = array[row : row + 1, at : at + unit]

    span = half * edge
    tiles = span // unit
    unit_y = unit // edge
    wide = span + 2 * unit
    at, to = iotas((wide, unit))
    y = at // edge - unit_y
    z = at % edge
    for octant_x in range(2):
        for octant_y in range(2):
            octant_z = (octant_x + octant_y) % 2
            rows = slice(octant_x * half, octant_x * half + half)
            begin = octant_y * span
            left = (
                low[rows, 0:unit] if octant_y == 0 else start[rows, begin - unit : begin]
            )
            right = (
                start[rows, begin + span : begin + span + unit]
                if octant_y == 0
                else high[rows, 0:unit]
            )
            block = jnp.concatenate([left, start[rows, begin : begin + span], right], axis=1)
            near_z = half if octant_z == 0 else half - 1
            goal = (2 + octant_z) * half
            chosen = (
                ((y == -1) & (to < half) & (z == octant_z * half + to))
                | ((y == half) & (to // half == 1) & (z == octant_z * half + to - half))
                | ((z == near_z) & (to // half == 2 + octant_z) & (y == to - goal))
            )
            entry = 2 * octant_x + octant_y
            table[entry, 0:half, :] = select_dot(block, ones_where(chosen))
            inner = (half, half + ROWS) if octant_x == 0 else (half - ROWS, half)
            outer = (edge - ROWS, edge) if octant_x == 0 else (0, ROWS)
            pick = 0 if octant_x == 0 else ROWS - 1
            outer_pick = ROWS - 1 if octant_x == 0 else 0
            other = 4 + 2 * octant_x + octant_y
            for (first_row, last_row), which, goes, side in (
                (inner, pick, entry, 1 - octant_x),
                (outer, outer_pick, other, octant_x),
            ):
                plane = start[first_row:last_row, begin : begin + span]
                if octant_z == 1:
                    plane = ahead(plane, half)
                for tile in range(tiles):
                    line = half + side * tiles + tile
                    table[goes, line : line + 1, :] = plane[
                        which : which + 1, tile * unit : (tile + 1) * unit
                    ]

    for holder in range(groups_x):
        owner, octant = place(position, holder * groups_y + mine_y, groups_y)
        octant_x = octant // 4
        octant_y = octant // 2 % 2
        entry = jnp.where(
            owner == me,
            2 * octant_x + octant_y,
            jnp.where(owner == me + 1, 4 + octant_y, 6 + octant_y),
        )
        slots[holder] = table[entry]


def fine_kernel(
    groups_x, groups_y, position, colours, faces, source, coefficient, start,
    smoothed, slots,
    ghost, values, kept, rest,
):
    edge = source.shape[0]
    half = edge // 2
    lanes = source.shape[1]
    me = lax.axis_index("gx") * groups_y + lax.axis_index("gy")
    owner, octant = place(position, me, groups_y)
    octant_x = octant // 4
    leading = colours[0]
    span = half * edge
    tiles = span // LANES

    at, to = iotas((LANES, lanes))
    fine_y = to // edge
    fine_z = to % edge
    chosen = (
        ((fine_y == 0) & (at == fine_z // 2))
        | ((fine_y == edge - 1) & (at == half + fine_z // 2))
        | ((fine_z == edge - 1) & (at == 2 * half + fine_y // 2))
        | ((fine_z == 0) & (at == 3 * half + fine_y // 2))
    )
    base = faces[owner]
    sides = select_dot(base[0:half, :], ones_where(chosen))
    double_rows(ghost, sides)
    before = faces[jnp.maximum(owner - 1, 0)][half:, :]
    after = faces[jnp.minimum(owner + 1, groups_x - 1)][half:, :]
    base = base[half:, :]
    before = jnp.where(owner > 0, before, 0.0)
    after = jnp.where(owner < groups_x - 1, after, 0.0)
    line, _ = iotas(base.shape)
    planes = jnp.where(
        line < tiles,
        jnp.where(octant_x == 0, before, base),
        jnp.where(octant_x == 1, after, base),
    )
    unit_fine = 2 * LANES
    at, to = iotas((LANES, unit_fine))
    grown = select_dot(
        planes,
        ones_where((at // edge == to // edge // 2) & (at % edge == to % edge // 2)),
    )
    for tile in range(tiles):
        for part in range(2):
            at = 2 * tile + part
            extra = grown[:, part * LANES : (part + 1) * LANES]
            ghost[at, 0:1, :] = ghost[at, 0:1, :] + extra[tile : tile + 1, :]
            ghost[at, edge - 1 : edge, :] = (
                ghost[at, edge - 1 : edge, :] + extra[tiles + tile : tiles + tile + 1, :]
            )
    every = range(lanes // LANES)

    _, lane = iotas((ROWS, lanes))
    first_y = lane < edge
    last_y = lane >= lanes - edge
    first_z = lane % edge == 0
    last_z = lane % edge == edge - 1

    def weights_at(row):
        k = coefficient[row : row + ROWS, :]
        if row == 0:
            x_low = jnp.concatenate([k[0:1, :], coefficient[0 : ROWS - 1, :]], axis=0)
        else:
            x_low = coefficient[row - 1 : row + ROWS - 1, :]
        if row + ROWS == edge:
            x_high = jnp.concatenate(
                [coefficient[row + 1 : edge, :], k[ROWS - 1 : ROWS, :]], axis=0
            )
        else:
            x_high = coefficient[row + 1 : row + ROWS + 1, :]
        x, _ = iotas((ROWS, lanes))
        outside = (x + row == 0, x + row == edge - 1, first_y, last_y, first_z, last_z)
        around = (x_low, x_high, behind(k, edge), ahead(k, edge), behind(k, 1), ahead(k, 1))
        faces_of = [0.5 * (k + other) for other in around]
        whole = [jnp.where(out, k, w) for out, w in zip(outside, faces_of)]
        diagonal = ((whole[0] + whole[1]) + (whole[2] + whole[3])) + (whole[4] + whole[5])
        inner = [jnp.where(out, 0.0, w) for out, w in zip(outside, faces_of)]
        return k, inner, diagonal

    def around_of(row):
        at = row + ROWS
        v = values[at : at + ROWS, :]
        return (
            values[at - 1 : at + ROWS - 1, :],
            values[at + 1 : at + ROWS + 1, :],
            behind(v, edge),
            ahead(v, edge),
            behind(v, 1),
            ahead(v, 1),
        )

    def summed(weights, around):
        total = weights[0] * around[0]
        for number in range(1, 6):
            total = total + weights[number] * around[number]
        return total

    edges = jnp.zeros((ROWS, lanes), F32)
    values[0:ROWS, :] = edges
    values[edge + ROWS :, :] = edges
    values[ROWS : edge + ROWS, :] = start[...]
    for step in range(2):
        colour = leading if step == 0 else 1 - leading
        fresh_blocks = []
        for row in range(0, edge, ROWS):
            rows = slice(row, row + ROWS)
            k, inner, diagonal = weights_at(row)
            if step == 0:
                kept[rows, :] = source[rows, :] + 4.0 * k * flat(ghost, rows, every)
            fresh = (kept[rows, :] + 4.0 * summed(inner, around_of(row))) / (4.0 * diagonal)
            rest[rows, :] = fresh
        for row in range(0, edge, ROWS):
            rows = slice(row, row + ROWS)
            at = slice(row + ROWS, row + 2 * ROWS)
            parity = parity_block(row, (ROWS, lanes), edge)
            values[at, :] = jnp.where(parity == colour, rest[rows, :], values[at, :])
    for row in range(0, edge, ROWS):
        rows = slice(row, row + ROWS)
        k, inner, diagonal = weights_at(row)
        v = values[row + ROWS : row + 2 * ROWS, :]
        smoothed[rows, :] = v
        value = kept[rows, :] - 4.0 * (diagonal * v - summed(inner, around_of(row)))
        for tile in every:
            ghost[tile, rows, :] = value[:, tiles_of(tile)]
    chosen = coarsening(edge, 4 * LANES, LANES)
    for part in range(lanes // (4 * LANES)):
        block = jnp.concatenate(
            [pair_rows(ghost, 4 * part + tile, 0, half) for tile in range(4)], axis=1
        )
        mean = 0.125 * select_dot(block, chosen)
        for holder in range(groups_x):
            slots[holder, :, part * LANES : (part + 1) * LANES] = mean


def composite_kernel(
    groups_x, groups_y, position, arrived, residual, start, coefficient, below, above,
    composite, upward, downward,
    grown,
):
    edge = start.shape[0]
    half = edge // 2
    lanes = start.shape[1]
    me = lax.axis_index("gx")
    mine_y = lax.axis_index("gy")
    span = half * edge
    composite[0:half, :] = below[:, 0:lanes]
    composite[half : half + edge, :] = residual[...]
    composite[half + edge :, :] = above[:, 0:lanes]
    body = body_lanes(below.shape[1], half)
    k_from = lanes + (body - 2 * lanes) // 2
    for block, mine, theirs, its_row in (
        (below, 0, half - 1, half - 1),
        (above, edge - 1, half + edge, 0),
    ):
        for tile in range(lanes // LANES):
            where = slice(tile * LANES, (tile + 1) * LANES)
            spot = body + tile // half * LANES
            line = tile % half
            v_other = block[line : line + 1, spot : spot + LANES]
            k_other = block[
                its_row : its_row + 1, k_from + tile * LANES : k_from + (tile + 1) * LANES
            ]
            v = start[mine : mine + 1, where]
            flux = 0.5 * (coefficient[mine : mine + 1, where] + k_other) * (v - v_other)
            row = mine + half
            composite[row : row + 1, where] = composite[row : row + 1, where] - flux
            composite[theirs : theirs + 1, where] = composite[theirs : theirs + 1, where] + flux

    at, to = iotas((LANES, 2 * LANES))
    chosen = ones_where((at // half == to // edge) & (at % half == to % half))
    for holder in range(groups_x):
        for part in range(arrived.shape[2] // LANES):
            grown[holder, :, part * 2 * LANES : (part + 1) * 2 * LANES] = select_dot(
                arrived[holder, :, part * LANES : (part + 1) * LANES], chosen
            )
    _, lane = iotas((half, span))
    half_of = lane % edge // half
    for holder in range(groups_x):
        owner, octant = place(position, holder * groups_y + mine_y, groups_y)
        block = 2 * (owner - me) + octant // 4 + 1

        @pl.when((block >= 0) & (block < 4))
        def _(holder=holder, octant=octant, block=block):
            rows = pl.ds(pl.multiple_of(block * half, half), half)
            where = pl.ds(pl.multiple_of(octant // 2 % 2 * span, span), span)
            composite[rows, where] = jnp.where(
                half_of == octant % 2, grown[holder], composite[rows, where]
            )

    upward[...] = composite[:, span:]
    downward[...] = composite[:, 0:span]


def body_lanes(total, rows):
    blocks = total // LANES
    extra = 1
    while -(-(blocks - extra) // rows) != extra:
        extra += 1
    return total - extra * LANES


def coarse_kernel(
    groups_x, groups_y, position, colours, start, coefficient, composite, comp_low,
    comp_high, low, high, below, above,
    solution_ref, slots,
    kext, comp, weights, inverse, first_values, second_values, left, ktiles, bottom, corrected, table,
):
    edge = start.shape[0]
    half = edge // 2
    lanes = start.shape[1]
    span = half * edge
    unit = LANES
    me = lax.axis_index("gx")
    mine_y = lax.axis_index("gy")
    pad = low.shape[1] - unit
    wide = lanes + 2 * pad
    rows_all = 2 * edge
    lanes_all = 2 * lanes
    top = half + ROWS

    kext[top : top + edge, 0:pad] = low[:, unit:]
    kext[top : top + edge, pad : pad + lanes] = coefficient[...]
    kext[top : top + edge, pad + lanes :] = high[:, unit:]
    kext[0:ROWS, :] = jnp.zeros((ROWS, wide), F32)
    kext[top + edge + half :, :] = jnp.zeros((ROWS, wide), F32)
    kext[ROWS:top, :] = below[:, lanes : lanes + wide]
    kext[top + edge : top + edge + half, :] = above[:, lanes : lanes + wide]
    body = lanes + wide
    for tile in range(wide // unit):
        number = lanes // unit + tile
        spot = body + number // half * unit
        line = number % half
        where = slice(tile * unit, (tile + 1) * unit)
        kext[ROWS - 1 : ROWS, where] = below[line : line + 1, spot : spot + unit]
        kext[top + edge + half : top + edge + half + 1, where] = above[
            line : line + 1, spot : spot + unit
        ]
    comp[:, 0:span] = comp_low[...]
    comp[:, span : span + lanes] = composite[...]
    comp[:, span + lanes :] = comp_high[...]

    def inside(shape, row, x_half, x_edge, stride, y_half):
        x, lane = iotas(shape)
        x = x + (row - x_half) + me * x_edge
        y = lane // stride - y_half + mine_y * x_edge
        return (
            (x >= 0) & (x < groups_x * x_edge) & (y >= 0) & (y < groups_y * x_edge)
        )

    def six(k, k_low, k_high, stride, depth_edge):
        _, lane = iotas(k.shape)
        depth = lane % depth_edge
        first = depth == 0
        last = depth == depth_edge - 1
        w = [
            0.5 * (k + k_low),
            0.5 * (k + k_high),
            0.5 * (k + behind(k, stride)),
            0.5 * (k + ahead(k, stride)),
        ]
        z_low = 0.5 * (k + jnp.where(first, 0.0, behind(k, 1)))
        z_high = 0.5 * (k + jnp.where(last, 0.0, ahead(k, 1)))
        diagonal = ((w[0] + w[1]) + (w[2] + w[3])) + (z_low + z_high)
        w = w + [jnp.where(first, 0.0, z_low), jnp.where(last, 0.0, z_high)]
        return w, diagonal

    shift = pad - span
    zero_rows = jnp.zeros((ROWS, lanes_all), F32)
    for ref in (first_values, second_values):
        ref[0:ROWS, :] = zero_rows
        ref[ROWS + rows_all :, :] = zero_rows
    leading = colours[1]
    cut = slice(shift, shift + lanes_all)
    for row in range(0, rows_all, ROWS):
        at = row + ROWS
        k = kext[at : at + ROWS, :]
        w, diagonal = six(
            k, kext[at - 1 : at + ROWS - 1, :], kext[at + 1 : at + ROWS + 1, :], edge, edge
        )
        rows = slice(row, row + ROWS)
        for number in range(6):
            weights[number, rows, :] = w[number][:, cut]
        shape = (ROWS, lanes_all)
        inv = jnp.where(
            inside(shape, row, half, edge, edge, half), 1.0 / diagonal[:, cut], 0.0
        )
        inverse[rows, :] = inv
        parity = parity_block(row, shape, edge)
        first_values[at : at + ROWS, :] = jnp.where(
            parity == leading, comp[rows, :] * inv, 0.0
        )

    def coupled(ref, row):
        at = row + ROWS
        rows = slice(row, row + ROWS)
        v = ref[at : at + ROWS, :]
        total = weights[0, rows, :] * ref[at - 1 : at + ROWS - 1, :]
        total = total + weights[1, rows, :] * ref[at + 1 : at + ROWS + 1, :]
        total = total + weights[2, rows, :] * behind(v, edge)
        total = total + weights[3, rows, :] * ahead(v, edge)
        total = total + weights[4, rows, :] * behind(v, 1)
        return total + weights[5, rows, :] * ahead(v, 1), v

    for row in range(0, rows_all, ROWS):
        rows = slice(row, row + ROWS)
        total, v = coupled(first_values, row)
        parity = parity_block(row, v.shape, edge)
        second_values[row + ROWS : row + 2 * ROWS, :] = jnp.where(
            parity == leading, v, (comp[rows, :] + total) * inverse[rows, :]
        )
    for row in range(0, rows_all, ROWS):
        rows = slice(row, row + ROWS)
        total, v = coupled(second_values, row)
        parity = parity_block(row, v.shape, edge)
        total = jnp.where(parity == leading, total, 0.0)
        for tile in range(lanes_all // unit):
            left[tile, rows, :] = total[:, tiles_of(tile)]
            other = shift // unit + tile
            ktiles[tile, rows, :] = kext[row + ROWS : row + 2 * ROWS, tiles_of(other)]

    chosen = coarsening(edge, 4 * unit, unit)
    bottom_lanes = lanes_all // 4
    f_parts = []
    k_parts = []
    for part in range(bottom_lanes // unit):
        for ref, parts in ((left, f_parts), (ktiles, k_parts)):
            pair = jnp.concatenate(
                [pair_rows(ref, 4 * part + tile, 0, edge) for tile in range(4)], axis=1
            )
            parts.append(0.125 * select_dot(pair, chosen))
    f_bottom = jnp.concatenate(f_parts, axis=1)
    k_bottom = jnp.concatenate(k_parts, axis=1)
    count = edge

    def rows_behind(value):
        return pltpu.roll(value, 1, 0)

    def rows_ahead(value):
        return pltpu.roll(value, count - 1, 0)

    w, diagonal = six(k_bottom, rows_behind(k_bottom), rows_ahead(k_bottom), half, half)
    shape = (edge, bottom_lanes)
    inside_b = inside(shape, 0, half // 2, half, half, half // 2)
    inv = jnp.where(inside_b, 1.0 / (0.25 * diagonal), 0.0)
    w = [0.25 * one for one in w]
    parity = parity_block(0, shape, half)
    values = jnp.zeros(shape, F32)
    for step in range(2 * SWEEPS):
        colour = colours[2] if step % 2 == 0 else 1 - colours[2]
        if step == 0:
            total = f_bottom
        else:
            total = f_bottom + w[0] * rows_behind(values)
            total = total + w[1] * rows_ahead(values)
            total = total + w[2] * behind(values, half)
            total = total + w[3] * ahead(values, half)
            total = total + w[4] * behind(values, 1)
            total = total + w[5] * ahead(values, 1)
        values = jnp.where(parity == colour, total * inv, values)
    bottom[...] = values

    quarter = half // 2
    skip = quarter * half
    chosen = refining(edge, unit, 4 * unit)
    for part in range(lanes // (4 * unit)):
        block = bottom[quarter : quarter + half, skip + part * unit : skip + (part + 1) * unit]
        double_rows(left.at[pl.ds(4 * part, 4)], select_dot(block, chosen))
    for row in range(0, edge, ROWS):
        rows = slice(row, row + ROWS)
        at = row + ROWS + half
        total = flat(left, rows, range(lanes // unit)) + second_values[at : at + ROWS, span : span + lanes]
        corrected[rows, :] = total
        solution_ref[rows, :] = start[rows, :] + total

    at, to = iotas((2 * unit, unit))
    chosen = ones_where((at // edge == to // half) & (at % edge == to % half))
    for octant_x in range(2):
        for octant_y in range(2):
            block = corrected[
                octant_x * half : (octant_x + 1) * half,
                octant_y * span : (octant_y + 1) * span,
            ]
            if (octant_x + octant_y) % 2 == 1:
                block = ahead(block, half)
            for part in range(span // (2 * unit)):
                table[2 * octant_x + octant_y, :, part * unit : (part + 1) * unit] = select_dot(
                    block[:, part * 2 * unit : (part + 1) * 2 * unit], chosen
                )
    for holder in range(groups_x):
        owner, octant = place(position, holder * groups_y + mine_y, groups_y)
        slots[holder] = table[octant // 4 * 2 + octant // 2 % 2]


def finish_kernel(groups_y, position, arrived, smoothed, out, grown):
    edge = smoothed.shape[0]
    half = edge // 2
    me = lax.axis_index("gx") * groups_y + lax.axis_index("gy")
    owner, _ = place(position, me, groups_y)
    value = arrived[owner]
    chosen = refining(edge, LANES, 4 * LANES)
    for part in range(value.shape[1] // LANES):
        fine = select_dot(value[:, tiles_of(part)], chosen)
        double_rows(grown.at[pl.ds(4 * part, 4)], fine)
    out[...] = smoothed[...] + flat(grown, slice(0, edge), range(smoothed.shape[1] // LANES))


def call(kernel, outs, scratch, specs, *operands):
    return pl.pallas_call(
        kernel,
        out_shape=[jax.ShapeDtypeStruct(shape, F32) for shape in outs],
        in_specs=specs,
        out_specs=[VMEM] * len(outs),
        scratch_shapes=[pltpu.VMEM(shape, F32) for shape in scratch],
        compiler_params=pltpu.CompilerParams(vmem_limit_bytes=40 * 1024 * 1024),
    )(*operands)


def tiled(rows, lanes):
    return (lanes // LANES, rows, LANES)


def both_ways(last, first, axis):
    size = lax.axis_size(axis)
    up = [(i, i + 1) for i in range(size - 1)]
    down = [(i + 1, i) for i in range(size - 1)]
    return lax.ppermute(last, axis, up), lax.ppermute(first, axis, down)


def on_device(
    coarse_source,
    coarse_coefficient,
    coarse_start,
    fine_source,
    fine_coefficient,
    fine_start,
    fine_position,
    first_colour,
):
    groups_x = lax.axis_size("gx")
    groups_y = lax.axis_size("gy")
    edge, lanes = coarse_source.shape
    half = edge // 2
    span = half * edge
    pad = span + LANES
    low, high = both_ways(
        jnp.concatenate([coarse_start[:, lanes - LANES :], coarse_coefficient[:, lanes - pad :]], 1),
        jnp.concatenate([coarse_start[:, :LANES], coarse_coefficient[:, :pad]], 1),
        "gy",
    )
    wide = lanes + 2 * pad
    extra = -(-(lanes + wide) // LANES // half) * LANES
    packed = lanes + wide + extra
    face_rows = half + 2 * (span // LANES)
    residual, upward, downward, slots = call(
        functools.partial(residual_kernel, groups_x, groups_y),
        [(edge, lanes), (half, packed), (half, packed), (groups_x, face_rows, LANES)],
        [(8, face_rows, LANES)],
        [SMEM] + [VMEM] * 5,
        fine_position, coarse_start, coarse_coefficient, coarse_source, low, high,
    )
    below, above = both_ways(upward, downward, "gx")
    faces = lax.all_to_all(slots, "gx", 0, 0, tiled=True)
    compact = half * half
    smoothed, restricted = call(
        functools.partial(fine_kernel, groups_x, groups_y),
        [(edge, lanes), (groups_x, half, compact)],
        [tiled(edge, lanes), (edge + 2 * ROWS, lanes), (edge, lanes), (edge, lanes)],
        [SMEM, SMEM] + [VMEM] * 4,
        fine_position, first_colour, faces, fine_source[0], fine_coefficient[0], fine_start[0],
    )
    arrived = lax.all_to_all(restricted, "gx", 0, 0, tiled=True)
    composite, upward, downward = call(
        functools.partial(composite_kernel, groups_x, groups_y),
        [(2 * edge, lanes), (2 * edge, span), (2 * edge, span)],
        [(groups_x, half, span)],
        [SMEM] + [VMEM] * 6,
        fine_position, arrived, residual, coarse_start, coarse_coefficient, below, above,
    )
    comp_low, comp_high = both_ways(upward, downward, "gy")
    rows = 2 * edge
    coarse_solution, slots = call(
        functools.partial(coarse_kernel, groups_x, groups_y),
        [(edge, lanes), (groups_x, half, compact)],
        [
            (rows + 2 * ROWS, wide),
            (rows, 2 * lanes),
            (6, rows, 2 * lanes),
            (rows, 2 * lanes),
            (rows + 2 * ROWS, 2 * lanes),
            (rows + 2 * ROWS, 2 * lanes),
            tiled(rows, 2 * lanes),
            tiled(rows, 2 * lanes),
            (edge, lanes // 2),
            (edge, lanes),
            (4, half, compact),
        ],
        [SMEM, SMEM] + [VMEM] * 9,
        fine_position, first_colour, coarse_start, coarse_coefficient, composite,
        comp_low, comp_high, low, high, below, above,
    )
    returned = lax.all_to_all(slots, "gx", 0, 0, tiled=True)
    (fine_solution,) = call(
        functools.partial(finish_kernel, groups_y),
        [(edge, lanes)],
        [tiled(edge, lanes)],
        [SMEM] + [VMEM] * 2,
        fine_position, returned, smoothed,
    )
    return (coarse_solution, fine_solution[None])


def solution(mesh):
    placed = (
        P("gx", "gy"),
        P("gx", "gy"),
        P("gx", "gy"),
        P(("gx", "gy"), None, None),
        P(("gx", "gy"), None, None),
        P(("gx", "gy"), None, None),
        P(),
        P(),
    )
    return jax.shard_map(
        on_device,
        mesh=mesh,
        in_specs=placed,
        out_specs=(P("gx", "gy"), P(("gx", "gy"), None, None)),
        check_vma=False,
    )
```

time: 293 us -> 67.6 us (0.23)
  starting transfers between devices: 130 us -> 13.9 us
  local copies, waits for them, and re-layouts: 86.7 us -> 2.4 us
  other arithmetic: 28.7 us -> 0.02 us
  blocking collectives: 12.1 us -> 27.5 us
  waiting for transfers between devices: 23.1 us -> 10.8 us
  Pallas kernels: 0 us -> 11.8 us
  between operations: 7.54 us -> 0.79 us
    ppermute x44 -> x6, starting transfers between devices: 122 us -> 13.9 us  [both_ways(): return (lax.ppermute(last, axis, up), lax.ppermute(first, axis, down))]
    reshape x25 -> x0, local copies, waits for them, and re-layouts: 38.3 us -> none  [the longest x3 29.9 us: coarsen(): volume = values.reshape(rows_count // 2, 2, planes // 2, 2, stride // 2, 2)]
    slice x82 -> x2, local copies, waits for them, and re-layouts: 30.9 us -> 1.71 us  [the longest x1 0.97 us: on_device(): coarse_coefficient[:, :pad]]
    all_to_all x1 -> x3, blocking collectives: 12.1 us -> 27.5 us  [the longest x1 11.7 us: on_device(): faces = lax.all_to_all(slots, 'gx', 0, 0, tiled=True)]
    pallas_call x0 -> x5, Pallas kernels: none -> 11.8 us  [call(): pl.pallas_call(kernel, out_shape=[jax.ShapeDtypeStruct(shape, F32) for sh...]
    all_to_all x2 -> x0, starting transfers between devices: 7.42 us -> none  [the longest x1 4.05 us: on_device(): lax.all_to_all(outgoing, 'gx', split_axis=0, concat_axis=0, tiled=True)]
    add x8 -> x0, other arithmetic: 7.07 us -> none  [the longest x3 5.57 us: coarsen(): summed = volume[:, 0] + volume[:, 1]]
    unnamed x171 -> x16, local copies, waits for them, and re-layouts: 7.16 us -> 0.69 us
  transfers between devices with their start and end apart: 46 -> 6, of which waited for: 11 -> 4; matrix products, arithmetic and copies ran while one was open for 36% -> 0% of each run, Pallas kernels for 0% -> 3%
where the time goes in v1:
time: 67.6 us; the launch traced here: 67.1 us
  blocking collectives  27.5 us (41%)
  starting transfers between devices  13.9 us (21%)
  Pallas kernels  11.8 us (17%)
  waiting for transfers between devices  10.8 us (16%)
  local copies, waits for them, and re-layouts  2.4 us (4%)
  between operations  0.79 us (1%)
    ppermute x6, starting transfers between devices, both_ways(): return (lax.ppermute(last, axis, up), lax.ppermute(first, axis, down))  13.9 us
    pallas_call x5, Pallas kernels, call(): pl.pallas_call(kernel, out_shape=[jax.ShapeDtypeStruct(shape, F32) for sh...  11.8 us
    all_to_all x1, blocking collectives, on_device(): faces = lax.all_to_all(slots, 'gx', 0, 0, tiled=True)  11.7 us
    ppermute x6, waiting for transfers between devices, both_ways(): return (lax.ppermute(last, axis, up), lax.ppermute(first, axis, down))  10.8 us
    all_to_all x1, blocking collectives, on_device(): arrived = lax.all_to_all(restricted, 'gx', 0, 0, tiled=True)  7.89 us
    all_to_all x1, blocking collectives, on_device(): returned = lax.all_to_all(slots, 'gx', 0, 0, tiled=True)  7.88 us
  transfers between devices with their start and end apart: 6, of which 4 were waited for; matrix products, arithmetic and copies ran while one was open for 0% of the time, Pallas kernels for 3%

profile of v1, /device:TPU:0, one launch (start us, length us, event | category | flops | bytes accessed | tf_op | source)
XLA Modules:
  0.0 67.1 jit_solution(11545299549505996305)
XLA Ops:
  0.6 0.7 %fusion = (f32[32,128]{1,0:T(8,128)S(1)}, f32[32,128]{1,0:T(8,128)S(1)}) fusion(f32[32,1024]{1,0:T(8,128)} %start.5), kind=kLoop, calls=%fused_computation.2 | loop fusion | bytes 65536 | tf_op jit(solution)/shard_map/slice | solution.py:700
  1.4 1.0 %fusion.1 = (f32[32,640]{1,0:T(8,128)S(1)}, f32[32,640]{1,0:T(8,128)S(1)}) fusion(f32[32,1024]{1,0:T(8,128)} %coefficient.5), kind=kLoop, calls=%fused_computation.3 | loop fusion | bytes 327680 | tf_op jit(solution)/shard_map/slice | solution.py:700
  2.4 0.0 copy-start
  2.4 5.1 %collective-permute-start = (f32[32,768]{1,0:T(8,128)S(1)}, f32[32,768]{1,0:T(8,128)S(1)}, u32[]{:S(2)}, u32[]{:S(2)}) collective-permute-start(f32[32,768]{1,0:T(8,128)S(1)} %pad_maximum_fusion), channel_id=1, source_target_pairs={{0,1},{1,2},{2,3},{4,5},{5,6},{6,7},{8,9},{9,10},{10,11},{12,13},{... | collective-permute-start | bytes 294920 | tf_op jit(solution)/shard_map/ppermute | solution.py:679
  7.5 0.0 copy-start.6
  7.5 1.3 %collective-permute-start.1 = (f32[32,768]{1,0:T(8,128)S(1)}, f32[32,768]{1,0:T(8,128)S(1)}, u32[]{:S(2)}, u32[]{:S(2)}) collective-permute-start(f32[32,768]{1,0:T(8,128)S(1)} %pad_maximum_fusion.1), channel_id=1, source_target_pairs={{1,0},{2,1},{3,2},{5,4},{6,5},{7,6},{9,8},{10,9},{11,10},{13,12},{... | collective-permute-start | bytes 294920 | tf_op jit(solution)/shard_map/ppermute | solution.py:679
  8.8 0.9 %collective-permute-done.low = f32[32,768]{1,0:T(8,128)S(1)} collective-permute-done((f32[32,768]{1,0:T(8,128)S(1)}, f32[32,768]{1,0:T(8,128)S(1)}, u32[]{:S(2)}, u32[]{:S(2)}) %collective-permute-start) | collective-permute-done | bytes 98336 | tf_op jit(solution)/shard_map/ppermute | solution.py:679
  9.7 4.3 %collective-permute-done.1.high = f32[32,768]{1,0:T(8,128)S(1)} collective-permute-done((f32[32,768]{1,0:T(8,128)S(1)}, f32[32,768]{1,0:T(8,128)S(1)}, u32[]{:S(2)}, u32[]{:S(2)}) %collective-permute-start.1) | collective-permute-done | bytes 98336 | tf_op jit(solution)/shard_map/ppermute | solution.py:679
  14.1 1.3 %shard_map.95 = (f32[32,1024]{1,0:T(8,128)S(1)}, f32[16,3584]{1,0:T(8,128)S(1)}, f32[16,3584]{1,0:T(8,128)S(1)}, f32[8,24,128]{2,1,0:T(8,128)S(1)}) custom-call(s32[32]{0:T(128)S(1)} %copy-done.6, f32[32,1024]{1,0:T(8,128)S(1)} %copy-done.1, f32[32,1024]{1,0:T(8,128)S(1)} %copy-done, f32[32,1024]{1,0:T(8,128)S(1)} %copy-done.2, ...), custom_call_target="tpu_custom_call" | custom-call | tf_op jit(solution)/shard_map/pallas_call | solution.py:661
  15.4 0.0 copy-start.3
  15.4 1.4 %collective-permute-start.2 = (f32[16,3584]{1,0:T(8,128)S(1)}, f32[16,3584]{1,0:T(8,128)S(1)}, u32[]{:S(2)}, u32[]{:S(2)}) collective-permute-start(f32[16,3584]{1,0:T(8,128)S(1)} %get-tuple-element.16), channel_id=1, source_target_pairs={{0,4},{4,8},{8,12},{12,16},{16,20},{20,24},{24,28},{1,5},{5,9},{9,... | collective-permute-start | bytes 688136 | tf_op jit(solution)/shard_map/ppermute | solution.py:679
  16.8 1.3 %collective-permute-start.3 = (f32[16,3584]{1,0:T(8,128)S(1)}, f32[16,3584]{1,0:T(8,128)S(1)}, u32[]{:S(2)}, u32[]{:S(2)}) collective-permute-start(f32[16,3584]{1,0:T(8,128)S(1)} %get-tuple-element.17), channel_id=1, source_target_pairs={{4,0},{8,4},{12,8},{16,12},{20,16},{24,20},{28,24},{5,1},{9,5},{13... | collective-permute-start | bytes 688136 | tf_op jit(solution)/shard_map/ppermute | solution.py:679
  18.1 11.7 %all_to_all.15.faces = f32[8,24,128]{2,1,0:T(8,128)S(1)} all-to-all(f32[8,24,128]{2,1,0:T(8,128)S(1)} %get-tuple-element.13), channel_id=1, replica_groups=mesh['gx'=8,'gy'=4] {'gx'}, dimensions={0} | all-to-all | bytes 196608 | tf_op jit(solution)/shard_map/all_to_all | solution.py:715
  29.8 0.6 copy-done.7
  30.5 2.3 %shard_map.96 = (f32[32,1024]{1,0:T(8,128)S(1)}, f32[8,16,256]{2,1,0:T(8,128)S(1)}) custom-call(s32[32]{0:T(128)S(1)} %copy-done.6, s32[3]{0:T(128)S(1)} %copy-done.7, f32[8,24,128]{2,1,0:T(8,128)S(1)} %all_to_all.15.faces, f32[32,1024]{1,0:T(8,128)S(1)} %bitcast.4, f32[32,1024]{1,0:T(8,128)S(1)} %bitcast.5, f32[32,1024]{1,0:T(8,128)S(1)} %bitcast.6), custom_call_target="tpu_custom_call" | custom-call | tf_op jit(solution)/shard_map/pallas_call | solution.py:661
  32.7 7.9 %all_to_all.16.arrived = f32[8,16,256]{2,1,0:T(8,128)S(1)} all-to-all(f32[8,16,256]{2,1,0:T(8,128)S(1)} %get-tuple-element.14), channel_id=1, replica_groups=mesh['gx'=8,'gy'=4] {'gx'}, dimensions={0} | all-to-all | bytes 262144 | tf_op jit(solution)/shard_map/all_to_all | solution.py:724
  40.6 1.2 %shard_map.97 = (f32[64,1024]{1,0:T(8,128)S(1)}, f32[64,512]{1,0:T(8,128)S(1)}, f32[64,512]{1,0:T(8,128)S(1)}) custom-call(s32[32]{0:T(128)S(1)} %copy-done.6, f32[8,16,256]{2,1,0:T(8,128)S(1)} %all_to_all.16.arrived, f32[32,1024]{1,0:T(8,128)S(1)} %get-tuple-element.15.residual, f32[32,1024]{1,0:T(8,128)S(1)} %copy-done.1, f32[32,1024]{1,0:T(8,128)S(1)} %copy-done, ...), custom_call_target="tpu_custom_call" | custom-call | tf_op jit(solution)/shard_map/pallas_call | solution.py:661
  41.9 3.5 %collective-permute-start.4 = (f32[64,512]{1,0:T(8,128)S(1)}, f32[64,512]{1,0:T(8,128)S(1)}, u32[]{:S(2)}, u32[]{:S(2)}) collective-permute-start(f32[64,512]{1,0:T(8,128)S(1)} %get-tuple-element.19), channel_id=1, source_target_pairs={{0,1},{1,2},{2,3},{4,5},{5,6},{6,7},{8,9},{9,10},{10,11},{12,13},{... | collective-permute-start | bytes 393224 | tf_op jit(solution)/shard_map/ppermute | solution.py:679
  45.3 1.3 %collective-permute-start.5 = (f32[64,512]{1,0:T(8,128)S(1)}, f32[64,512]{1,0:T(8,128)S(1)}, u32[]{:S(2)}, u32[]{:S(2)}) collective-permute-start(f32[64,512]{1,0:T(8,128)S(1)} %get-tuple-element.20), channel_id=1, source_target_pairs={{1,0},{2,1},{3,2},{5,4},{6,5},{7,6},{9,8},{10,9},{11,10},{13,12},{... | collective-permute-start | bytes 393224 | tf_op jit(solution)/shard_map/ppermute | solution.py:679
  46.6 1.2 %collective-permute-done.4.comp_low = f32[64,512]{1,0:T(8,128)S(1)} collective-permute-done((f32[64,512]{1,0:T(8,128)S(1)}, f32[64,512]{1,0:T(8,128)S(1)}, u32[]{:S(2)}, u32[]{:S(2)}) %collective-permute-start.4) | collective-permute-done | bytes 131104 | tf_op jit(solution)/shard_map/ppermute | solution.py:679
  47.8 4.4 %collective-permute-done.5.comp_high = f32[64,512]{1,0:T(8,128)S(1)} collective-permute-done((f32[64,512]{1,0:T(8,128)S(1)}, f32[64,512]{1,0:T(8,128)S(1)}, u32[]{:S(2)}, u32[]{:S(2)}) %collective-permute-start.5) | collective-permute-done | bytes 131104 | tf_op jit(solution)/shard_map/ppermute | solution.py:679
  52.2 5.6 %shard_map.98 = (f32[32,1024]{1,0:T(8,128)}, f32[8,16,256]{2,1,0:T(8,128)S(1)}) custom-call(s32[32]{0:T(128)S(1)} %copy-done.6, s32[3]{0:T(128)S(1)} %copy-done.7, f32[32,1024]{1,0:T(8,128)S(1)} %copy-done.1, f32[32,1024]{1,0:T(8,128)S(1)} %copy-done, f32[64,1024]{1,0:T(8,128)S(1)} %get-tuple-element.18.composite, ...), custom_call_target="tpu_custom_call" | custom-call | tf_op jit(solution)/shard_map/pallas_call | solution.py:661
  57.8 7.9 %all_to_all.17.arrived = f32[8,16,256]{2,1,0:T(8,128)S(1)} all-to-all(f32[8,16,256]{2,1,0:T(8,128)S(1)} %get-tuple-element.22), channel_id=1, replica_groups=mesh['gx'=8,'gy'=4] {'gx'}, dimensions={0} | all-to-all | bytes 262144 | tf_op jit(solution)/shard_map/all_to_all | solution.py:754
  65.7 1.4 %shard_map.99 = f32[32,1024]{1,0:T(8,128)} custom-call(s32[32]{0:T(128)S(1)} %copy-done.6, f32[8,16,256]{2,1,0:T(8,128)S(1)} %all_to_all.17.arrived, f32[32,1024]{1,0:T(8,128)S(1)} %get-tuple-element.23.smoothed), custom_call_target="tpu_custom_call" | custom-call | tf_op jit(solution)/shard_map/pallas_call | solution.py:661
  (16 shorter events, 0.1 us)
Async XLA Ops:
  2.3 11.7 %copy-start.1 = (f32[32,1024]{1,0:T(8,128)S(1)}, f32[32,1024]{1,0:T(8,128)}, u32[]{:S(2)}) copy-start(f32[32,1024]{1,0:T(8,128)} %start.5) | copy-start | bytes 393220
  2.4 11.7 %copy-start.2 = (f32[32,1024]{1,0:T(8,128)S(1)}, f32[32,1024]{1,0:T(8,128)}, u32[]{:S(2)}) copy-start(f32[32,1024]{1,0:T(8,128)} %source.1) | copy-start | bytes 393220
  2.4 11.7 %copy-start = (f32[32,1024]{1,0:T(8,128)S(1)}, f32[32,1024]{1,0:T(8,128)}, u32[]{:S(2)}) copy-start(f32[32,1024]{1,0:T(8,128)} %coefficient.5) | copy-start | bytes 393220
  2.4 7.3 %collective-permute-start = (f32[32,768]{1,0:T(8,128)S(1)}, f32[32,768]{1,0:T(8,128)S(1)}, u32[]{:S(2)}, u32[]{:S(2)}) collective-permute-start(f32[32,768]{1,0:T(8,128)S(1)} %pad_maximum_fusion), channel_id=1, source_target_pairs={{0,1},{1,2},{2,3},{4,5},{5,6},{6,7},{8,9},{9,10},{10,11},{12,13},{... | collective-permute-start | bytes 294920 | tf_op jit(solution)/shard_map/ppermute | solution.py:679
  7.5 6.6 %copy-start.6 = (s32[32]{0:T(128)S(1)}, s32[32]{0:T(128)}, u32[]{:S(2)}) copy-start(s32[32]{0:T(128)} %position.9) | copy-start | bytes 388
  7.5 6.5 %collective-permute-start.1 = (f32[32,768]{1,0:T(8,128)S(1)}, f32[32,768]{1,0:T(8,128)S(1)}, u32[]{:S(2)}, u32[]{:S(2)}) collective-permute-start(f32[32,768]{1,0:T(8,128)S(1)} %pad_maximum_fusion.1), channel_id=1, source_target_pairs={{1,0},{2,1},{3,2},{5,4},{6,5},{7,6},{9,8},{10,9},{11,10},{13,12},{... | collective-permute-start | bytes 294920 | tf_op jit(solution)/shard_map/ppermute | solution.py:679
  14.1 15.8 %copy-start.4 = (f32[1,32,1024]{2,1,0:T(8,128)S(1)}, f32[1,32,1024]{2,1,0:T(8,128)}, u32[]{:S(2)}) copy-start(f32[1,32,1024]{2,1,0:T(8,128)} %param.12) | copy-start | bytes 393220
  14.1 15.8 %copy-start.5 = (f32[1,32,1024]{2,1,0:T(8,128)S(1)}, f32[1,32,1024]{2,1,0:T(8,128)}, u32[]{:S(2)}) copy-start(f32[1,32,1024]{2,1,0:T(8,128)} %param.13) | copy-start | bytes 393220
  15.4 14.4 %copy-start.3 = (f32[1,32,1024]{2,1,0:T(8,128)S(1)}, f32[1,32,1024]{2,1,0:T(8,128)}, u32[]{:S(2)}) copy-start(f32[1,32,1024]{2,1,0:T(8,128)} %param.11) | copy-start | bytes 393220
  15.4 25.2 %collective-permute-start.2 = (f32[16,3584]{1,0:T(8,128)S(1)}, f32[16,3584]{1,0:T(8,128)S(1)}, u32[]{:S(2)}, u32[]{:S(2)}) collective-permute-start(f32[16,3584]{1,0:T(8,128)S(1)} %get-tuple-element.16), channel_id=1, source_target_pairs={{0,4},{4,8},{8,12},{12,16},{16,20},{20,24},{24,28},{1,5},{5,9},{9,... | collective-permute-start | bytes 688136 | tf_op jit(solution)/shard_map/ppermute | solution.py:679
  16.8 23.8 %collective-permute-start.3 = (f32[16,3584]{1,0:T(8,128)S(1)}, f32[16,3584]{1,0:T(8,128)S(1)}, u32[]{:S(2)}, u32[]{:S(2)}) collective-permute-start(f32[16,3584]{1,0:T(8,128)S(1)} %get-tuple-element.17), channel_id=1, source_target_pairs={{4,0},{8,4},{12,8},{16,12},{20,16},{24,20},{28,24},{5,1},{9,5},{13... | collective-permute-start | bytes 688136 | tf_op jit(solution)/shard_map/ppermute | solution.py:679
  29.8 0.7 copy-start.7
  41.9 6.0 %collective-permute-start.4 = (f32[64,512]{1,0:T(8,128)S(1)}, f32[64,512]{1,0:T(8,128)S(1)}, u32[]{:S(2)}, u32[]{:S(2)}) collective-permute-start(f32[64,512]{1,0:T(8,128)S(1)} %get-tuple-element.19), channel_id=1, source_target_pairs={{0,1},{1,2},{2,3},{4,5},{5,6},{6,7},{8,9},{9,10},{10,11},{12,13},{... | collective-permute-start | bytes 393224 | tf_op jit(solution)/shard_map/ppermute | solution.py:679
  45.3 6.9 %collective-permute-start.5 = (f32[64,512]{1,0:T(8,128)S(1)}, f32[64,512]{1,0:T(8,128)S(1)}, u32[]{:S(2)}, u32[]{:S(2)}) collective-permute-start(f32[64,512]{1,0:T(8,128)S(1)} %get-tuple-element.20), channel_id=1, source_target_pairs={{1,0},{2,1},{3,2},{5,4},{6,5},{7,6},{9,8},{10,9},{11,10},{13,12},{... | collective-permute-start | bytes 393224 | tf_op jit(solution)/shard_map/ppermute | solution.py:679

commit v2 on v1

v2 whole, which is shorter than its diff:
```python
import functools

import jax
import jax.numpy as jnp
from jax import lax
from jax.experimental import pallas as pl
from jax.experimental.pallas import tpu as pltpu
from jax.sharding import PartitionSpec as P

SWEEPS = 4
LANES = 128
ROWS = 8
F32 = jnp.float32
BF16 = jnp.bfloat16
VMEM = pl.BlockSpec(memory_space=pltpu.VMEM)
HBM = pl.BlockSpec(memory_space=pl.ANY)


def iotas(shape):
    return (
        lax.broadcasted_iota(jnp.int32, shape, 0),
        lax.broadcasted_iota(jnp.int32, shape, 1),
    )


def ones_where(mask):
    return jnp.where(mask, 1.0, 0.0).astype(BF16)


def select_dot(value, chosen):
    high = value.astype(BF16)
    rest = value - high.astype(F32)
    middle = rest.astype(BF16)
    low = (rest - middle.astype(F32)).astype(BF16)
    rows = value.shape[0]
    if rows % (2 * ROWS) == 0:
        parts = jnp.concatenate([low, middle, high], axis=0)
        whole = jnp.dot(parts, chosen, preferred_element_type=F32)
        return (whole[0:rows] + whole[rows : 2 * rows]) + whole[2 * rows :]
    total = jnp.dot(low, chosen, preferred_element_type=F32)
    total = total + jnp.dot(middle, chosen, preferred_element_type=F32)
    return total + jnp.dot(high, chosen, preferred_element_type=F32)


def ahead(value, lanes):
    return pltpu.roll(value, value.shape[1] - lanes, 1)


def behind(value, lanes):
    return pltpu.roll(value, lanes, 1)


def parity_block(row, shape, stride):
    x, lane = iotas(shape)
    return (x + row + lane // stride + lane % stride) % 2


def coarsening(edge, fine_lanes, coarse_lanes):
    half = edge // 2
    fine, coarse = iotas((fine_lanes, coarse_lanes))
    same_y = fine // edge // 2 == coarse // half
    return ones_where(same_y & (fine % edge // 2 == coarse % half))


def refining(edge, coarse_lanes, fine_lanes):
    half = edge // 2
    coarse, fine = iotas((coarse_lanes, fine_lanes))
    same_y = fine // edge // 2 == coarse // half
    return ones_where(same_y & (fine % edge // 2 == coarse % half))


def double_rows(ref, value):
    rows = value.shape[0]
    for tile in range(value.shape[1] // LANES):
        part = value[:, tile * LANES : (tile + 1) * LANES]
        ref[tile, pl.ds(0, rows, 2), :] = part
        ref[tile, pl.ds(1, rows, 2), :] = part


def pair_rows(ref, tile, first, rows):
    return ref[tile, pl.ds(first, rows, 2), :] + ref[tile, pl.ds(first + 1, rows, 2), :]


def tiles_of(lane):
    return slice(lane * LANES, (lane + 1) * LANES)


def flat(ref, rows, tiles):
    return jnp.concatenate([ref[tile, rows, :] for tile in tiles], axis=1)


def six_faces(k, k_low, k_high, stride, depth_edge):
    _, lane = iotas(k.shape)
    depth = lane % depth_edge
    first = depth == 0
    last = depth == depth_edge - 1
    w = [
        0.5 * (k + k_low),
        0.5 * (k + k_high),
        0.5 * (k + behind(k, stride)),
        0.5 * (k + ahead(k, stride)),
    ]
    z_low = 0.5 * (k + jnp.where(first, 0.0, behind(k, 1)))
    z_high = 0.5 * (k + jnp.where(last, 0.0, ahead(k, 1)))
    diagonal = ((w[0] + w[1]) + (w[2] + w[3])) + (z_low + z_high)
    return w + [jnp.where(first, 0.0, z_low), jnp.where(last, 0.0, z_high)], diagonal


def in_grid(shape, x_first, y_first, stride, x_cells, y_cells):
    x, lane = iotas(shape)
    x = x + x_first
    y = lane // stride + y_first
    return (x >= 0) & (x < x_cells) & (y >= 0) & (y < y_cells)


def two_sides(place_in_axis, size, even, odd):
    parity = place_in_axis % 2
    below = jnp.where(parity == 0, odd, even)
    above = jnp.where(parity == 0, even, odd)
    return (
        jnp.where(place_in_axis > 0, below, 0.0),
        jnp.where(place_in_axis < size - 1, above, 0.0),
    )


def place(positions, number, groups_y):
    _, lane = iotas(positions.shape)
    position = jnp.sum(jnp.where(lane == number, positions[...], 0))
    holder = position // 8
    return (holder // groups_y, position % 8)


def border_kernel(start, coefficient, even_packet, odd_packet, semaphores):
    last = start.shape[1] - LANES
    parity = lax.axis_index("gy") % 2
    copies = []
    for packet, at in (
        (even_packet, (1 - parity) * last),
        (odd_packet, parity * last),
    ):
        for goes, array in enumerate((start, coefficient)):
            copies.append(
                pltpu.make_async_copy(
                    array.at[:, pl.ds(pl.multiple_of(at, LANES), LANES)],
                    packet.at[:, tiles_of(goes)],
                    semaphores.at[len(copies)],
                )
            )
    for copy in copies:
        copy.start()
    for copy in copies:
        copy.wait()


def residual_kernel(
    groups_x, groups_y, position, start, coefficient, source, from_even, from_odd,
    residual, even_packet, odd_packet, slots,
    table, low, high,
):
    edge = start.shape[0]
    half = edge // 2
    lanes = start.shape[1]
    unit = LANES
    me = lax.axis_index("gx")
    mine_y = lax.axis_index("gy")
    table[...] = jnp.zeros_like(table)
    low[...], high[...] = two_sides(mine_y, groups_y, from_even[...], from_odd[...])

    wide = lanes + 2 * unit
    _, lane = iotas((ROWS, wide))
    depth = lane % edge
    blank = jnp.zeros((1, wide), F32)
    for row in range(0, edge, ROWS):
        rows = slice(row, row + ROWS)

        def widened(array, offset, rows=rows):
            return jnp.concatenate(
                [
                    low[rows, offset[0] : offset[0] + unit],
                    array[rows, :],
                    high[rows, offset[1] : offset[1] + unit],
                ],
                axis=1,
            )

        v = widened(start, (0, 0))
        k = widened(coefficient, (unit, unit))

        def term(k_other, v_other, k=k, v=v):
            return 0.5 * (k + k_other) * (v_other - v)

        total = term(behind(k, edge), behind(v, edge))
        total = total + term(ahead(k, edge), ahead(v, edge))
        first = depth == 0
        last = depth == edge - 1
        total = total + term(
            jnp.where(first, 0.0, behind(k, 1)), jnp.where(first, 0.0, behind(v, 1))
        )
        total = total + term(
            jnp.where(last, 0.0, ahead(k, 1)), jnp.where(last, 0.0, ahead(v, 1))
        )
        total = total[:, unit : unit + lanes]
        v = start[rows, :]
        k = coefficient[rows, :]

        def flux(near, k=k, v=v):
            return 0.5 * (k + coefficient[near, :]) * (start[near, :] - v)

        x, _ = iotas((ROWS, lanes))
        if row == 0:
            near = jnp.concatenate([start[0:1, :], start[0 : ROWS - 1, :]], axis=0)
            knear = jnp.concatenate(
                [coefficient[0:1, :], coefficient[0 : ROWS - 1, :]], axis=0
            )
            total = total + 0.5 * (k + knear) * (near - v)
        else:
            total = total + flux(slice(row - 1, row + ROWS - 1))
        if row + ROWS == edge:
            near = jnp.concatenate(
                [start[row + 1 : edge, :], start[edge - 1 : edge, :]], axis=0
            )
            knear = jnp.concatenate(
                [coefficient[row + 1 : edge, :], coefficient[edge - 1 : edge, :]], axis=0
            )
            total = total + 0.5 * (k + knear) * (near - v)
        else:
            total = total + flux(slice(row + 1, row + ROWS + 1))
        residual[rows, :] = source[rows, :] + total

    body = 2 * lanes + 2 * unit

    def pack(buffer, rows, k_row, v_row):
        buffer[:, 0:lanes] = residual[rows, :]
        buffer[:, lanes : lanes + unit] = low[rows, unit:]
        buffer[:, lanes + unit : 2 * lanes + unit] = coefficient[rows, :]
        buffer[:, 2 * lanes + unit : body] = high[rows, unit:]
        buffer[:, body:] = jnp.zeros((half, buffer.shape[1] - body), F32)
        pieces = [(start, v_row, at) for at in range(0, lanes, unit)]
        pieces.append((low, k_row, unit))
        pieces = pieces + [(coefficient, k_row, at) for at in range(0, lanes, unit)]
        pieces.append((high, k_row, unit))
        for number, (array, row, at) in enumerate(pieces):
            spot = body + number // half * unit
            line = number % half
            buffer[line : line + 1, spot : spot + unit] = array[row : row + 1, at : at + unit]

    for parity in range(2):
        upper, lower = (even_packet, odd_packet) if parity == 0 else (odd_packet, even_packet)

        @pl.when(me % 2 == parity)
        def _(upper=upper, lower=lower):
            pack(upper, slice(half, edge), half - 1, edge - 1)
            pack(lower, slice(0, half), half, 0)

    span = half * edge
    tiles = span // unit
    unit_y = unit // edge
    wide = span + 2 * unit
    at, to = iotas((wide, unit))
    y = at // edge - unit_y
    z = at % edge
    for octant_x in range(2):
        for octant_y in range(2):
            octant_z = (octant_x + octant_y) % 2
            rows = slice(octant_x * half, octant_x * half + half)
            begin = octant_y * span
            left = (
                low[rows, 0:unit] if octant_y == 0 else start[rows, begin - unit : begin]
            )
            right = (
                start[rows, begin + span : begin + span + unit]
                if octant_y == 0
                else high[rows, 0:unit]
            )
            block = jnp.concatenate([left, start[rows, begin : begin + span], right], axis=1)
            near_z = half if octant_z == 0 else half - 1
            goal = (2 + octant_z) * half
            chosen = (
                ((y == -1) & (to < half) & (z == octant_z * half + to))
                | ((y == half) & (to // half == 1) & (z == octant_z * half + to - half))
                | ((z == near_z) & (to // half == 2 + octant_z) & (y == to - goal))
            )
            entry = 2 * octant_x + octant_y
            table[entry, 0:half, :] = select_dot(block, ones_where(chosen))
            inner = (half, half + ROWS) if octant_x == 0 else (half - ROWS, half)
            outer = (edge - ROWS, edge) if octant_x == 0 else (0, ROWS)
            pick = 0 if octant_x == 0 else ROWS - 1
            outer_pick = ROWS - 1 if octant_x == 0 else 0
            other = 4 + 2 * octant_x + octant_y
            for (first_row, last_row), which, goes, side in (
                (inner, pick, entry, 1 - octant_x),
                (outer, outer_pick, other, octant_x),
            ):
                plane = start[first_row:last_row, begin : begin + span]
                if octant_z == 1:
                    plane = ahead(plane, half)
                for tile in range(tiles):
                    line = half + side * tiles + tile
                    table[goes, line : line + 1, :] = plane[
                        which : which + 1, tile * unit : (tile + 1) * unit
                    ]

    for holder in range(groups_x):
        owner, octant = place(position, holder * groups_y + mine_y, groups_y)
        octant_x = octant // 4
        octant_y = octant // 2 % 2
        entry = jnp.where(
            owner == me,
            2 * octant_x + octant_y,
            jnp.where(owner == me + 1, 4 + octant_y, 6 + octant_y),
        )
        slots[holder] = table[entry]


def box_terms_kernel(source, coefficient, start, weights, inverse, base):
    edge = source.shape[0]
    lanes = source.shape[1]
    _, lane = iotas((ROWS, lanes))
    first_y = lane < edge
    last_y = lane >= lanes - edge
    first_z = lane % edge == 0
    last_z = lane % edge == edge - 1

    def shifted_rows(array, row):
        block = array[row : row + ROWS, :]
        if row == 0:
            low = jnp.concatenate([block[0:1, :], array[0 : ROWS - 1, :]], axis=0)
        else:
            low = array[row - 1 : row + ROWS - 1, :]
        if row + ROWS == edge:
            high = jnp.concatenate([array[row + 1 : edge, :], block[ROWS - 1 :, :]], axis=0)
        else:
            high = array[row + 1 : row + ROWS + 1, :]
        return (
            block, low, high,
            behind(block, edge), ahead(block, edge), behind(block, 1), ahead(block, 1),
        )

    for row in range(0, edge, ROWS):
        rows = slice(row, row + ROWS)
        x, _ = iotas((ROWS, lanes))
        outside = (x + row == 0, x + row == edge - 1, first_y, last_y, first_z, last_z)
        k, *around = shifted_rows(coefficient, row)
        v, *beside = shifted_rows(start, row)
        total = None
        sums = None
        for number in range(6):
            face = 0.5 * (k + around[number])
            whole = jnp.where(outside[number], k, face)
            inner = jnp.where(outside[number], 0.0, face)
            weights[number, rows, :] = inner
            sums = whole if sums is None else sums + whole
            term = inner * beside[number]
            total = term if total is None else total + term
        inverse[rows, :] = 1.0 / (4.0 * sums)
        base[rows, :] = source[rows, :] + 4.0 * total


def fine_kernel(
    groups_x, groups_y, position, colours, faces, source, coefficient, start,
    weights, inverse, base_terms,
    smoothed, slots,
    ghost, values, kept,
):
    edge = source.shape[0]
    half = edge // 2
    lanes = source.shape[1]
    me = lax.axis_index("gx") * groups_y + lax.axis_index("gy")
    owner, octant = place(position, me, groups_y)
    octant_x = octant // 4
    leading = colours[0:1, 0:1]
    span = half * edge
    tiles = span // LANES

    at, to = iotas((4 * half, lanes))
    fine_y = to // edge
    fine_z = to % edge
    chosen = (
        ((fine_y == 0) & (at == fine_z // 2))
        | ((fine_y == edge - 1) & (at == half + fine_z // 2))
        | ((fine_z == edge - 1) & (at == 2 * half + fine_y // 2))
        | ((fine_z == 0) & (at == 3 * half + fine_y // 2))
    )
    base = faces[owner]
    sides = select_dot(base[0:half, 0 : 4 * half], ones_where(chosen))
    double_rows(ghost, sides)
    before = faces[jnp.maximum(owner - 1, 0)][half:, :]
    after = faces[jnp.minimum(owner + 1, groups_x - 1)][half:, :]
    base = base[half:, :]
    before = jnp.where(owner > 0, before, 0.0)
    after = jnp.where(owner < groups_x - 1, after, 0.0)
    line, _ = iotas(base.shape)
    planes = jnp.where(
        line < tiles,
        jnp.where(octant_x == 0, before, base),
        jnp.where(octant_x == 1, after, base),
    )
    unit_fine = 2 * LANES
    at, to = iotas((LANES, unit_fine))
    grown = select_dot(
        planes,
        ones_where((at // edge == to // edge // 2) & (at % edge == to % edge // 2)),
    )
    for tile in range(tiles):
        for part in range(2):
            at = 2 * tile + part
            extra = grown[:, part * LANES : (part + 1) * LANES]
            ghost[at, 0:1, :] = ghost[at, 0:1, :] + extra[tile : tile + 1, :]
            ghost[at, edge - 1 : edge, :] = (
                ghost[at, edge - 1 : edge, :] + extra[tiles + tile : tiles + tile + 1, :]
            )
    every = range(lanes // LANES)


    edges = jnp.zeros((ROWS, lanes), F32)
    values[0:ROWS, :] = edges
    values[edge + ROWS :, :] = edges
    values[ROWS : edge + ROWS, :] = start[...]

    def coupled(row):
        at = row + ROWS
        rows = slice(row, row + ROWS)
        v = values[at : at + ROWS, :]
        total = weights[0, rows, :] * values[at - 1 : at + ROWS - 1, :]
        total = total + weights[1, rows, :] * values[at + 1 : at + ROWS + 1, :]
        total = total + weights[2, rows, :] * behind(v, edge)
        total = total + weights[3, rows, :] * ahead(v, edge)
        total = total + weights[4, rows, :] * behind(v, 1)
        return total + weights[5, rows, :] * ahead(v, 1), v

    for row in range(0, edge, ROWS):
        rows = slice(row, row + ROWS)
        extra = 4.0 * coefficient[rows, :] * flat(ghost, rows, every)
        parity = parity_block(row, (ROWS, lanes), edge)
        values[row + ROWS : row + 2 * ROWS, :] = jnp.where(
            parity == leading, (base_terms[rows, :] + extra) * inverse[rows, :], start[rows, :]
        )
        kept[rows, :] = source[rows, :] + extra
    for row in range(0, edge, ROWS):
        rows = slice(row, row + ROWS)
        total, v = coupled(row)
        parity = parity_block(row, v.shape, edge)
        smoothed[rows, :] = jnp.where(
            parity == leading, v, (kept[rows, :] + 4.0 * total) * inverse[rows, :]
        )
    values[ROWS : edge + ROWS, :] = smoothed[...]
    for row in range(0, edge, ROWS):
        rows = slice(row, row + ROWS)
        total, v = coupled(row)
        parity = parity_block(row, v.shape, edge)
        value = jnp.where(
            parity == leading, (source[rows, :] - base_terms[rows, :]) + 4.0 * total, 0.0
        )
        for tile in every:
            ghost[tile, rows, :] = value[:, tiles_of(tile)]
    chosen = coarsening(edge, 4 * LANES, LANES)
    for part in range(lanes // (4 * LANES)):
        block = jnp.concatenate(
            [pair_rows(ghost, 4 * part + tile, 0, half) for tile in range(4)], axis=1
        )
        mean = 0.125 * select_dot(block, chosen)
        for holder in range(groups_x):
            slots[holder, :, part * LANES : (part + 1) * LANES] = mean


def coarse_kernel(
    groups_x, groups_y, position, colours, arrived, residual, start, coefficient,
    y_even, y_odd, from_even, from_odd,
    source_b, coefficient_b, correction, even_packet, odd_packet,
    grown, kext, comp, extra_v, weights, inverse, first_values, second_values, left, ktiles,
):
    edge = start.shape[0]
    half = edge // 2
    lanes = start.shape[1]
    span = half * edge
    unit = LANES
    me = lax.axis_index("gx")
    mine_y = lax.axis_index("gy")
    wide = lanes + 2 * unit
    body = lanes + wide
    rows_all = 2 * edge
    top = half + ROWS
    own = slice(unit, unit + lanes)

    k_low, k_high = two_sides(mine_y, groups_y, y_even[:, unit:], y_odd[:, unit:])
    kext[top : top + edge, 0:unit] = k_low
    kext[top : top + edge, own] = coefficient[...]
    kext[top : top + edge, unit + lanes :] = k_high
    kext[0:ROWS, :] = jnp.zeros((ROWS, wide), F32)
    kext[top + edge + half :, :] = jnp.zeros((ROWS, wide), F32)
    comp[:, 0:unit] = jnp.zeros((rows_all, unit), F32)
    comp[:, unit + lanes :] = jnp.zeros((rows_all, unit), F32)
    comp[half : half + edge, own] = residual[...]

    def unpack(block, there, k_rows, c_rows, k_row, number):
        comp[c_rows, own] = jnp.where(there, block[:, 0:lanes], 0.0)
        kext[k_rows, :] = jnp.where(there, block[:, lanes:body], 0.0)
        for piece in range((lanes + wide) // unit):
            spot = body + piece // half * unit
            line = piece % half
            value = jnp.where(there, block[line : line + 1, spot : spot + unit], 0.0)
            if piece < lanes // unit:
                extra_v[number : number + 1, tiles_of(piece)] = value
            else:
                kext[k_row : k_row + 1, tiles_of(piece - lanes // unit)] = value

    for parity in range(2):
        above, below = (from_even, from_odd) if parity == 0 else (from_odd, from_even)

        @pl.when(me % 2 == parity)
        def _(above=above, below=below):
            unpack(below, me > 0, slice(ROWS, top), slice(0, half), ROWS - 1, 0)
            last = top + edge
            unpack(
                above, me < groups_x - 1, slice(last, last + half),
                slice(half + edge, rows_all), last + half, 1,
            )

    for number, mine, theirs in ((0, half, half - 1), (1, half + edge - 1, half + edge)):
        v = start[mine - half : mine - half + 1, :]
        k = kext[mine + ROWS : mine + ROWS + 1, own]
        k_other = kext[theirs + ROWS : theirs + ROWS + 1, own]
        flux = 0.5 * (k + k_other) * (v - extra_v[number : number + 1, :])
        comp[mine : mine + 1, own] = comp[mine : mine + 1, own] - flux
        comp[theirs : theirs + 1, own] = comp[theirs : theirs + 1, own] + flux

    at, to = iotas((unit, 2 * unit))
    chosen = ones_where((at // half == to // edge) & (at % half == to % half))
    for part in range(arrived.shape[2] // unit):
        every = arrived[:, :, tiles_of(part)].reshape(groups_x * half, unit)
        grown[:, part * 2 * unit : (part + 1) * 2 * unit] = select_dot(every, chosen)
    _, lane = iotas((half, span))
    half_of = lane % edge // half
    for holder in range(groups_x):
        owner, octant = place(position, holder * groups_y + mine_y, groups_y)
        block = 2 * (owner - me) + octant // 4 + 1

        @pl.when((block >= 0) & (block < 4))
        def _(holder=holder, octant=octant, block=block):
            rows = pl.ds(pl.multiple_of(block * half, half), half)
            where = pl.ds(pl.multiple_of(unit + octant // 2 % 2 * span, unit), span)
            comp[rows, where] = jnp.where(
                half_of == octant % 2,
                grown[holder * half : (holder + 1) * half, :],
                comp[rows, where],
            )

    zero_rows = jnp.zeros((ROWS, wide), F32)
    for ref in (first_values, second_values):
        ref[0:ROWS, :] = zero_rows
        ref[ROWS + rows_all :, :] = zero_rows
    leading = colours[0:1, 1:2]
    shape = (ROWS, wide)
    for row in range(0, rows_all, ROWS):
        at = row + ROWS
        rows = slice(row, row + ROWS)
        w, diagonal = six_faces(
            kext[at : at + ROWS, :],
            kext[at - 1 : at + ROWS - 1, :],
            kext[at + 1 : at + ROWS + 1, :],
            edge,
            edge,
        )
        for number in range(6):
            weights[number, rows, :] = w[number]
        inside = in_grid(
            shape, row - half + me * edge, mine_y * edge - unit // edge, edge,
            groups_x * edge, groups_y * edge,
        )
        inv = jnp.where(inside, 1.0 / diagonal, 0.0)
        inverse[rows, :] = inv
        parity = parity_block(row, shape, edge)
        first_values[at : at + ROWS, :] = jnp.where(
            parity == leading, comp[rows, :] * inv, 0.0
        )

    def coupled(ref, row):
        at = row + ROWS
        rows = slice(row, row + ROWS)
        v = ref[at : at + ROWS, :]
        total = weights[0, rows, :] * ref[at - 1 : at + ROWS - 1, :]
        total = total + weights[1, rows, :] * ref[at + 1 : at + ROWS + 1, :]
        total = total + weights[2, rows, :] * behind(v, edge)
        total = total + weights[3, rows, :] * ahead(v, edge)
        total = total + weights[4, rows, :] * behind(v, 1)
        return total + weights[5, rows, :] * ahead(v, 1), v

    for row in range(0, rows_all, ROWS):
        rows = slice(row, row + ROWS)
        total, v = coupled(first_values, row)
        parity = parity_block(row, v.shape, edge)
        second_values[row + ROWS : row + 2 * ROWS, :] = jnp.where(
            parity == leading, v, (comp[rows, :] + total) * inverse[rows, :]
        )
    for row in range(0, rows_all, ROWS):
        rows = slice(row, row + ROWS)
        total, v = coupled(second_values, row)
        parity = parity_block(row, v.shape, edge)
        total = jnp.where(parity == leading, total, 0.0)
        for tile in range(wide // unit):
            left[tile, rows, :] = total[:, tiles_of(tile)]
        for tile in range(lanes // unit):
            ktiles[tile, rows, :] = kext[row + ROWS : row + 2 * ROWS, tiles_of(tile + 1)]

    chosen = coarsening(edge, 4 * unit, unit)

    def pairs(ref, tiles):
        return jnp.concatenate([pair_rows(ref, tile, 0, edge) for tile in tiles], axis=1)

    blocks = lanes // unit // 4
    last = wide // unit - 1
    source_b[:, 0:unit] = 0.125 * select_dot(pairs(left, [0]), chosen[3 * unit :, :])
    source_b[:, (blocks + 1) * unit :] = 0.125 * select_dot(
        pairs(left, [last]), chosen[0:unit, :]
    )
    for part in range(blocks):
        source_b[:, tiles_of(part + 1)] = 0.125 * select_dot(
            pairs(left, range(4 * part + 1, 4 * part + 5)), chosen
        )
        coefficient_b[:, tiles_of(part)] = 0.125 * select_dot(
            pairs(ktiles, range(4 * part, 4 * part + 4)), chosen
        )
    middle = (blocks + 2) // 2 * unit
    rows = slice(ROWS + half, ROWS + half + edge)
    correction[...] = second_values[rows, own]
    for parity in range(2):
        up, down = (even_packet, odd_packet) if parity == 0 else (odd_packet, even_packet)

        @pl.when(mine_y % 2 == parity)
        def _(up=up, down=down):
            up[:, 0:middle] = source_b[:, middle:]
            up[:, middle : middle + unit] = coefficient_b[:, (blocks - 1) * unit :]
            up[:, middle + unit :] = second_values[rows, unit + lanes :]
            down[:, 0:middle] = source_b[:, 0:middle]
            down[:, middle : middle + unit] = coefficient_b[:, 0:unit]
            down[:, middle + unit :] = second_values[rows, 0:unit]


def bottom_kernel(
    groups_x, groups_y, position, colours, source_b, coefficient_b, correction,
    from_even, from_odd,
    corrected, slots,
    bottom, spread, table, low, high,
):
    edge = correction.shape[0]
    half = edge // 2
    lanes = correction.shape[1]
    span = half * edge
    unit = LANES
    me = lax.axis_index("gx")
    mine_y = lax.axis_index("gy")
    low[...], high[...] = two_sides(mine_y, groups_y, from_even[...], from_odd[...])
    shape = source_b.shape
    middle = shape[1] // 2
    f_bottom = source_b[...] + jnp.concatenate([low[:, 0:middle], high[:, 0:middle]], axis=1)
    k_bottom = jnp.concatenate(
        [
            low[:, middle : middle + unit],
            coefficient_b[...],
            high[:, middle : middle + unit],
        ],
        axis=1,
    )
    quarter = half // 2

    def rows_behind(value):
        return pltpu.roll(value, 1, 0)

    def rows_ahead(value):
        return pltpu.roll(value, edge - 1, 0)

    w, diagonal = six_faces(k_bottom, rows_behind(k_bottom), rows_ahead(k_bottom), half, half)
    inside = in_grid(
        shape, me * half - quarter, mine_y * half - unit // half, half,
        groups_x * half, groups_y * half,
    )
    inv = jnp.where(inside, 1.0 / (0.25 * diagonal), 0.0)
    w = [0.25 * one for one in w]
    parity = parity_block(0, shape, half)
    values = jnp.zeros(shape, F32)
    first = colours[0:1, 2:3]
    for step in range(2 * SWEEPS):
        colour = first if step % 2 == 0 else 1 - first
        if step == 0:
            total = f_bottom
        else:
            total = f_bottom + w[0] * rows_behind(values)
            total = total + w[1] * rows_ahead(values)
            total = total + w[2] * behind(values, half)
            total = total + w[3] * ahead(values, half)
            total = total + w[4] * behind(values, 1)
            total = total + w[5] * ahead(values, 1)
        values = jnp.where(parity == colour, total * inv, values)
    bottom[...] = values

    chosen = refining(edge, unit, 4 * unit)
    for part in range(lanes // (4 * unit)):
        block = bottom[quarter : quarter + half, tiles_of(part + 1)]
        double_rows(spread.at[pl.ds(4 * part, 4)], select_dot(block, chosen))
    every = range(lanes // unit)
    for row in range(0, edge, ROWS):
        rows = slice(row, row + ROWS)
        total = correction[rows, :] + flat(spread, rows, every)
        ring = [total[:, tiles_of(tile)] for tile in every]
        ring[0] = ring[0] + low[rows, middle + unit :]
        ring[-1] = ring[-1] + high[rows, middle + unit :]
        total = jnp.concatenate(ring, axis=1)
        corrected[rows, :] = total

    at, to = iotas((2 * unit, unit))
    chosen = ones_where((at // edge == to // half) & (at % edge == to % half))
    for octant_x in range(2):
        for octant_y in range(2):
            block = corrected[
                octant_x * half : (octant_x + 1) * half,
                octant_y * span : (octant_y + 1) * span,
            ]
            if (octant_x + octant_y) % 2 == 1:
                block = ahead(block, half)
            for part in range(span // (2 * unit)):
                table[2 * octant_x + octant_y, :, part * unit : (part + 1) * unit] = select_dot(
                    block[:, part * 2 * unit : (part + 1) * 2 * unit], chosen
                )
    for holder in range(groups_x):
        owner, octant = place(position, holder * groups_y + mine_y, groups_y)
        slots[holder] = table[octant // 4 * 2 + octant // 2 % 2]


def finish_kernel(
    groups_y, position, arrived, smoothed, start, correction, coarse_out, out, grown
):
    edge = smoothed.shape[0]
    half = edge // 2
    me = lax.axis_index("gx") * groups_y + lax.axis_index("gy")
    owner, _ = place(position, me, groups_y)
    coarse_out[...] = start[...] + correction[...]
    value = arrived[owner]
    chosen = refining(edge, LANES, 4 * LANES)
    for part in range(value.shape[1] // LANES):
        fine = select_dot(value[:, tiles_of(part)], chosen)
        double_rows(grown.at[pl.ds(4 * part, 4)], fine)
    out[...] = smoothed[...] + flat(grown, slice(0, edge), range(smoothed.shape[1] // LANES))


def call(kernel, outs, scratch, specs, *operands):
    return pl.pallas_call(
        kernel,
        out_shape=[jax.ShapeDtypeStruct(shape, F32) for shape in outs],
        in_specs=specs,
        out_specs=[VMEM] * len(outs),
        scratch_shapes=[pltpu.VMEM(shape, F32) for shape in scratch],
        compiler_params=pltpu.CompilerParams(vmem_limit_bytes=40 * 1024 * 1024),
    )(*operands)


def tiled(rows, lanes):
    return (lanes // LANES, rows, LANES)


def matching(axis, first):
    sizes = (lax.axis_size("gx"), lax.axis_size("gy"))
    along_x = axis == "gx"
    size, others = sizes if along_x else sizes[::-1]
    pairs = []
    for other in range(others):
        for i in range(size):
            j = i + 1 if (i - first) % 2 == 0 else i - 1
            goes, beside = j, other
            if not 0 <= j < size:
                goes, beside = i, other ^ 1
            if beside < others:
                here, there = (i, other), (goes, beside)
                if not along_x:
                    here, there = here[::-1], there[::-1]
                pairs.append((here[0] * sizes[1] + here[1], there[0] * sizes[1] + there[1]))
    return pairs


def swapped(even_packet, odd_packet, axis):
    return tuple(
        lax.ppermute(packet, ("gx", "gy"), matching(axis, first))
        for first, packet in ((0, even_packet), (1, odd_packet))
    )


def on_device(
    coarse_source,
    coarse_coefficient,
    coarse_start,
    fine_source,
    fine_coefficient,
    fine_start,
    fine_position,
    first_colour,
):
    groups_x = lax.axis_size("gx")
    groups_y = lax.axis_size("gy")
    edge, lanes = coarse_source.shape
    half = edge // 2
    span = half * edge
    compact = half * half
    wide = lanes + 2 * LANES
    positions = fine_position.reshape(1, -1)
    colours = first_colour.reshape(1, -1)
    packets = pl.pallas_call(
        border_kernel,
        out_shape=[jax.ShapeDtypeStruct((edge, 2 * LANES), F32)] * 2,
        in_specs=[HBM] * 2,
        out_specs=[VMEM] * 2,
        scratch_shapes=[pltpu.SemaphoreType.DMA((4,))],
    )(coarse_start, coarse_coefficient)
    y_even, y_odd = swapped(*packets, "gy")
    box = (fine_source[0], fine_coefficient[0], fine_start[0])
    weights, inverse, base = call(
        box_terms_kernel, [(6, edge, lanes), (edge, lanes), (edge, lanes)], [], [VMEM] * 3, *box
    )
    extra = -(-(lanes + wide) // LANES // half) * LANES
    packed = lanes + wide + extra
    face_rows = half + 2 * (span // LANES)
    residual, even_packet, odd_packet, slots = call(
        functools.partial(residual_kernel, groups_x, groups_y),
        [(edge, lanes), (half, packed), (half, packed), (groups_x, face_rows, LANES)],
        [(8, face_rows, LANES), (edge, 2 * LANES), (edge, 2 * LANES)],
        [VMEM] * 6,
        positions, coarse_start, coarse_coefficient, coarse_source, y_even, y_odd,
    )
    from_even, from_odd = swapped(even_packet, odd_packet, "gx")
    faces = lax.all_to_all(slots, "gx", 0, 0, tiled=True)
    smoothed, restricted = call(
        functools.partial(fine_kernel, groups_x, groups_y),
        [(edge, lanes), (groups_x, half, compact)],
        [tiled(edge, lanes), (edge + 2 * ROWS, lanes), (edge, lanes)],
        [VMEM] * 9,
        positions, colours, faces, *box, weights, inverse, base,
    )
    arrived = lax.all_to_all(restricted, "gx", 0, 0, tiled=True)
    rows = 2 * edge
    lanes_b = (wide // LANES - 2) // 4 * LANES
    source_b, coefficient_b, correction, even_packet, odd_packet = call(
        functools.partial(coarse_kernel, groups_x, groups_y),
        [
            (edge, lanes_b + 2 * LANES),
            (edge, lanes_b),
            (edge, lanes),
            (edge, lanes_b // 2 + 3 * LANES),
            (edge, lanes_b // 2 + 3 * LANES),
        ],
        [
            (groups_x * half, span),
            (rows + 2 * ROWS, wide),
            (rows, wide),
            (ROWS, lanes),
            (6, rows, wide),
            (rows, wide),
            (rows + 2 * ROWS, wide),
            (rows + 2 * ROWS, wide),
            tiled(rows, wide),
            tiled(rows, lanes),
        ],
        [VMEM] * 10,
        positions, colours, arrived, residual, coarse_start, coarse_coefficient,
        y_even, y_odd, from_even, from_odd,
    )
    y_even, y_odd = swapped(even_packet, odd_packet, "gy")
    corrected, slots = call(
        functools.partial(bottom_kernel, groups_x, groups_y),
        [(edge, lanes), (groups_x, half, compact)],
        [(edge, lanes_b + 2 * LANES), tiled(edge, lanes), (4, half, compact)]
        + [(edge, lanes_b // 2 + 3 * LANES)] * 2,
        [VMEM] * 7,
        positions, colours, source_b, coefficient_b, correction, y_even, y_odd,
    )
    returned = lax.all_to_all(slots, "gx", 0, 0, tiled=True)
    coarse_solution, fine_solution = call(
        functools.partial(finish_kernel, groups_y),
        [(edge, lanes), (edge, lanes)],
        [tiled(edge, lanes)],
        [VMEM] * 5,
        positions, returned, smoothed, coarse_start, corrected,
    )
    return (coarse_solution, fine_solution[None])


def solution(mesh):
    placed = (
        P("gx", "gy"),
        P("gx", "gy"),
        P("gx", "gy"),
        P(("gx", "gy"), None, None),
        P(("gx", "gy"), None, None),
        P(("gx", "gy"), None, None),
        P(),
        P(),
    )
    return jax.shard_map(
        on_device,
        mesh=mesh,
        in_specs=placed,
        out_specs=(P("gx", "gy"), P(("gx", "gy"), None, None)),
        check_vma=False,
    )
```

time: 67.6 us -> 49.1 us (0.73)
  blocking collectives: 27.5 us -> 7.89 us
  starting transfers between devices: 13.9 us -> 16.8 us
  Pallas kernels: 11.8 us -> 10.3 us
  local copies, waits for them, and re-layouts: 2.4 us -> 1.58 us
    all_to_all x2 -> x0, blocking collectives: 19.6 us -> none  [the longest x1 11.7 us: on_device(): faces = lax.all_to_all(slots, 'gx', 0, 0, tiled=True)]
    all_to_all x0 -> x2, starting transfers between devices: none -> 7.67 us  [the longest x1 4.3 us: on_device(): faces = lax.all_to_all(slots, 'gx', 0, 0, tiled=True)]
    all_to_all x0 -> x2, waiting for transfers between devices: none -> 7.03 us  [the longest x1 5.41 us: on_device(): arrived = lax.all_to_all(restricted, 'gx', 0, 0, tiled=True)]
    ppermute x6, waiting for transfers between devices: 10.8 us -> 4.35 us  [swapped(): lax.ppermute(packet, ('gx', 'gy'), matching(axis, first))]
    ppermute x6, starting transfers between devices: 13.9 us -> 9.1 us  [swapped(): lax.ppermute(packet, ('gx', 'gy'), matching(axis, first))]
    pallas_call x5 -> x6, Pallas kernels: 11.8 us -> 8.79 us  [call(): pl.pallas_call(kernel, out_shape=[jax.ShapeDtypeStruct(shape, F32) for sh...]
    slice x2 -> x0, local copies, waits for them, and re-layouts: 1.71 us -> none  [the longest x1 0.97 us: on_device(): coarse_coefficient[:, :pad]]
    pallas_call x0 -> x1, Pallas kernels: none -> 1.49 us  [on_device(): pl.pallas_call(border_kernel, out_shape=[jax.ShapeDtypeStruct((edge, 2 *...]
  transfers between devices with their start and end apart: 6 -> 8, of which waited for: 4 -> 4; matrix products, arithmetic and copies ran while one was open for 0% -> 0% of each run, Pallas kernels for 3% -> 4%
where the time goes in v2:
time: 49.1 us; the launch traced here: 48.6 us
  starting transfers between devices  16.8 us (34%)
  waiting for transfers between devices  11.4 us (23%)
  Pallas kernels  10.3 us (21%)
  blocking collectives  7.89 us (16%)
  local copies, waits for them, and re-layouts  1.58 us (3%)
  between operations  0.73 us (1%)
    ppermute x6, starting transfers between devices, swapped(): lax.ppermute(packet, ('gx', 'gy'), matching(axis, first))  9.1 us
    pallas_call x6, Pallas kernels, call(): pl.pallas_call(kernel, out_shape=[jax.ShapeDtypeStruct(shape, F32) for sh...  8.79 us
    all_to_all x1, blocking collectives, on_device(): returned = lax.all_to_all(slots, 'gx', 0, 0, tiled=True)  7.89 us
    all_to_all x1, waiting for transfers between devices, on_device(): arrived = lax.all_to_all(restricted, 'gx', 0, 0, tiled=True)  5.41 us
    ppermute x6, waiting for transfers between devices, swapped(): lax.ppermute(packet, ('gx', 'gy'), matching(axis, first))  4.35 us
    all_to_all x1, starting transfers between devices, on_device(): faces = lax.all_to_all(slots, 'gx', 0, 0, tiled=True)  4.3 us
    all_to_all x1, starting transfers between devices, on_device(): arrived = lax.all_to_all(restricted, 'gx', 0, 0, tiled=True)  3.37 us
    all_to_all x1, waiting for transfers between devices, on_device(): faces = lax.all_to_all(slots, 'gx', 0, 0, tiled=True)  1.62 us
  transfers between devices with their start and end apart: 8, of which 4 were waited for; matrix products, arithmetic and copies ran while one was open for 0% of the time, Pallas kernels for 4%

profile of v2, /device:TPU:0, one launch (start us, length us, event | category | flops | bytes accessed | tf_op | source)
XLA Modules:
  0.0 48.6 jit_solution(4147370814059237332)
XLA Ops:
  0.6 1.5 %shard_map.95 = (f32[32,256]{1,0:T(8,128)}, f32[32,256]{1,0:T(8,128)}) custom-call(f32[32,1024]{1,0:T(8,128)} %start.7, f32[32,1024]{1,0:T(8,128)} %coefficient.5), custom_call_target="tpu_custom_call" | custom-call | tf_op jit(solution)/shard_map/pallas_call | solution.py:805
  2.1 3.1 %collective-permute-start = (f32[32,256]{1,0:T(8,128)}, f32[32,256]{1,0:T(8,128)S(1)}, u32[]{:S(2)}, u32[]{:S(2)}) collective-permute-start(f32[32,256]{1,0:T(8,128)} %get-tuple-element.22), channel_id=1, source_target_pairs={{0,1},{1,0},{2,3},{3,2},{4,5},{5,4},{6,7},{7,6},{8,9},{9,8},{10,11... | collective-permute-start | bytes 98312 | tf_op jit(solution)/shard_map/ppermute | solution.py:781
  5.3 0.0 collective-permute-start.1
  5.3 2.1 %collective-permute-done.from_even.y_even = f32[32,256]{1,0:T(8,128)S(1)} collective-permute-done((f32[32,256]{1,0:T(8,128)}, f32[32,256]{1,0:T(8,128)S(1)}, u32[]{:S(2)}, u32[]{:S(2)}) %collective-permute-start) | collective-permute-done | bytes 32800 | tf_op jit(solution)/shard_map/ppermute | solution.py:781
  7.4 0.0 collective-permute-done.1.from_odd.y_odd
  7.4 0.0 copy-start.5
  7.4 0.9 %copy-done.5 = f32[32,1024]{1,0:T(8,128)S(1)} copy-done((f32[32,1024]{1,0:T(8,128)S(1)}, f32[32,1024]{1,0:T(8,128)}, u32[]{:S(2)}) %copy-start.5) | copy-done | bytes 131096
  8.3 1.5 %shard_map.96 = (f32[32,1024]{1,0:T(8,128)S(1)}, f32[16,2560]{1,0:T(8,128)S(1)}, f32[16,2560]{1,0:T(8,128)S(1)}, f32[8,24,128]{2,1,0:T(8,128)}) custom-call(s32[1,32]{1,0:T(1,128)S(1)} %bitcast.12, f32[32,1024]{1,0:T(8,128)S(1)} %copy-done, f32[32,1024]{1,0:T(8,128)S(1)} %copy-done.1, f32[32,1024]{1,0:T(8,128)S(1)} %copy-done.5, ...), custom_call_target="tpu_custom_call" | custom-call | tf_op jit(solution)/shard_map/pallas_call | solution.py:746
  9.8 4.3 %all-to-all-start = ((f32[8,24,128]{2,1,0:T(8,128)}), f32[8,24,128]{2,1,0:T(8,128)S(1)}, u32[]{:S(2)}, u32[]{:S(2)}) async-start(f32[8,24,128]{2,1,0:T(8,128)} %get-tuple-element.24), calls=%async_computation | async-start | bytes 196608 | tf_op jit(solution)/shard_map/all_to_all | solution.py:828
  14.1 0.5 %collective-permute-start.2 = (f32[16,2560]{1,0:T(8,128)S(1)}, f32[16,2560]{1,0:T(8,128)S(1)}, u32[]{:S(2)}, u32[]{:S(2)}) collective-permute-start(f32[16,2560]{1,0:T(8,128)S(1)} %get-tuple-element.30), channel_id=1, source_target_pairs={{0,4},{4,0},{8,12},{12,8},{16,20},{20,16},{24,28},{28,24},{1,5},{5... | collective-permute-start | bytes 491528 | tf_op jit(solution)/shard_map/ppermute | solution.py:781
  14.6 2.7 %collective-permute-start.3 = (f32[16,2560]{1,0:T(8,128)S(1)}, f32[16,2560]{1,0:T(8,128)S(1)}, u32[]{:S(2)}, u32[]{:S(2)}) collective-permute-start(f32[16,2560]{1,0:T(8,128)S(1)} %get-tuple-element.31), channel_id=1, source_target_pairs={{0,1},{4,8},{8,4},{12,16},{16,12},{20,24},{24,20},{28,29},{1,0},{5... | collective-permute-start | bytes 491528 | tf_op jit(solution)/shard_map/ppermute | solution.py:781
  17.3 0.4 shard_map.97
  17.6 1.6 %all-to-all-done.faces = f32[8,24,128]{2,1,0:T(8,128)S(1)} async-done(((f32[8,24,128]{2,1,0:T(8,128)}), f32[8,24,128]{2,1,0:T(8,128)S(1)}, u32[]{:S(2)}, u32[]{:S(2)}) %all-to-all-start) | async-done | bytes 98336 | tf_op jit(solution)/shard_map/all_to_all | solution.py:828
  19.3 0.7 %copy-done.7 = s32[3]{0:T(128)S(1)} copy-done((s32[3]{0:T(128)S(1)}, s32[3]{0:T(128)}, u32[]{:S(2)}) %copy-start.7) | copy-done | bytes 36
  19.9 1.6 %shard_map.98 = (f32[32,1024]{1,0:T(8,128)S(1)}, f32[8,16,256]{2,1,0:T(8,128)}) custom-call(s32[1,32]{1,0:T(1,128)S(1)} %bitcast.13, s32[1,3]{1,0:T(1,128)S(1)} %bitcast.17, f32[8,24,128]{2,1,0:T(8,128)S(1)} %all-to-all-done.faces, f32[32,1024]{1,0:T(8,128)S(1)} %bitcast.7, f32[32,1024]{1,0:T(8,128)S(1)} %bitcast.9, f32[32,1024]{1,0:T(8,128)S(1)} %bitcast.11, ...), custom_call_target="tpu_custom_call" | custom-call | tf_op jit(solution)/shard_map/pallas_call | solution.py:746
  21.5 3.4 %all-to-all-start.1 = ((f32[8,16,256]{2,1,0:T(8,128)}), f32[8,16,256]{2,1,0:T(8,128)S(1)}, u32[]{:S(2)}, u32[]{:S(2)}) async-start(f32[8,16,256]{2,1,0:T(8,128)} %get-tuple-element.28), calls=%async_computation.1 | async-start | bytes 262144 | tf_op jit(solution)/shard_map/all_to_all | solution.py:836
  24.9 5.4 %all-to-all-done.1.arrived = f32[8,16,256]{2,1,0:T(8,128)S(1)} async-done(((f32[8,16,256]{2,1,0:T(8,128)}), f32[8,16,256]{2,1,0:T(8,128)S(1)}, u32[]{:S(2)}, u32[]{:S(2)}) %all-to-all-start.1) | async-done | bytes 131104 | tf_op jit(solution)/shard_map/all_to_all | solution.py:836
  30.3 3.1 %shard_map.99 = (f32[32,512]{1,0:T(8,128)S(1)}, f32[32,256]{1,0:T(8,128)S(1)}, f32[32,1024]{1,0:T(8,128)S(1)}, f32[32,512]{1,0:T(8,128)S(1)}, f32[32,512]{1,0:T(8,128)S(1)}) custom-call(s32[1,32]{1,0:T(1,128)S(1)} %bitcast.14, s32[1,3]{1,0:T(1,128)S(1)} %bitcast.18, f32[8,16,256]{2,1,0:T(8,128)S(1)} %all-to-all-done.1.arrived, ...), custom_call_target="tpu_custom_call" | custom-call | tf_op jit(solution)/shard_map/pallas_call | solution.py:746
  33.4 2.8 %collective-permute-start.4 = (f32[32,512]{1,0:T(8,128)S(1)}, f32[32,512]{1,0:T(8,128)S(1)}, u32[]{:S(2)}, u32[]{:S(2)}) collective-permute-start(f32[32,512]{1,0:T(8,128)S(1)} %get-tuple-element.35), channel_id=1, source_target_pairs={{0,1},{1,0},{2,3},{3,2},{4,5},{5,4},{6,7},{7,6},{8,9},{9,8},{10,11... | collective-permute-start | bytes 196616 | tf_op jit(solution)/shard_map/ppermute | solution.py:781
  36.2 2.2 %collective-permute-done.4.from_even = f32[32,512]{1,0:T(8,128)S(1)} collective-permute-done((f32[32,512]{1,0:T(8,128)S(1)}, f32[32,512]{1,0:T(8,128)S(1)}, u32[]{:S(2)}, u32[]{:S(2)}) %collective-permute-start.4) | collective-permute-done | bytes 65568 | tf_op jit(solution)/shard_map/ppermute | solution.py:781
  38.5 0.0 collective-permute-done.5.from_odd
  38.5 1.3 %shard_map.100 = (f32[32,1024]{1,0:T(8,128)S(1)}, f32[8,16,256]{2,1,0:T(8,128)S(1)}) custom-call(s32[1,32]{1,0:T(1,128)S(1)} %bitcast.15, s32[1,3]{1,0:T(1,128)S(1)} %bitcast.19, f32[32,512]{1,0:T(8,128)S(1)} %get-tuple-element.32.source_b, f32[32,256]{1,0:T(8,128)S(1)} %get-tuple-element.33.coefficient_b, f32[32,1024]{1,0:T(8,128)S(1)} %get-tuple-element.34.correction, ...), custom_call_target="tpu_custom_call" | custom-call | tf_op jit(solution)/shard_map/pallas_call | solution.py:746
  39.8 7.9 %all_to_all.15.arrived = f32[8,16,256]{2,1,0:T(8,128)S(1)} all-to-all(f32[8,16,256]{2,1,0:T(8,128)S(1)} %get-tuple-element.37), channel_id=1, replica_groups=mesh['gx'=8,'gy'=4] {'gx'}, dimensions={0} | all-to-all | bytes 262144 | tf_op jit(solution)/shard_map/all_to_all | solution.py:873
  47.7 1.0 %shard_map.101 = (f32[32,1024]{1,0:T(8,128)}, f32[32,1024]{1,0:T(8,128)}) custom-call(s32[1,32]{1,0:T(1,128)S(1)} %bitcast.16, f32[8,16,256]{2,1,0:T(8,128)S(1)} %all_to_all.15.arrived, f32[32,1024]{1,0:T(8,128)S(1)} %get-tuple-element.38.smoothed, f32[32,1024]{1,0:T(8,128)S(1)} %copy-done, f32[32,1024]{1,0:T(8,128)S(1)} %get-tuple-element.39.correction), custom_call_target="tpu_custom_call" | custom-call | tf_op jit(solution)/shard_map/pallas_call | solution.py:746
  (16 shorter events, 0.0 us)
Async XLA Ops:
  0.6 6.7 %copy-start = (f32[32,1024]{1,0:T(8,128)S(1)}, f32[32,1024]{1,0:T(8,128)}, u32[]{:S(2)}) copy-start(f32[32,1024]{1,0:T(8,128)} %start.7) | copy-start | bytes 393220
  0.6 6.7 %copy-start.1 = (f32[32,1024]{1,0:T(8,128)S(1)}, f32[32,1024]{1,0:T(8,128)}, u32[]{:S(2)}) copy-start(f32[32,1024]{1,0:T(8,128)} %coefficient.5) | copy-start | bytes 393220
  2.1 5.2 %collective-permute-start = (f32[32,256]{1,0:T(8,128)}, f32[32,256]{1,0:T(8,128)S(1)}, u32[]{:S(2)}, u32[]{:S(2)}) collective-permute-start(f32[32,256]{1,0:T(8,128)} %get-tuple-element.22), channel_id=1, source_target_pairs={{0,1},{1,0},{2,3},{3,2},{4,5},{5,4},{6,7},{7,6},{8,9},{9,8},{10,11... | collective-permute-start | bytes 98312 | tf_op jit(solution)/shard_map/ppermute | solution.py:781
  5.3 2.1 %copy-start.6 = (s32[32]{0:T(128)S(1)}, s32[32]{0:T(128)}, u32[]{:S(2)}) copy-start(s32[32]{0:T(128)} %param.14) | copy-start | bytes 388
  5.3 2.1 %collective-permute-start.1 = (f32[32,256]{1,0:T(8,128)}, f32[32,256]{1,0:T(8,128)S(1)}, u32[]{:S(2)}, u32[]{:S(2)}) collective-permute-start(f32[32,256]{1,0:T(8,128)} %get-tuple-element.23), channel_id=1, source_target_pairs={{0,4},{1,2},{2,1},{3,7},{4,0},{5,6},{6,5},{7,3},{8,12},{9,10},{10,... | collective-permute-start | bytes 98312 | tf_op jit(solution)/shard_map/ppermute | solution.py:781
  7.4 0.9 %copy-start.5 = (f32[32,1024]{1,0:T(8,128)S(1)}, f32[32,1024]{1,0:T(8,128)}, u32[]{:S(2)}) copy-start(f32[32,1024]{1,0:T(8,128)} %source.1) | copy-start | bytes 393220
  8.3 9.0 %copy-start.3 = (f32[1,32,1024]{2,1,0:T(8,128)S(1)}, f32[1,32,1024]{2,1,0:T(8,128)}, u32[]{:S(2)}) copy-start(f32[1,32,1024]{2,1,0:T(8,128)} %param.12) | copy-start | bytes 393220
  8.3 9.0 %copy-start.4 = (f32[1,32,1024]{2,1,0:T(8,128)S(1)}, f32[1,32,1024]{2,1,0:T(8,128)}, u32[]{:S(2)}) copy-start(f32[1,32,1024]{2,1,0:T(8,128)} %param.13) | copy-start | bytes 393220
  9.8 7.5 %copy-start.2 = (f32[1,32,1024]{2,1,0:T(8,128)S(1)}, f32[1,32,1024]{2,1,0:T(8,128)}, u32[]{:S(2)}) copy-start(f32[1,32,1024]{2,1,0:T(8,128)} %param.11) | copy-start | bytes 393220
  9.8 9.5 %all-to-all-start = ((f32[8,24,128]{2,1,0:T(8,128)}), f32[8,24,128]{2,1,0:T(8,128)S(1)}, u32[]{:S(2)}, u32[]{:S(2)}) async-start(f32[8,24,128]{2,1,0:T(8,128)} %get-tuple-element.24), calls=%async_computation | async-start | bytes 196608 | tf_op jit(solution)/shard_map/all_to_all | solution.py:828
  14.1 10.8 %collective-permute-start.2 = (f32[16,2560]{1,0:T(8,128)S(1)}, f32[16,2560]{1,0:T(8,128)S(1)}, u32[]{:S(2)}, u32[]{:S(2)}) collective-permute-start(f32[16,2560]{1,0:T(8,128)S(1)} %get-tuple-element.30), channel_id=1, source_target_pairs={{0,4},{4,0},{8,12},{12,8},{16,20},{20,16},{24,28},{28,24},{1,5},{5... | collective-permute-start | bytes 491528 | tf_op jit(solution)/shard_map/ppermute | solution.py:781
  14.6 10.3 %collective-permute-start.3 = (f32[16,2560]{1,0:T(8,128)S(1)}, f32[16,2560]{1,0:T(8,128)S(1)}, u32[]{:S(2)}, u32[]{:S(2)}) collective-permute-start(f32[16,2560]{1,0:T(8,128)S(1)} %get-tuple-element.31), channel_id=1, source_target_pairs={{0,1},{4,8},{8,4},{12,16},{16,12},{20,24},{24,20},{28,29},{1,0},{5... | collective-permute-start | bytes 491528 | tf_op jit(solution)/shard_map/ppermute | solution.py:781
  19.3 0.7 %copy-start.7 = (s32[3]{0:T(128)S(1)}, s32[3]{0:T(128)}, u32[]{:S(2)}) copy-start(s32[3]{0:T(128)} %param.15) | copy-start | bytes 40
  21.5 8.8 %all-to-all-start.1 = ((f32[8,16,256]{2,1,0:T(8,128)}), f32[8,16,256]{2,1,0:T(8,128)S(1)}, u32[]{:S(2)}, u32[]{:S(2)}) async-start(f32[8,16,256]{2,1,0:T(8,128)} %get-tuple-element.28), calls=%async_computation.1 | async-start | bytes 262144 | tf_op jit(solution)/shard_map/all_to_all | solution.py:836
  33.4 5.0 %collective-permute-start.4 = (f32[32,512]{1,0:T(8,128)S(1)}, f32[32,512]{1,0:T(8,128)S(1)}, u32[]{:S(2)}, u32[]{:S(2)}) collective-permute-start(f32[32,512]{1,0:T(8,128)S(1)} %get-tuple-element.35), channel_id=1, source_target_pairs={{0,1},{1,0},{2,3},{3,2},{4,5},{5,4},{6,7},{7,6},{8,9},{9,8},{10,11... | collective-permute-start | bytes 196616 | tf_op jit(solution)/shard_map/ppermute | solution.py:781
  36.2 2.2 %collective-permute-start.5 = (f32[32,512]{1,0:T(8,128)S(1)}, f32[32,512]{1,0:T(8,128)S(1)}, u32[]{:S(2)}, u32[]{:S(2)}) collective-permute-start(f32[32,512]{1,0:T(8,128)S(1)} %get-tuple-element.36), channel_id=1, source_target_pairs={{0,4},{1,2},{2,1},{3,7},{4,0},{5,6},{6,5},{7,3},{8,12},{9,10},{10,... | collective-permute-start | bytes 196616 | tf_op jit(solution)/shard_map/ppermute | solution.py:781

commit v3 on v2

v3 whole, which is shorter than its diff:
```python
import functools

import jax
import jax.numpy as jnp
from jax import lax
from jax.experimental import pallas as pl
from jax.experimental.pallas import tpu as pltpu
from jax.sharding import PartitionSpec as P


SWEEPS = 4
LANES = 128
ROWS = 8
F32 = jnp.float32
BF16 = jnp.bfloat16
VMEM = pl.BlockSpec(memory_space=pltpu.VMEM)
HBM = pl.BlockSpec(memory_space=pltpu.HBM)
PARAMS = pltpu.CompilerParams(vmem_limit_bytes=20 * 1024 * 1024)


def iotas(shape):
    return (
        lax.broadcasted_iota(jnp.int32, shape, 0),
        lax.broadcasted_iota(jnp.int32, shape, 1),
    )


def ones_where(mask):
    return jnp.where(mask, 1.0, 0.0).astype(BF16)


def select_dot(value, chosen):
    high = value.astype(BF16)
    rest = value - high.astype(F32)
    middle = rest.astype(BF16)
    low = (rest - middle.astype(F32)).astype(BF16)
    rows = value.shape[0]
    if rows % (2 * ROWS) == 0:
        parts = jnp.concatenate([low, middle, high], axis=0)
        whole = jnp.dot(parts, chosen, preferred_element_type=F32)
        return (whole[0:rows] + whole[rows : 2 * rows]) + whole[2 * rows :]
    total = jnp.dot(low, chosen, preferred_element_type=F32)
    total = total + jnp.dot(middle, chosen, preferred_element_type=F32)
    return total + jnp.dot(high, chosen, preferred_element_type=F32)


def ahead(value, lanes):
    return pltpu.roll(value, value.shape[1] - lanes, 1)


def behind(value, lanes):
    return pltpu.roll(value, lanes, 1)


def cell_parity(edge):
    x, lane = iotas((ROWS, LANES))
    return (x + lane // edge + lane % edge) % 2


def along_y(tiles, edge):
    _, lane = iotas(tiles[0].shape)
    up = [0.0] + [pltpu.roll(one, edge, 1) for one in tiles]
    down = [pltpu.roll(one, LANES - edge, 1) for one in tiles] + [0.0]
    count = len(tiles)
    low = [jnp.where(lane < edge, up[t], up[t + 1]) for t in range(count)]
    high = [jnp.where(lane >= LANES - edge, down[t + 1], down[t]) for t in range(count)]
    return low, high


def along_z(tiles):
    return (
        [pltpu.roll(one, 1, 1) for one in tiles],
        [pltpu.roll(one, LANES - 1, 1) for one in tiles],
    )


def six_around(ref, tiles, at, edge):
    own = [ref[t, at : at + ROWS, :] for t in tiles]
    x_low = [ref[t, at - 1 : at + ROWS - 1, :] for t in tiles]
    x_high = [ref[t, at + 1 : at + ROWS + 1, :] for t in tiles]
    return own, (x_low, x_high) + along_y(own, edge) + along_z(own)


def coupled(weights, rows, ref, tiles, at, edge):
    own, around = six_around(ref, tiles, at, edge)
    sums = []
    for spot, tile in enumerate(tiles):
        total = weights[0, tile, rows, :] * around[0][spot]
        for number in range(1, 6):
            total = total + weights[number, tile, rows, :] * around[number][spot]
        sums.append(total)
    return own, sums


def coarsening(edge, fine_lanes, coarse_lanes):
    half = edge // 2
    fine, coarse = iotas((fine_lanes, coarse_lanes))
    same_y = fine // edge // 2 == coarse // half
    return ones_where(same_y & (fine % edge // 2 == coarse % half))


def refining(edge, coarse_lanes, fine_lanes):
    half = edge // 2
    coarse, fine = iotas((coarse_lanes, fine_lanes))
    same_y = fine // edge // 2 == coarse // half
    return ones_where(same_y & (fine % edge // 2 == coarse % half))


def double_rows(ref, value):
    rows = value.shape[0]
    for tile in range(value.shape[1] // LANES):
        part = value[:, tile * LANES : (tile + 1) * LANES]
        ref[tile, pl.ds(0, rows, 2), :] = part
        ref[tile, pl.ds(1, rows, 2), :] = part


def pair_rows(ref, tile, first, rows):
    return ref[tile, pl.ds(first, rows, 2), :] + ref[tile, pl.ds(first + 1, rows, 2), :]


def tiles_of(lane):
    return slice(lane * LANES, (lane + 1) * LANES)


def flat(ref, rows, tiles):
    return jnp.concatenate([ref[tile, rows, :] for tile in tiles], axis=1)


def twice_faces(own, around, edge):
    _, lane = iotas(own[0].shape)
    first = lane % edge == 0
    last = lane % edge == edge - 1
    weights = []
    diagonals = []
    for spot, k in enumerate(own):
        w = [k + around[number][spot] for number in range(6)]
        diagonals.append(
            ((w[0] + w[1]) + (w[2] + w[3]))
            + (jnp.where(first, k, w[4]) + jnp.where(last, k, w[5]))
        )
        w[4] = jnp.where(first, 0.0, w[4])
        w[5] = jnp.where(last, 0.0, w[5])
        weights.append(w)
    return weights, diagonals


def two_sides(place_in_axis, size, even, odd):
    parity = place_in_axis % 2
    below = jnp.where(parity == 0, odd, even)
    above = jnp.where(parity == 0, even, odd)
    return (
        jnp.where(place_in_axis > 0, below, 0.0),
        jnp.where(place_in_axis < size - 1, above, 0.0),
    )


def place(positions, number, groups_y):
    _, lane = iotas(positions.shape)
    position = jnp.sum(jnp.where(lane == number, positions[...], 0))
    holder = position // 8
    return (holder // groups_y, position % 8)


def select_faces(edge, octant_z):
    half = edge // 2
    unit_y = LANES // edge
    at, to = iotas((half * edge + 2 * LANES, LANES))
    y = at // edge - unit_y
    z = at % edge
    near_z = half if octant_z == 0 else half - 1
    goal = (2 + octant_z) * half
    which = to // half
    spot = to % half
    return ones_where(
        ((y == -1) & (which == 0) & (z == octant_z * half + spot))
        | ((y == half) & (which == 1) & (z == octant_z * half + spot))
        | ((z == near_z) & (which == 2 + octant_z) & (y == to - goal))
    )


def select_ghosts(edge, lanes):
    half = edge // 2
    at, to = iotas((4 * half, lanes))
    fine_y = to // edge
    fine_z = to % edge
    return ones_where(
        ((fine_y == 0) & (at == fine_z // 2))
        | ((fine_y == edge - 1) & (at == half + fine_z // 2))
        | ((fine_z == edge - 1) & (at == 2 * half + fine_y // 2))
        | ((fine_z == 0) & (at == 3 * half + fine_y // 2))
    )


def select_planes(edge):
    at, to = iotas((LANES, 2 * LANES))
    return ones_where((at // edge == to // edge // 2) & (at % edge == to % edge // 2))


def select_both_halves(edge):
    half = edge // 2
    at, to = iotas((LANES, 2 * LANES))
    return ones_where((at // half == to // edge) & (at % half == to % half))


def select_low_half(edge):
    half = edge // 2
    at, to = iotas((2 * LANES, LANES))
    return ones_where((at // edge == to // half) & (at % edge == to % half))


def border_kernel(
    start, coefficient, position, colours,
    even_packet, odd_packet, position_out, colours_out, faces_0, faces_1,
    semaphores,
):
    edge, lanes = start.shape
    last = lanes - LANES
    parity = lax.axis_index("gy") % 2
    copies = []
    for packet, at in (
        (even_packet, (1 - parity) * last),
        (odd_packet, parity * last),
    ):
        for goes, array in enumerate((start, coefficient)):
            copies.append(
                pltpu.make_async_copy(
                    array.at[:, pl.ds(pl.multiple_of(at, LANES), LANES)],
                    packet.at[:, tiles_of(goes)],
                    semaphores.at[len(copies)],
                )
            )
    for array, goes in ((position, position_out), (colours, colours_out)):
        copies.append(pltpu.make_async_copy(array, goes, semaphores.at[len(copies)]))
    for copy in copies:
        copy.start()
    faces_0[...] = select_faces(edge, 0)
    faces_1[...] = select_faces(edge, 1)
    for copy in copies:
        copy.wait()


def faces_kernel(
    groups_x, groups_y, position, colours, start, from_even, from_odd, faces_0, faces_1,
    slots,
    table, low, high,
):
    edge = start.shape[0]
    half = edge // 2
    unit = LANES
    me = lax.axis_index("gx")
    mine_y = lax.axis_index("gy")
    table[...] = jnp.zeros_like(table)
    low[...], high[...] = two_sides(
        mine_y, groups_y, from_even[:, 0:unit], from_odd[:, 0:unit]
    )

    span = half * edge
    tiles = span // unit
    chosen = (faces_0[...], faces_1[...])
    for octant_x in range(2):
        for octant_y in range(2):
            octant_z = (octant_x + octant_y) % 2
            rows = slice(octant_x * half, octant_x * half + half)
            begin = octant_y * span
            left = (
                low[rows, 0:unit] if octant_y == 0 else start[rows, begin - unit : begin]
            )
            right = (
                start[rows, begin + span : begin + span + unit]
                if octant_y == 0
                else high[rows, 0:unit]
            )
            block = jnp.concatenate([left, start[rows, begin : begin + span], right], axis=1)
            entry = 2 * octant_x + octant_y
            table[entry, 0:half, :] = select_dot(block, chosen[octant_z])
            inner = (half, half + ROWS) if octant_x == 0 else (half - ROWS, half)
            outer = (edge - ROWS, edge) if octant_x == 0 else (0, ROWS)
            pick = 0 if octant_x == 0 else ROWS - 1
            outer_pick = ROWS - 1 if octant_x == 0 else 0
            other = 4 + 2 * octant_x + octant_y
            for (first_row, last_row), which, goes, side in (
                (inner, pick, entry, 1 - octant_x),
                (outer, outer_pick, other, octant_x),
            ):
                plane = start[first_row:last_row, begin : begin + span]
                if octant_z == 1:
                    plane = ahead(plane, half)
                for tile in range(tiles):
                    line = half + side * tiles + tile
                    table[goes, line : line + 1, :] = plane[
                        which : which + 1, tile * unit : (tile + 1) * unit
                    ]

    for holder in range(groups_x):
        owner, octant = place(position, holder * groups_y + mine_y, groups_y)
        octant_x = octant // 4
        octant_y = octant // 2 % 2
        entry = jnp.where(
            owner == me,
            2 * octant_x + octant_y,
            jnp.where(owner == me + 1, 4 + octant_y, 6 + octant_y),
        )
        slots[holder] = table[entry]


def residual_kernel(
    groups_y, start, coefficient, source, from_even, from_odd,
    residual, even_packet, odd_packet,
    values, kappas, low, high,
):
    edge = start.shape[0]
    half = edge // 2
    lanes = start.shape[1]
    unit = LANES
    me = lax.axis_index("gx")
    mine_y = lax.axis_index("gy")
    low[...], high[...] = two_sides(mine_y, groups_y, from_even[...], from_odd[...])
    every = range(lanes // unit)
    for ref, array, border in ((values, start, 0), (kappas, coefficient, 1)):
        ref[0, ROWS : ROWS + edge, :] = low[:, tiles_of(border)]
        ref[lanes // unit + 1, ROWS : ROWS + edge, :] = high[:, tiles_of(border)]
        for tile in every:
            ref[tile + 1, ROWS - 1 : ROWS, :] = array[0:1, tiles_of(tile)]
            ref[tile + 1, ROWS : ROWS + edge, :] = array[:, tiles_of(tile)]
            ref[tile + 1, ROWS + edge : ROWS + edge + 1, :] = array[edge - 1 :, tiles_of(tile)]
    _, lane = iotas((ROWS, unit))
    first = lane % edge == 0
    last = lane % edge == edge - 1
    for row in range(0, edge, ROWS):
        at = row + ROWS
        for tile in every:
            near = (tile, tile + 1, tile + 2)
            v = values[tile + 1, at : at + ROWS, :]
            k = kappas[tile + 1, at : at + ROWS, :]
            total = 2.0 * source[row : row + ROWS, tiles_of(tile)]
            for move in (-1, 1):
                rows = slice(at + move, at + move + ROWS)
                total = total + (k + kappas[tile + 1, rows, :]) * (values[tile + 1, rows, :] - v)
            vs = along_y([values[t, at : at + ROWS, :] for t in near], edge)
            ks = along_y([kappas[t, at : at + ROWS, :] for t in near], edge)
            for side in range(2):
                total = total + (k + ks[side][1]) * (vs[side][1] - v)
            vz = along_z([v])
            kz = along_z([k])
            for side, border in ((0, first), (1, last)):
                k_other = jnp.where(border, 0.0, kz[side][0])
                v_other = jnp.where(border, 0.0, vz[side][0])
                total = total + (k + k_other) * (v_other - v)
            residual[tile, row : row + ROWS, :] = total

    body = 2 * lanes + 2 * unit

    def pack(buffer, rows, k_row, v_row):
        for tile in every:
            buffer[:, tiles_of(tile)] = residual[tile, rows, :]
        buffer[:, lanes : lanes + unit] = low[rows, unit:]
        buffer[:, lanes + unit : 2 * lanes + unit] = coefficient[rows, :]
        buffer[:, 2 * lanes + unit : body] = high[rows, unit:]
        buffer[:, body:] = jnp.zeros((half, buffer.shape[1] - body), F32)
        pieces = [(start, v_row, at) for at in range(0, lanes, unit)]
        pieces.append((low, k_row, unit))
        pieces = pieces + [(coefficient, k_row, at) for at in range(0, lanes, unit)]
        pieces.append((high, k_row, unit))
        for number, (array, row, at) in enumerate(pieces):
            spot = body + number // half * unit
            line = number % half
            buffer[line : line + 1, spot : spot + unit] = array[row : row + 1, at : at + unit]

    for parity in range(2):
        upper, lower = (even_packet, odd_packet) if parity == 0 else (odd_packet, even_packet)

        @pl.when(me % 2 == parity)
        def _(upper=upper, lower=lower):
            pack(upper, slice(half, edge), half - 1, edge - 1)
            pack(lower, slice(0, half), half, 0)


def box_terms_kernel(
    source, coefficient, start,
    weights, inverse, base, ghosts, planes, both, low_half, coarsen, refine,
):
    edge = source.shape[0]
    lanes = source.shape[1]
    _, lane = iotas((ROWS, lanes))
    first_y = lane < edge
    last_y = lane >= lanes - edge
    first_z = lane % edge == 0
    last_z = lane % edge == edge - 1

    def shifted_rows(array, row):
        block = array[row : row + ROWS, :]
        if row == 0:
            low = jnp.concatenate([block[0:1, :], array[0 : ROWS - 1, :]], axis=0)
        else:
            low = array[row - 1 : row + ROWS - 1, :]
        if row + ROWS == edge:
            high = jnp.concatenate([array[row + 1 : edge, :], block[ROWS - 1 :, :]], axis=0)
        else:
            high = array[row + 1 : row + ROWS + 1, :]
        return (
            block, low, high,
            behind(block, edge), ahead(block, edge), behind(block, 1), ahead(block, 1),
        )

    for row in range(0, edge, ROWS):
        rows = slice(row, row + ROWS)
        x, _ = iotas((ROWS, lanes))
        outside = (x + row == 0, x + row == edge - 1, first_y, last_y, first_z, last_z)
        k, *around = shifted_rows(coefficient, row)
        v, *beside = shifted_rows(start, row)
        total = None
        sums = None
        for number in range(6):
            face = 0.5 * (k + around[number])
            whole = jnp.where(outside[number], k, face)
            inner = jnp.where(outside[number], 0.0, face)
            for tile in range(lanes // LANES):
                weights[number, tile, rows, :] = inner[:, tiles_of(tile)]
            sums = whole if sums is None else sums + whole
            term = inner * beside[number]
            total = term if total is None else total + term
        sums = 1.0 / (4.0 * sums)
        total = source[rows, :] + 4.0 * total
        for tile in range(lanes // LANES):
            inverse[tile, rows, :] = sums[:, tiles_of(tile)]
            base[tile, rows, :] = total[:, tiles_of(tile)]
    ghosts[...] = select_ghosts(edge, lanes)
    planes[...] = select_planes(edge)
    both[...] = select_both_halves(edge)
    low_half[...] = select_low_half(edge)
    coarsen[...] = coarsening(edge, 4 * LANES, LANES)
    refine[...] = refining(edge, LANES, 4 * LANES)


def fine_kernel(
    groups_x, groups_y, position, colours, faces, source, coefficient, start,
    weights, inverse, base_terms, ghosts, planes_grown, coarsen,
    smoothed, slots,
    ghost, values, kept,
):
    edge = source.shape[0]
    half = edge // 2
    lanes = source.shape[1]
    me = lax.axis_index("gx") * groups_y + lax.axis_index("gy")
    owner, octant = place(position, me, groups_y)
    octant_x = octant // 4
    leading = colours[0:1, 0:1]
    span = half * edge
    tiles = span // LANES

    base = faces[owner]
    sides = select_dot(base[0:half, 0 : 4 * half], ghosts[...])
    double_rows(ghost, sides)
    before = faces[jnp.maximum(owner - 1, 0)][half:, :]
    after = faces[jnp.minimum(owner + 1, groups_x - 1)][half:, :]
    base = base[half:, :]
    before = jnp.where(owner > 0, before, 0.0)
    after = jnp.where(owner < groups_x - 1, after, 0.0)
    line, _ = iotas(base.shape)
    planes = jnp.where(
        line < tiles,
        jnp.where(octant_x == 0, before, base),
        jnp.where(octant_x == 1, after, base),
    )
    planes = jnp.concatenate([planes, planes], axis=0)
    grown = select_dot(planes, planes_grown[...])
    for tile in range(tiles):
        for part in range(2):
            at = 2 * tile + part
            extra = grown[:, part * LANES : (part + 1) * LANES]
            ghost[at, 0:1, :] = ghost[at, 0:1, :] + extra[tile : tile + 1, :]
            ghost[at, edge - 1 : edge, :] = (
                ghost[at, edge - 1 : edge, :] + extra[tiles + tile : tiles + tile + 1, :]
            )
    every = range(lanes // LANES)


    leads = cell_parity(edge) == leading
    row_zero = jnp.zeros((1, LANES), F32)
    for tile in every:
        values[tile, ROWS - 1 : ROWS, :] = row_zero
        values[tile, edge + ROWS : edge + ROWS + 1, :] = row_zero
    for row in range(0, edge, ROWS):
        rows = slice(row, row + ROWS)
        for tile in every:
            lane = tiles_of(tile)
            extra = 4.0 * coefficient[rows, lane] * ghost[tile, rows, :]
            values[tile, row + ROWS : row + 2 * ROWS, :] = jnp.where(
                leads, (base_terms[tile, rows, :] + extra) * inverse[tile, rows, :],
                start[rows, lane],
            )
            kept[tile, rows, :] = source[rows, lane] + extra
    for row in range(0, edge, ROWS):
        rows = slice(row, row + ROWS)
        own, sums = coupled(weights, rows, values, every, row + ROWS, edge)
        for tile in every:
            smoothed[rows, tiles_of(tile)] = jnp.where(
                leads, own[tile],
                (kept[tile, rows, :] + 4.0 * sums[tile]) * inverse[tile, rows, :],
            )
    for tile in every:
        values[tile, ROWS : edge + ROWS, :] = smoothed[:, tiles_of(tile)]
    for row in range(0, edge, ROWS):
        rows = slice(row, row + ROWS)
        own, sums = coupled(weights, rows, values, every, row + ROWS, edge)
        for tile in every:
            ghost[tile, rows, :] = jnp.where(
                leads,
                (source[rows, tiles_of(tile)] - base_terms[tile, rows, :]) + 4.0 * sums[tile],
                0.0,
            )
    chosen = coarsen[...]
    for part in range(lanes // (4 * LANES)):
        block = jnp.concatenate(
            [pair_rows(ghost, 4 * part + tile, 0, half) for tile in range(4)], axis=1
        )
        mean = 0.25 * select_dot(block, chosen)
        for holder in range(groups_x):
            slots[holder, :, part * LANES : (part + 1) * LANES] = mean


def coarse_kernel(
    groups_x, groups_y, position, colours, arrived, residual, start, coefficient,
    y_even, y_odd, from_even, from_odd, both, coarsen,
    source_b, coefficient_b, correction, even_packet, odd_packet,
    grown, kext, comp, extra_v, weights, inverse, first_values, second_values, left,
):
    edge = start.shape[0]
    half = edge // 2
    lanes = start.shape[1]
    span = half * edge
    unit = LANES
    me = lax.axis_index("gx")
    mine_y = lax.axis_index("gy")
    count = lanes // unit
    wide = lanes + 2 * unit
    body = lanes + wide
    rows_all = 2 * edge
    top = half + ROWS
    every = range(count)
    tiles = range(count + 2)

    k_low, k_high = two_sides(mine_y, groups_y, y_even[:, unit:], y_odd[:, unit:])
    kext[0, top : top + edge, :] = k_low
    kext[count + 1, top : top + edge, :] = k_high
    for tile in every:
        kext[tile + 1, top : top + edge, :] = coefficient[:, tiles_of(tile)]
        comp[tile, half : half + edge, :] = residual[tile]

    def unpack(block, there, k_rows, c_rows, k_row, number):
        for tile in every:
            comp[tile, c_rows, :] = jnp.where(there, block[:, tiles_of(tile)], 0.0)
        for tile in tiles:
            kext[tile, k_rows, :] = jnp.where(there, block[:, tiles_of(count + tile)], 0.0)
        for piece in range(body // unit):
            spot = body + piece // half * unit
            line = piece % half
            value = jnp.where(there, block[line : line + 1, spot : spot + unit], 0.0)
            if piece < count:
                extra_v[number : number + 1, tiles_of(piece)] = value
            else:
                kext[piece - count, k_row : k_row + 1, :] = value

    for parity in range(2):
        above, below = (from_even, from_odd) if parity == 0 else (from_odd, from_even)

        @pl.when(me % 2 == parity)
        def _(above=above, below=below):
            unpack(below, me > 0, slice(ROWS, top), slice(0, half), ROWS - 1, 0)
            last = top + edge
            unpack(
                above, me < groups_x - 1, slice(last, last + half),
                slice(half + edge, rows_all), last + half, 1,
            )

    for number, mine, theirs in ((0, half, half - 1), (1, half + edge - 1, half + edge)):
        for tile in every:
            v = start[mine - half : mine - half + 1, tiles_of(tile)]
            k = kext[tile + 1, mine + ROWS : mine + ROWS + 1, :]
            k_other = kext[tile + 1, theirs + ROWS : theirs + ROWS + 1, :]
            flux = (k + k_other) * (v - extra_v[number : number + 1, tiles_of(tile)])
            comp[tile, mine : mine + 1, :] = comp[tile, mine : mine + 1, :] - flux
            comp[tile, theirs : theirs + 1, :] = comp[tile, theirs : theirs + 1, :] + flux

    chosen = both[...]
    for part in range(arrived.shape[2] // unit):
        flat_rows = arrived[:, :, tiles_of(part)].reshape(groups_x * half, unit)
        wider = select_dot(flat_rows, chosen)
        for piece in range(2):
            grown[2 * part + piece] = wider[:, tiles_of(piece)]
    _, lane = iotas((half, unit))
    half_of = lane % edge // half
    for holder in range(groups_x):
        owner, octant = place(position, holder * groups_y + mine_y, groups_y)
        block = 2 * (owner - me) + octant // 4 + 1

        @pl.when((block >= 0) & (block < 4))
        def _(holder=holder, octant=octant, block=block):
            rows = pl.ds(pl.multiple_of(block * half, half), half)
            here = half_of == octant % 2
            for tile in range(span // unit):
                goes = octant // 2 % 2 * (span // unit) + tile
                comp[goes, rows, :] = jnp.where(
                    here, grown[tile, holder * half : (holder + 1) * half, :], comp[goes, rows, :]
                )

    zeros = jnp.zeros((ROWS, unit), F32)
    for ref in (first_values, second_values):
        for tile in tiles:
            ref[tile, 0:ROWS, :] = zeros
            ref[tile, ROWS + rows_all :, :] = zeros
    leads = cell_parity(edge) == colours[0:1, 1:2]
    y_there = {0: mine_y > 0, count + 1: mine_y < groups_y - 1}
    for row in range(0, rows_all, ROWS):
        at = row + ROWS
        rows = slice(row, row + ROWS)
        w, diagonals = twice_faces(*six_around(kext, tiles, at, edge), edge)
        x_there = None
        if row < half:
            x_there = me > 0
        elif row >= half + edge:
            x_there = me < groups_x - 1
        for tile in tiles:
            for number in range(6):
                weights[number, tile, rows, :] = w[tile][number]
            inv = 1.0 / diagonals[tile]
            for there in (x_there, y_there.get(tile)):
                if there is not None:
                    inv = jnp.where(there, inv, 0.0)
            inverse[tile, rows, :] = inv
            if tile in y_there:
                first_values[tile, at : at + ROWS, :] = zeros
            else:
                first_values[tile, at : at + ROWS, :] = jnp.where(
                    leads, comp[tile - 1, rows, :] * inv, 0.0
                )

    for row in range(0, rows_all, ROWS):
        rows = slice(row, row + ROWS)
        at = row + ROWS
        own, sums = coupled(weights, rows, first_values, tiles, at, edge)
        for tile in tiles:
            total = sums[tile]
            if tile not in y_there:
                total = total + comp[tile - 1, rows, :]
            total = jnp.where(leads, 0.0, total * inverse[tile, rows, :])
            second_values[tile, at : at + ROWS, :] = total
            if half <= row < half + edge and tile not in y_there:
                correction[row - half : row - half + ROWS, tiles_of(tile - 1)] = own[tile] + total
    for row in range(0, rows_all, ROWS):
        rows = slice(row, row + ROWS)
        own, sums = coupled(weights, rows, second_values, tiles, row + ROWS, edge)
        for tile in tiles:
            left[tile, rows, :] = jnp.where(leads, sums[tile], 0.0)

    chosen = coarsen[...]

    def pairs(ref, these, first):
        return jnp.concatenate([pair_rows(ref, tile, first, edge) for tile in these], axis=1)

    blocks = count // 4
    source_b[:, 0:unit] = 0.0625 * select_dot(pairs(left, [0], 0), chosen[3 * unit :, :])
    source_b[:, (blocks + 1) * unit :] = 0.0625 * select_dot(
        pairs(left, [count + 1], 0), chosen[0:unit, :]
    )
    for part in range(blocks):
        these = range(4 * part + 1, 4 * part + 5)
        source_b[:, tiles_of(part + 1)] = 0.0625 * select_dot(pairs(left, these, 0), chosen)
        coefficient_b[:, tiles_of(part)] = 0.125 * select_dot(pairs(kext, these, ROWS), chosen)
    middle = (blocks + 2) // 2 * unit
    rows = slice(ROWS + half, ROWS + half + edge)
    for parity in range(2):
        up, down = (even_packet, odd_packet) if parity == 0 else (odd_packet, even_packet)

        @pl.when(mine_y % 2 == parity)
        def _(up=up, down=down):
            up[:, 0:middle] = source_b[:, middle:]
            up[:, middle : middle + unit] = coefficient_b[:, (blocks - 1) * unit :]
            up[:, middle + unit :] = second_values[count + 1, rows, :]
            down[:, 0:middle] = source_b[:, 0:middle]
            down[:, middle : middle + unit] = coefficient_b[:, 0:unit]
            down[:, middle + unit :] = second_values[0, rows, :]


def bottom_kernel(
    groups_x, groups_y, position, colours, source_b, coefficient_b, correction,
    from_even, from_odd, low_half, refine,
    corrected, slots,
    spread, table, low, high,
):
    edge = correction.shape[0]
    half = edge // 2
    lanes = correction.shape[1]
    span = half * edge
    unit = LANES
    me = lax.axis_index("gx")
    mine_y = lax.axis_index("gy")
    low[...], high[...] = two_sides(mine_y, groups_y, from_even[...], from_odd[...])
    middle = source_b.shape[1] // 2
    count = 2 * middle // unit
    f_bottom = []
    k_bottom = []
    for tile in range(count):
        side, at = (low, tile) if tile < count // 2 else (high, tile - count // 2)
        f_bottom.append(source_b[:, tiles_of(tile)] + side[:, tiles_of(at)])
        if tile == 0:
            k_bottom.append(low[:, middle : middle + unit])
        elif tile == count - 1:
            k_bottom.append(high[:, middle : middle + unit])
        else:
            k_bottom.append(coefficient_b[:, tiles_of(tile - 1)])
    quarter = half // 2

    def around(tiles):
        return (
            [pltpu.roll(one, 1, 0) for one in tiles],
            [pltpu.roll(one, edge - 1, 0) for one in tiles],
        ) + along_y(tiles, half) + along_z(tiles)

    w, diagonals = twice_faces(k_bottom, around(k_bottom), half)
    x, lane = iotas((edge, unit))
    x = x + (me * half - quarter)
    x_there = (x >= 0) & (x < groups_x * half)
    first = colours[0:1, 2:3]
    parity = (x + lane // half + lane % half) % 2
    scaled = []
    shares = []
    for tile in range(count):
        inv = 1.0 / diagonals[tile]
        there = x_there
        if tile == 0:
            there = there & (mine_y > 0)
        if tile == count - 1:
            there = there & (mine_y < groups_y - 1)
        inv = jnp.where(there, inv, 0.0)
        shares.append([jnp.where(parity == c, inv, 0.0) for c in (first, 1 - first)])
        scaled.append([8.0 * f_bottom[tile] * one for one in shares[tile]])
    values = [[one[0] for one in scaled], None]
    for step in range(1, 2 * SWEEPS):
        colour = step % 2
        beside = around(values[1 - colour])
        fresh = []
        for tile in range(count):
            total = w[tile][0] * beside[0][tile]
            for number in range(1, 6):
                total = total + w[tile][number] * beside[number][tile]
            fresh.append(scaled[tile][colour] + total * shares[tile][colour])
        values[colour] = fresh
    bottom = [one + other for one, other in zip(*values)]

    chosen = refine[...]
    for part in range(lanes // (4 * unit)):
        block = bottom[part + 1][quarter : quarter + half, :]
        double_rows(spread.at[pl.ds(4 * part, 4)], select_dot(block, chosen))
    every = range(lanes // unit)
    for row in range(0, edge, ROWS):
        rows = slice(row, row + ROWS)
        total = correction[rows, :] + flat(spread, rows, every)
        ring = [total[:, tiles_of(tile)] for tile in every]
        ring[0] = ring[0] + low[rows, middle + unit :]
        ring[-1] = ring[-1] + high[rows, middle + unit :]
        total = jnp.concatenate(ring, axis=1)
        corrected[rows, :] = total

    chosen = low_half[...]
    for octant_x in range(2):
        for octant_y in range(2):
            block = corrected[
                octant_x * half : (octant_x + 1) * half,
                octant_y * span : (octant_y + 1) * span,
            ]
            if (octant_x + octant_y) % 2 == 1:
                block = ahead(block, half)
            for part in range(span // (2 * unit)):
                table[2 * octant_x + octant_y, :, part * unit : (part + 1) * unit] = select_dot(
                    block[:, part * 2 * unit : (part + 1) * 2 * unit], chosen
                )
    for holder in range(groups_x):
        _, octant = place(position, holder * groups_y + mine_y, groups_y)
        slots[holder] = table[octant // 4 * 2 + octant // 2 % 2]


def finish_kernel(
    groups_y, position, arrived, smoothed, start, correction, refine,
    coarse_out, out, grown,
):
    edge = smoothed.shape[0]
    me = lax.axis_index("gx") * groups_y + lax.axis_index("gy")
    owner, _ = place(position, me, groups_y)
    coarse_out[...] = start[...] + correction[...]
    value = arrived[owner]
    chosen = refine[...]
    for part in range(value.shape[1] // LANES):
        fine = select_dot(value[:, tiles_of(part)], chosen)
        double_rows(grown.at[pl.ds(4 * part, 4)], fine)
    out[...] = smoothed[...] + flat(grown, slice(0, edge), range(smoothed.shape[1] // LANES))


def call(kernel, outs, scratch, specs, *operands):
    return pl.pallas_call(
        kernel,
        out_shape=[jax.ShapeDtypeStruct(shape, F32) for shape in outs],
        in_specs=specs,
        out_specs=[VMEM] * len(outs),
        scratch_shapes=[pltpu.VMEM(shape, F32) for shape in scratch],
        compiler_params=PARAMS,
    )(*operands)


def tiled(rows, lanes):
    return (lanes // LANES, rows, LANES)


def matching(axis, first):
    sizes = (lax.axis_size("gx"), lax.axis_size("gy"))
    along_x = axis == "gx"
    size, others = sizes if along_x else sizes[::-1]
    pairs = []
    for other in range(others):
        for i in range(size):
            j = i + 1 if (i - first) % 2 == 0 else i - 1
            goes, beside = j, other
            if not 0 <= j < size:
                goes, beside = i, other ^ 1
            if beside < others:
                here, there = (i, other), (goes, beside)
                if not along_x:
                    here, there = here[::-1], there[::-1]
                pairs.append((here[0] * sizes[1] + here[1], there[0] * sizes[1] + there[1]))
    return pairs


def swapped(even_packet, odd_packet, axis):
    return tuple(
        lax.ppermute(packet, ("gx", "gy"), matching(axis, first))
        for first, packet in ((0, even_packet), (1, odd_packet))
    )


def on_device(
    coarse_source,
    coarse_coefficient,
    coarse_start,
    fine_source,
    fine_coefficient,
    fine_start,
    fine_position,
    first_colour,
):
    groups_x = lax.axis_size("gx")
    groups_y = lax.axis_size("gy")
    edge, lanes = coarse_source.shape
    half = edge // 2
    span = half * edge
    compact = half * half
    wide = lanes + 2 * LANES
    positions = fine_position.reshape(1, -1)
    colours = first_colour.reshape(1, -1)
    even_packet, odd_packet, positions, colours, faces_0, faces_1 = pl.pallas_call(
        border_kernel,
        out_shape=[jax.ShapeDtypeStruct((edge, 2 * LANES), F32)] * 2
        + [jax.ShapeDtypeStruct(array.shape, array.dtype) for array in (positions, colours)]
        + [jax.ShapeDtypeStruct((span + 2 * LANES, LANES), BF16)] * 2,
        in_specs=[HBM] * 4,
        out_specs=[VMEM] * 6,
        scratch_shapes=[pltpu.SemaphoreType.DMA((6,))],
        compiler_params=PARAMS,
    )(coarse_start, coarse_coefficient, positions, colours)
    y_even, y_odd = swapped(even_packet, odd_packet, "gy")
    face_rows = half + 2 * (span // LANES)
    (slots,) = call(
        functools.partial(faces_kernel, groups_x, groups_y),
        [(groups_x, face_rows, LANES)],
        [(8, face_rows, LANES), (edge, LANES), (edge, LANES)],
        [VMEM] * 7,
        positions, colours, coarse_start, y_even, y_odd, faces_0, faces_1,
    )
    faces = lax.all_to_all(slots, "gx", 0, 0, tiled=True)
    _, y_even, y_odd = lax.optimization_barrier((slots, y_even, y_odd))
    extra = -(-(lanes + wide) // LANES // half) * LANES
    packed = lanes + wide + extra
    residual, even_packet, odd_packet = call(
        functools.partial(residual_kernel, groups_y),
        [tiled(edge, lanes), (half, packed), (half, packed)],
        [tiled(edge + 2 * ROWS, wide)] * 2 + [(edge, 2 * LANES)] * 2,
        [VMEM] * 5,
        coarse_start, coarse_coefficient, coarse_source, y_even, y_odd,
    )
    from_even, from_odd = swapped(even_packet, odd_packet, "gx")
    box = (fine_source[0], fine_coefficient[0], fine_start[0])
    weights, inverse, base, ghosts, planes, both, low_half, coarsen, refine = pl.pallas_call(
        box_terms_kernel,
        out_shape=[
            jax.ShapeDtypeStruct(shape, F32)
            for shape in [(6,) + tiled(edge, lanes), tiled(edge, lanes), tiled(edge, lanes)]
        ]
        + [
            jax.ShapeDtypeStruct(shape, BF16)
            for shape in [
                (4 * half, lanes),
                (LANES, 2 * LANES),
                (LANES, 2 * LANES),
                (2 * LANES, LANES),
                (4 * LANES, LANES),
                (LANES, 4 * LANES),
            ]
        ],
        in_specs=[VMEM] * 3,
        out_specs=[VMEM] * 9,
        compiler_params=PARAMS,
    )(*box)
    smoothed, restricted = call(
        functools.partial(fine_kernel, groups_x, groups_y),
        [(edge, lanes), (groups_x, half, compact)],
        [tiled(edge, lanes), tiled(edge + 2 * ROWS, lanes), tiled(edge, lanes)],
        [VMEM] * 12,
        positions, colours, faces, *box, weights, inverse, base, ghosts, planes, coarsen,
    )
    arrived = lax.all_to_all(restricted, "gx", 0, 0, tiled=True)
    rows = 2 * edge
    lanes_b = (wide // LANES - 2) // 4 * LANES
    source_b, coefficient_b, correction, even_packet, odd_packet = call(
        functools.partial(coarse_kernel, groups_x, groups_y),
        [
            (edge, lanes_b + 2 * LANES),
            (edge, lanes_b),
            (edge, lanes),
            (edge, lanes_b // 2 + 3 * LANES),
            (edge, lanes_b // 2 + 3 * LANES),
        ],
        [
            (span // LANES, groups_x * half, LANES),
            tiled(rows + 2 * ROWS, wide),
            tiled(rows, lanes),
            (ROWS, lanes),
            (6,) + tiled(rows, wide),
            tiled(rows, wide),
            tiled(rows + 2 * ROWS, wide),
            tiled(rows + 2 * ROWS, wide),
            tiled(rows, wide),
        ],
        [VMEM] * 12,
        positions, colours, arrived, residual, coarse_start, coarse_coefficient,
        y_even, y_odd, from_even, from_odd, both, coarsen,
    )
    y_even, y_odd = swapped(even_packet, odd_packet, "gy")
    corrected, slots = call(
        functools.partial(bottom_kernel, groups_x, groups_y),
        [(edge, lanes), (groups_x, half, compact)],
        [tiled(edge, lanes), (4, half, compact)]
        + [(edge, lanes_b // 2 + 3 * LANES)] * 2,
        [VMEM] * 9,
        positions, colours, source_b, coefficient_b, correction, y_even, y_odd, low_half, refine,
    )
    returned = lax.all_to_all(slots, "gx", 0, 0, tiled=True)
    coarse_solution, fine_solution = call(
        functools.partial(finish_kernel, groups_y),
        [(edge, lanes), (edge, lanes)],
        [tiled(edge, lanes)],
        [VMEM] * 6,
        positions, returned, smoothed, coarse_start, corrected, refine,
    )
    return (coarse_solution, fine_solution[None])


def solution(mesh):
    placed = (
        P("gx", "gy"),
        P("gx", "gy"),
        P("gx", "gy"),
        P(("gx", "gy"), None, None),
        P(("gx", "gy"), None, None),
        P(("gx", "gy"), None, None),
        P(),
        P(),
    )

    return jax.shard_map(
        on_device,
        mesh=mesh,
        in_specs=placed,
        out_specs=(P("gx", "gy"), P(("gx", "gy"), None, None)),
        check_vma=False,
    )
```

time: 49.1 us -> 47.3 us (0.963)
  Pallas kernels: 10.3 us -> 8.72 us
  waiting for transfers between devices: 11.4 us -> 10.2 us
  local copies, waits for them, and re-layouts: 1.58 us -> 2.49 us
    pallas_call x1, Pallas kernels: 1.49 us -> 0.16 us  [on_device(): pl.pallas_call(border_kernel, out_shape=[jax.ShapeDtypeStruct((edge, 2 *...]
    all_to_all x1, waiting for transfers between devices: 1.62 us -> 0.62 us  [on_device(): faces = lax.all_to_all(slots, 'gx', 0, 0, tiled=True)]
    pallas_call x6, Pallas kernels: 8.79 us -> 7.85 us  [call(): pl.pallas_call(kernel, out_shape=[jax.ShapeDtypeStruct(shape, F32) for sh...]
    unnamed x16 -> x20, local copies, waits for them, and re-layouts: 1.58 us -> 2.49 us
    pallas_call x0 -> x1, Pallas kernels: none -> 0.71 us  [on_device(): pl.pallas_call(box_terms_kernel, out_shape=[jax.ShapeDtypeStruct(shape, F...]
  transfers between devices with their start and end apart: 8 -> 8, of which waited for: 4 -> 4; matrix products, arithmetic and copies ran while one was open for 0% -> 0% of each run, Pallas kernels for 4% -> 6%
where the time goes in v3:
time: 47.3 us; the launch traced here: 46.9 us
  starting transfers between devices  16.9 us (36%)
  waiting for transfers between devices  10.2 us (22%)
  Pallas kernels  8.72 us (18%)
  blocking collectives  7.89 us (17%)
  local copies, waits for them, and re-layouts  2.49 us (5%)
  between operations  0.77 us (2%)
    ppermute x6, starting transfers between devices, swapped(): lax.ppermute(packet, ('gx', 'gy'), matching(axis, first))  9.19 us
    all_to_all x1, blocking collectives, on_device(): returned = lax.all_to_all(slots, 'gx', 0, 0, tiled=True)  7.89 us
    pallas_call x6, Pallas kernels, call(): pl.pallas_call(kernel, out_shape=[jax.ShapeDtypeStruct(shape, F32) for sh...  7.85 us
    all_to_all x1, waiting for transfers between devices, on_device(): arrived = lax.all_to_all(restricted, 'gx', 0, 0, tiled=True)  5.41 us
    all_to_all x1, starting transfers between devices, on_device(): faces = lax.all_to_all(slots, 'gx', 0, 0, tiled=True)  4.3 us
    ppermute x6, waiting for transfers between devices, swapped(): lax.ppermute(packet, ('gx', 'gy'), matching(axis, first))  4.14 us
    all_to_all x1, starting transfers between devices, on_device(): arrived = lax.all_to_all(restricted, 'gx', 0, 0, tiled=True)  3.37 us
    unnamed x20, local copies, waits for them, and re-layouts  2.49 us
  transfers between devices with their start and end apart: 8, of which 4 were waited for; matrix products, arithmetic and copies ran while one was open for 0% of the time, Pallas kernels for 6%

profile of v3, /device:TPU:0, one launch (start us, length us, event | category | flops | bytes accessed | tf_op | source)
XLA Modules:
  0.0 46.9 jit_solution(11571845128971107286)
XLA Ops:
  0.6 0.6 %copy-done.8 = s32[32]{0:T(128)S(1)} copy-done((s32[32]{0:T(128)S(1)}, s32[32]{0:T(128)}, u32[]{:S(2)}) %copy-start.8) | copy-done | bytes 152
  1.3 0.0 copy-done.9
  1.3 0.9 %copy-done = f32[32,1024]{1,0:T(8,128)S(1)} copy-done((f32[32,1024]{1,0:T(8,128)S(1)}, f32[32,1024]{1,0:T(8,128)}, u32[]{:S(2)}) %copy-start) | copy-done | bytes 131096
  2.2 0.9 %copy-done.2 = f32[32,1024]{1,0:T(8,128)S(1)} copy-done((f32[32,1024]{1,0:T(8,128)S(1)}, f32[32,1024]{1,0:T(8,128)}, u32[]{:S(2)}) %copy-start.2) | copy-done | bytes 131096
  3.1 0.2 shard_map.95
  3.3 3.1 %collective-permute-start = (f32[32,256]{1,0:T(8,128)S(1)}, f32[32,256]{1,0:T(8,128)S(1)}, u32[]{:S(2)}, u32[]{:S(2)}) collective-permute-start(f32[32,256]{1,0:T(8,128)S(1)} %get-tuple-element.35), channel_id=1, source_target_pairs={{0,1},{1,0},{2,3},{3,2},{4,5},{5,4},{6,7},{7,6},{8,9},{9,8},{10,11... | collective-permute-start | bytes 98312 | tf_op jit(solution)/shard_map/ppermute | solution.py:835
  6.4 1.9 %collective-permute-done.from_even.y_even = f32[32,256]{1,0:T(8,128)S(1)} collective-permute-done((f32[32,256]{1,0:T(8,128)S(1)}, f32[32,256]{1,0:T(8,128)S(1)}, u32[]{:S(2)}, u32[]{:S(2)}) %collective-permute-start) | collective-permute-done | bytes 32800 | tf_op jit(solution)/shard_map/ppermute | solution.py:835
  8.3 1.0 %shard_map.96 = f32[8,24,128]{2,1,0:T(8,128)} custom-call(s32[1,32]{1,0:T(1,128)S(1)} %get-tuple-element.33.position, s32[1,3]{1,0:T(1,128)S(1)} %get-tuple-element.34.colours, f32[32,1024]{1,0:T(8,128)S(1)} %copy-done, f32[32,256]{1,0:T(8,128)S(1)} %collective-permute-done.from_even.y_even, f32[32,256]{1,0:T(8,128)S(1)} %collective-permute-done.1.from_odd.y_odd, ...), custom_call_target="tpu_custom_call" | custom-call | tf_op jit(solution)/shard_map/pallas_call | solution.py:800
  9.3 4.3 %all-to-all-start = ((f32[8,24,128]{2,1,0:T(8,128)}), f32[8,24,128]{2,1,0:T(8,128)S(1)}, u32[]{:S(2)}, u32[]{:S(2)}) async-start(f32[8,24,128]{2,1,0:T(8,128)} %shard_map.96), calls=%async_computation | async-start | bytes 196608 | tf_op jit(solution)/shard_map/all_to_all | solution.py:878
  13.7 0.0 copy-start.6
  13.7 0.5 %shard_map.99 = (f32[8,32,128]{2,1,0:T(8,128)S(1)}, f32[16,2560]{1,0:T(8,128)S(1)}, f32[16,2560]{1,0:T(8,128)S(1)}) custom-call(f32[32,1024]{1,0:T(8,128)S(1)} %copy-done.1, f32[32,1024]{1,0:T(8,128)S(1)} %copy-done.3, f32[32,1024]{1,0:T(8,128)S(1)} %copy-done.7, f32[32,256]{1,0:T(8,128)S(1)} %collective-permute-done.from_even.y_even, ...), custom_call_target="tpu_custom_call" | custom-call | tf_op jit(solution)/shard_map/pallas_call | solution.py:800
  14.2 0.6 %collective-permute-start.2 = (f32[16,2560]{1,0:T(8,128)S(1)}, f32[16,2560]{1,0:T(8,128)S(1)}, u32[]{:S(2)}, u32[]{:S(2)}) collective-permute-start(f32[16,2560]{1,0:T(8,128)S(1)} %get-tuple-element.49), channel_id=1, source_target_pairs={{0,4},{4,0},{8,12},{12,8},{16,20},{20,16},{24,28},{28,24},{1,5},{5... | collective-permute-start | bytes 491528 | tf_op jit(solution)/shard_map/ppermute | solution.py:835
  14.7 2.7 %collective-permute-start.3 = (f32[16,2560]{1,0:T(8,128)S(1)}, f32[16,2560]{1,0:T(8,128)S(1)}, u32[]{:S(2)}, u32[]{:S(2)}) collective-permute-start(f32[16,2560]{1,0:T(8,128)S(1)} %get-tuple-element.50), channel_id=1, source_target_pairs={{0,1},{4,8},{8,4},{12,16},{16,12},{20,24},{24,20},{28,29},{1,0},{5... | collective-permute-start | bytes 491528 | tf_op jit(solution)/shard_map/ppermute | solution.py:835
  17.5 0.7 %shard_map.97 = (f32[6,8,32,128]{3,2,1,0:T(8,128)S(1)}, f32[8,32,128]{2,1,0:T(8,128)S(1)}, f32[8,32,128]{2,1,0:T(8,128)S(1)}, bf16[64,1024]{1,0:T(8,128)(2,1)S(1...) custom-call(f32[32,1024]{1,0:T(8,128)S(1)} %bitcast.6, ...), custom_call_target="tpu_custom_call" | custom-call | tf_op jit(solution)/shard_map/pallas_call | solution.py:891
  18.2 0.6 %all-to-all-done.faces = f32[8,24,128]{2,1,0:T(8,128)S(1)} async-done(((f32[8,24,128]{2,1,0:T(8,128)}), f32[8,24,128]{2,1,0:T(8,128)S(1)}, u32[]{:S(2)}, u32[]{:S(2)}) %all-to-all-start) | async-done | bytes 98336 | tf_op jit(solution)/shard_map/all_to_all | solution.py:878
  18.8 1.4 %shard_map.98 = (f32[32,1024]{1,0:T(8,128)S(1)}, f32[8,16,256]{2,1,0:T(8,128)}) custom-call(s32[1,32]{1,0:T(1,128)S(1)} %get-tuple-element.33.position, s32[1,3]{1,0:T(1,128)S(1)} %get-tuple-element.34.colours, f32[8,24,128]{2,1,0:T(8,128)S(1)} %all-to-all-done.faces, f32[32,1024]{1,0:T(8,128)S(1)} %bitcast.7, f32[32,1024]{1,0:T(8,128)S(1)} %bitcast.9, ...), custom_call_target="tpu_custom_call" | custom-call | tf_op jit(solution)/shard_map/pallas_call | solution.py:800
  20.2 3.4 %all-to-all-start.1 = ((f32[8,16,256]{2,1,0:T(8,128)}), f32[8,16,256]{2,1,0:T(8,128)S(1)}, u32[]{:S(2)}, u32[]{:S(2)}) async-start(f32[8,16,256]{2,1,0:T(8,128)} %get-tuple-element.45), calls=%async_computation.1 | async-start | bytes 262144 | tf_op jit(solution)/shard_map/all_to_all | solution.py:919
  23.6 5.4 %all-to-all-done.1.arrived = f32[8,16,256]{2,1,0:T(8,128)S(1)} async-done(((f32[8,16,256]{2,1,0:T(8,128)}), f32[8,16,256]{2,1,0:T(8,128)S(1)}, u32[]{:S(2)}, u32[]{:S(2)}) %all-to-all-start.1) | async-done | bytes 131104 | tf_op jit(solution)/shard_map/all_to_all | solution.py:919
  29.1 2.7 %shard_map.100 = (f32[32,512]{1,0:T(8,128)S(1)}, f32[32,256]{1,0:T(8,128)S(1)}, f32[32,1024]{1,0:T(8,128)S(1)}, f32[32,512]{1,0:T(8,128)S(1)}, f32[32,512]{1,0:T(8,128)S(1)}) custom-call(s32[1,32]{1,0:T(1,128)S(1)} %get-tuple-element.33.position, s32[1,3]{1,0:T(1,128)S(1)} %get-tuple-element.34.colours, f32[8,16,256]{2,1,0:T(8,128)S(1)} %all-to-all-done.1.arrived, ...), custom_call_target="tpu_custom_call" | custom-call | tf_op jit(solution)/shard_map/pallas_call | solution.py:800
  31.7 2.8 %collective-permute-start.4 = (f32[32,512]{1,0:T(8,128)S(1)}, f32[32,512]{1,0:T(8,128)S(1)}, u32[]{:S(2)}, u32[]{:S(2)}) collective-permute-start(f32[32,512]{1,0:T(8,128)S(1)} %get-tuple-element.55), channel_id=1, source_target_pairs={{0,1},{1,0},{2,3},{3,2},{4,5},{5,4},{6,7},{7,6},{8,9},{9,8},{10,11... | collective-permute-start | bytes 196616 | tf_op jit(solution)/shard_map/ppermute | solution.py:835
  34.5 2.2 %collective-permute-done.4.from_even = f32[32,512]{1,0:T(8,128)S(1)} collective-permute-done((f32[32,512]{1,0:T(8,128)S(1)}, f32[32,512]{1,0:T(8,128)S(1)}, u32[]{:S(2)}, u32[]{:S(2)}) %collective-permute-start.4) | collective-permute-done | bytes 65568 | tf_op jit(solution)/shard_map/ppermute | solution.py:835
  36.8 1.3 %shard_map.101 = (f32[32,1024]{1,0:T(8,128)S(1)}, f32[8,16,256]{2,1,0:T(8,128)S(1)}) custom-call(s32[1,32]{1,0:T(1,128)S(1)} %get-tuple-element.33.position, s32[1,3]{1,0:T(1,128)S(1)} %get-tuple-element.34.colours, f32[32,512]{1,0:T(8,128)S(1)} %get-tuple-element.52.source_b, f32[32,256]{1,0:T(8,128)S(1)} %get-tuple-element.53.coefficient_b, ...), custom_call_target="tpu_custom_call" | custom-call | tf_op jit(solution)/shard_map/pallas_call | solution.py:800
  38.0 7.9 %all_to_all.15.arrived = f32[8,16,256]{2,1,0:T(8,128)S(1)} all-to-all(f32[8,16,256]{2,1,0:T(8,128)S(1)} %get-tuple-element.59), channel_id=1, replica_groups=mesh['gx'=8,'gy'=4] {'gx'}, dimensions={0} | all-to-all | bytes 262144 | tf_op jit(solution)/shard_map/all_to_all | solution.py:955
  45.9 1.0 %shard_map.102 = (f32[32,1024]{1,0:T(8,128)}, f32[32,1024]{1,0:T(8,128)}) custom-call(s32[1,32]{1,0:T(1,128)S(1)} %get-tuple-element.33.position, f32[8,16,256]{2,1,0:T(8,128)S(1)} %all_to_all.15.arrived, f32[32,1024]{1,0:T(8,128)S(1)} %get-tuple-element.60.smoothed, f32[32,1024]{1,0:T(8,128)S(1)} %copy-done.1, f32[32,1024]{1,0:T(8,128)S(1)} %get-tuple-element.61.correction, ...), custom_call_target="tpu_custom_call" | custom-call | tf_op jit(solution)/shard_map/pallas_call | solution.py:800
  (21 shorter events, 0.0 us)
Async XLA Ops:
  0.6 0.7 %copy-start.8 = (s32[32]{0:T(128)S(1)}, s32[32]{0:T(128)}, u32[]{:S(2)}) copy-start(s32[32]{0:T(128)} %param.14) | copy-start | bytes 388
  0.6 0.7 %copy-start.9 = (s32[3]{0:T(128)S(1)}, s32[3]{0:T(128)}, u32[]{:S(2)}) copy-start(s32[3]{0:T(128)} %param.15) | copy-start | bytes 40
  1.3 0.9 %copy-start = (f32[32,1024]{1,0:T(8,128)S(1)}, f32[32,1024]{1,0:T(8,128)}, u32[]{:S(2)}) copy-start(f32[32,1024]{1,0:T(8,128)} %start.9) | copy-start | bytes 393220
  2.2 0.9 %copy-start.2 = (f32[32,1024]{1,0:T(8,128)S(1)}, f32[32,1024]{1,0:T(8,128)}, u32[]{:S(2)}) copy-start(f32[32,1024]{1,0:T(8,128)} %coefficient.5) | copy-start | bytes 393220
  3.3 5.0 %collective-permute-start = (f32[32,256]{1,0:T(8,128)S(1)}, f32[32,256]{1,0:T(8,128)S(1)}, u32[]{:S(2)}, u32[]{:S(2)}) collective-permute-start(f32[32,256]{1,0:T(8,128)S(1)} %get-tuple-element.35), channel_id=1, source_target_pairs={{0,1},{1,0},{2,3},{3,2},{4,5},{5,4},{6,7},{7,6},{8,9},{9,8},{10,11... | collective-permute-start | bytes 98312 | tf_op jit(solution)/shard_map/ppermute | solution.py:835
  6.4 1.9 %collective-permute-start.1 = (f32[32,256]{1,0:T(8,128)S(1)}, f32[32,256]{1,0:T(8,128)S(1)}, u32[]{:S(2)}, u32[]{:S(2)}) collective-permute-start(f32[32,256]{1,0:T(8,128)S(1)} %get-tuple-element.36), channel_id=1, source_target_pairs={{0,4},{1,2},{2,1},{3,7},{4,0},{5,6},{6,5},{7,3},{8,12},{9,10},{10,... | collective-permute-start | bytes 98312 | tf_op jit(solution)/shard_map/ppermute | solution.py:835
  8.3 5.3 %copy-start.3 = (f32[32,1024]{1,0:T(8,128)S(1)}, f32[32,1024]{1,0:T(8,128)}, u32[]{:S(2)}) copy-start(f32[32,1024]{1,0:T(8,128)} %coefficient.5) | copy-start | bytes 393220
  8.3 5.3 %copy-start.7 = (f32[32,1024]{1,0:T(8,128)S(1)}, f32[32,1024]{1,0:T(8,128)}, u32[]{:S(2)}) copy-start(f32[32,1024]{1,0:T(8,128)} %source.1) | copy-start | bytes 393220
  9.3 4.3 %copy-start.1 = (f32[32,1024]{1,0:T(8,128)S(1)}, f32[32,1024]{1,0:T(8,128)}, u32[]{:S(2)}) copy-start(f32[32,1024]{1,0:T(8,128)} %start.9) | copy-start | bytes 393220
  9.3 9.5 %all-to-all-start = ((f32[8,24,128]{2,1,0:T(8,128)}), f32[8,24,128]{2,1,0:T(8,128)S(1)}, u32[]{:S(2)}, u32[]{:S(2)}) async-start(f32[8,24,128]{2,1,0:T(8,128)} %shard_map.96), calls=%async_computation | async-start | bytes 196608 | tf_op jit(solution)/shard_map/all_to_all | solution.py:878
  13.6 3.8 %copy-start.4 = (f32[1,32,1024]{2,1,0:T(8,128)S(1)}, f32[1,32,1024]{2,1,0:T(8,128)}, u32[]{:S(2)}) copy-start(f32[1,32,1024]{2,1,0:T(8,128)} %param.11) | copy-start | bytes 393220
  13.6 3.8 %copy-start.5 = (f32[1,32,1024]{2,1,0:T(8,128)S(1)}, f32[1,32,1024]{2,1,0:T(8,128)}, u32[]{:S(2)}) copy-start(f32[1,32,1024]{2,1,0:T(8,128)} %param.12) | copy-start | bytes 393220
  13.7 3.8 %copy-start.6 = (f32[1,32,1024]{2,1,0:T(8,128)S(1)}, f32[1,32,1024]{2,1,0:T(8,128)}, u32[]{:S(2)}) copy-start(f32[1,32,1024]{2,1,0:T(8,128)} %param.13) | copy-start | bytes 393220
  14.2 9.5 %collective-permute-start.2 = (f32[16,2560]{1,0:T(8,128)S(1)}, f32[16,2560]{1,0:T(8,128)S(1)}, u32[]{:S(2)}, u32[]{:S(2)}) collective-permute-start(f32[16,2560]{1,0:T(8,128)S(1)} %get-tuple-element.49), channel_id=1, source_target_pairs={{0,4},{4,0},{8,12},{12,8},{16,20},{20,16},{24,28},{28,24},{1,5},{5... | collective-permute-start | bytes 491528 | tf_op jit(solution)/shard_map/ppermute | solution.py:835
  14.7 8.9 %collective-permute-start.3 = (f32[16,2560]{1,0:T(8,128)S(1)}, f32[16,2560]{1,0:T(8,128)S(1)}, u32[]{:S(2)}, u32[]{:S(2)}) collective-permute-start(f32[16,2560]{1,0:T(8,128)S(1)} %get-tuple-element.50), channel_id=1, source_target_pairs={{0,1},{4,8},{8,4},{12,16},{16,12},{20,24},{24,20},{28,29},{1,0},{5... | collective-permute-start | bytes 491528 | tf_op jit(solution)/shard_map/ppermute | solution.py:835
  20.2 8.8 %all-to-all-start.1 = ((f32[8,16,256]{2,1,0:T(8,128)}), f32[8,16,256]{2,1,0:T(8,128)S(1)}, u32[]{:S(2)}, u32[]{:S(2)}) async-start(f32[8,16,256]{2,1,0:T(8,128)} %get-tuple-element.45), calls=%async_computation.1 | async-start | bytes 262144 | tf_op jit(solution)/shard_map/all_to_all | solution.py:919
  31.7 5.0 %collective-permute-start.4 = (f32[32,512]{1,0:T(8,128)S(1)}, f32[32,512]{1,0:T(8,128)S(1)}, u32[]{:S(2)}, u32[]{:S(2)}) collective-permute-start(f32[32,512]{1,0:T(8,128)S(1)} %get-tuple-element.55), channel_id=1, source_target_pairs={{0,1},{1,0},{2,3},{3,2},{4,5},{5,4},{6,7},{7,6},{8,9},{9,8},{10,11... | collective-permute-start | bytes 196616 | tf_op jit(solution)/shard_map/ppermute | solution.py:835
  34.5 2.2 %collective-permute-start.5 = (f32[32,512]{1,0:T(8,128)S(1)}, f32[32,512]{1,0:T(8,128)S(1)}, u32[]{:S(2)}, u32[]{:S(2)}) collective-permute-start(f32[32,512]{1,0:T(8,128)S(1)} %get-tuple-element.56), channel_id=1, source_target_pairs={{0,4},{1,2},{2,1},{3,7},{4,0},{5,6},{6,5},{7,3},{8,12},{9,10},{10,... | collective-permute-start | bytes 196616 | tf_op jit(solution)/shard_map/ppermute | solution.py:835
